TPU v7x, 8 devices: a whole 2x2x1 slice. The times are simulated.
8 devices in a mesh: data: 1 (over z), tp: 2 (over y), cp: 4 (over x, core).
Axes of the slice: x: 2, y: 2, z: 1, core: 2. Of those that a mesh axis runs over, the one named last changes fastest.
Arguments:
- x: bfloat16 [16, 1024, 8192], P('data', ('cp', 'tp'))
- positions: int32 [16, 1024], P('data', ('cp', 'tp'))
- w_query: bfloat16 [8192, 8192], P(None, 'tp')
- w_key: bfloat16 [8192, 8192], P(None, 'tp')
- w_value: bfloat16 [8192, 8192], P(None, 'tp')
- w_out: bfloat16 [8192, 8192], P('tp')
Outputs:
- output: bfloat16 [16, 1024, 8192], P('data', ('cp', 'tp'))
All inputs are finite; a program needn't handle non-finite values.
Results may differ from a plain program's by a relative error of at most 0.00652.
Values are sent between devices in bfloat16 or wider.
A program may use at most 1.5 GiB of HBM per device.

v0:
```python
import math
import jax
import jax.numpy as jnp
from jax import lax
from jax.sharding import PartitionSpec as P

HEAD_DIM = 128
ROPE_BASE = 500000


def rope_tables(pos_vals):
    inv_freq = jnp.asarray([ROPE_BASE ** (-2.0 * freq_idx / HEAD_DIM) for freq_idx in range(HEAD_DIM // 2)], dtype=jnp.float32)
    angles = pos_vals.astype(jnp.float32)[..., None] * inv_freq
    return jnp.cos(angles), jnp.sin(angles)


def apply_rope(head_vals, cos_t, sin_t):
    half_dim = head_vals.shape[-1] // 2
    lower_half = head_vals[..., :half_dim]
    upper_half = head_vals[..., half_dim:]
    return jnp.concatenate([lower_half * cos_t - upper_half * sin_t, upper_half * cos_t + lower_half * sin_t], axis=-1)


def project_heads(x_rows, pos_rows, w_query, w_key, w_value):
    batch_rows, n_rows = pos_rows.shape
    kv_local = w_key.shape[1] // HEAD_DIM
    q_per_kv = w_query.shape[1] // w_key.shape[1]
    cos_t, sin_t = rope_tables(pos_rows)
    q_proj = jnp.dot(x_rows, w_query, preferred_element_type=jnp.float32).astype(jnp.bfloat16)
    k_proj = jnp.dot(x_rows, w_key, preferred_element_type=jnp.float32).astype(jnp.bfloat16)
    v_proj = jnp.dot(x_rows, w_value, preferred_element_type=jnp.float32).astype(jnp.bfloat16)
    q_heads = q_proj.reshape(batch_rows, n_rows, kv_local, q_per_kv, HEAD_DIM).astype(jnp.float32)
    q_rot = apply_rope(q_heads, cos_t[:, :, None, None, :], sin_t[:, :, None, None, :]).astype(jnp.bfloat16)
    k_heads = k_proj.reshape(batch_rows, n_rows, kv_local, HEAD_DIM).astype(jnp.float32)
    k_rot = apply_rope(k_heads, cos_t[:, :, None, :], sin_t[:, :, None, :]).astype(jnp.bfloat16)
    return q_rot, k_rot, v_proj.reshape(batch_rows, n_rows, kv_local, HEAD_DIM)


def block_scores(q_blk, k_blk):
    return jnp.einsum('bqhgd,bkhd->bhgqk', q_blk, k_blk, preferred_element_type=jnp.float32) * (1.0 / math.sqrt(HEAD_DIM))


def masked_scores(q_blk, k_blk, qpos_blk, kpos_blk):
    visible = kpos_blk[:, None, None, None, :] <= qpos_blk[:, None, None, :, None]
    return jnp.where(visible, block_scores(q_blk, k_blk), -jnp.inf)


def start_state(scores, v_blk):
    row_max = scores.max(axis=-1)
    exp_scores = jnp.exp(scores - row_max[..., None])
    out_accum = jnp.einsum('bhgqk,bkhd->bhgqd', exp_scores.astype(jnp.bfloat16), v_blk, preferred_element_type=jnp.float32)
    return row_max, exp_scores.sum(axis=-1), out_accum


def absorb(soft_state, scores, v_blk):
    run_max, run_sum, out_accum = soft_state
    new_max = jnp.maximum(run_max, scores.max(axis=-1))
    rescale = jnp.exp(run_max - new_max)
    exp_scores = jnp.exp(scores - new_max[..., None])
    new_sum = run_sum * rescale + exp_scores.sum(axis=-1)
    new_accum = out_accum * rescale[..., None] + jnp.einsum('bhgqk,bkhd->bhgqd', exp_scores.astype(jnp.bfloat16), v_blk, preferred_element_type=jnp.float32)
    return new_max, new_sum, new_accum


def finish(soft_state):
    run_sum = soft_state[1]
    return (soft_state[2] / run_sum[..., None]).astype(jnp.bfloat16)


def project_out(attn_out, w_out):
    w_out_heads = w_out.reshape(attn_out.shape[1], attn_out.shape[2], HEAD_DIM, w_out.shape[1])
    return jnp.einsum('bhgqd,hgde->bqe', attn_out, w_out_heads, preferred_element_type=jnp.float32)


def solution(mesh):
    cp_size = mesh.shape['cp']
    send_pairs = [(src_dev, (src_dev + 1) % cp_size) for src_dev in range(cp_size)]
    row_spec = P('data', ('cp', 'tp'))

    def local_fn(x_rows, pos_rows, w_query, w_key, w_value, w_out):
        x_pair = lax.all_gather(x_rows, 'tp', axis=1, tiled=True)
        pos_pair = lax.all_gather(pos_rows, 'tp', axis=1, tiled=True)
        half_len = x_pair.shape[1] // 2
        q_rot, k_rot, v_heads = project_heads(x_pair, pos_pair, w_query, w_key, w_value)
        q_low = q_rot[:, :half_len]
        q_high = q_rot[:, half_len:]
        pos_low = pos_pair[:, :half_len]
        pos_high = pos_pair[:, half_len:]
        low_state = start_state(masked_scores(q_low, k_rot[:, :half_len], pos_low, pos_low), v_heads[:, :half_len])
        high_state = start_state(masked_scores(q_high, k_rot, pos_high, pos_pair), v_heads)
        my_index = lax.axis_index('cp')

        def source_below(low_state, high_state, kv_blk):
            k_first = kv_blk[0][:, :half_len]
            v_first = kv_blk[1][:, :half_len]
            return (absorb(low_state, block_scores(q_low, k_first), v_first),
                    absorb(high_state, block_scores(q_high, k_first), v_first))

        def source_above(low_state, high_state, kv_blk):
            return low_state, absorb(high_state, block_scores(q_high, kv_blk[0]), kv_blk[1])

        def kv_step(step_idx, loop_carry):
            kv_blk, low_state, high_state = loop_carry
            kv_blk = lax.ppermute(kv_blk, 'cp', send_pairs)
            source = (my_index - step_idx) % cp_size
            low_state, high_state = lax.cond(source < my_index, source_below, source_above, low_state, high_state, kv_blk)
            return kv_blk, low_state, high_state

        kv_own = jnp.stack([k_rot, v_heads])
        _, low_state, high_state = lax.fori_loop(1, cp_size, kv_step, (kv_own, low_state, high_state))
        attn_out = jnp.concatenate([finish(low_state), finish(high_state)], axis=3)
        partial_y = project_out(attn_out, w_out)
        y_rows = lax.psum_scatter(partial_y, 'tp', scatter_dimension=1, tiled=True)
        return (x_rows.astype(jnp.float32) + y_rows).astype(jnp.bfloat16)

    return jax.shard_map(local_fn, mesh=mesh,
                         in_specs=(row_spec, row_spec, P(None, 'tp'), P(None, 'tp'), P(None, 'tp'), P('tp', None)),
                         out_specs=row_spec, check_vma=False)
```

profile of v0, /device:TPU:0, one launch (start us, length us, event | category | flops | bytes accessed | tf_op | source)
XLA Modules:
  0.0 7224.4 jit_solution(18116647210150341559)
XLA Ops:
  6.5 0.7 all-gather.2.cloned.1.call-update
  7.3 0.0 reduce-scatter.2.cloned.1.call-start
  7.3 0.0 copy-done.14
  7.3 5.7 all_gather.7
  13.0 1.1 broadcast_compare_fusion.1
  14.1 1.4 broadcast_compare_fusion
  15.4 8.8 multiply_cosine_fusion
  24.2 750.6 %all-gather.2.cloned.1.call-done = bf16[16,256,8192]{2,1,0:T(8,128)(2,1)} async-done(((bf16[16,128,8192]{2,1,0:T(8,128)(2,1)}), bf16[16,256,8192]{2,1,0:T(8,128)(2,1)}) %all-gather.2.cloned.1.call-update) | async-done | bytes 67108880 | tf_op jit(solution)/shard_map/all_gather | solution.py:81
  774.9 292.1 %convert_convert_fusion = f32[16,256,4096]{2,1,0:T(8,128)} fusion(bf16[16,256,8192]{2,1,0:T(8,128)(2,1)} %all-gather.2.cloned.1.call-done, bf16[8192,4096]{1,0:T(8,128)(2,1)} %param.13), kind=kOutput, calls=%fused_computation.98 | convolution fusion | flops 274911461376 | bytes 201326592 | tf_op jit(solution)/shard_map/dot_general | solution.py:29
  1067.0 44.1 copy.33
  1111.1 88.0 %fusion.118 = (f32[16,256,32,1,64]{4,2,1,0,3:T(8,128)}, f32[16,256,32,1,64]{4,2,1,0,3:T(8,128)}) fusion(f32[16,256,32,1,128]{4,2,1,0,3:T(8,128)} %bitcast.77), kind=kLoop, calls=%fused_computation.133 | loop fusion | bytes 134217728 | tf_op jit(solution)/shard_map/slice | solution.py:19
  1199.1 292.4 %convert_convert_fusion.1 = f32[16,256,4096]{2,1,0:T(8,128)} fusion(bf16[16,256,8192]{2,1,0:T(8,128)(2,1)} %all-gather.2.cloned.1.call-done, bf16[8192,4096]{1,0:T(8,128)(2,1)} %param.14), kind=kOutput, calls=%fused_computation.99 | convolution fusion | flops 274911461376 | bytes 201326592 | tf_op jit(solution)/shard_map/dot_general | solution.py:30
  1491.4 44.1 copy.31
  1535.5 88.0 %fusion.119 = (f32[16,256,32,64]{3,2,1,0:T(8,128)}, f32[16,256,32,64]{3,2,1,0:T(8,128)}) fusion(f32[16,256,32,128]{3,2,1,0:T(8,128)} %bitcast.68), kind=kLoop, calls=%fused_computation.134 | loop fusion | bytes 134217728 | tf_op jit(solution)/shard_map/slice | solution.py:19
  1623.5 119.1 %add_convert_fusion.1 = (bf16[16,256,32,1,64]{4,1,2,0,3:T(8,128)(2,1)}, bf16[16,256,32,1,64]{4,1,2,0,3:T(8,128)(2,1)}) fusion(f32[16,256,32,1,64]{4,2,1,0,3:T(8,128)} %get-tuple-element.409, f32[16,256,32,1,64]{4,2,1,0,3:T(8,128)} %get-tuple-element.408, f32[16,256,64]{2,1,0:T(8,128)S(1)} %copy-done.8, f32[16,256,64]{2,1,0:T(8,128)S(1)} %copy-done.7), kind=kLoop, calls=%fused_computation.72 | loop fusion | flops 67108864 | bytes 102760448 | tf_op jit(solution)/shard_map/convert.3
  1742.6 36.9 pad_maximum_fusion.1
  1779.5 118.8 %subtract_convert_fusion.1 = (bf16[16,256,32,64]{3,1,2,0:T(8,128)(2,1)}, bf16[16,256,32,64]{3,1,2,0:T(8,128)(2,1)}) fusion(f32[16,256,32,64]{3,2,1,0:T(8,128)} %get-tuple-element.411, f32[16,256,32,64]{3,2,1,0:T(8,128)} %get-tuple-element.410, f32[16,256,64]{2,1,0:T(8,128)S(1)} %copy-done.8, f32[16,256,64]{2,1,0:T(8,128)S(1)} %copy-done.7), kind=kLoop, calls=%fused_computation.75 | loop fusion | flops 67108864 | bytes 102760448 | tf_op jit(solution)/shard_map/convert.9
  1898.4 0.0 copy-done.12
  1898.4 57.9 fusion.64
  1956.3 22.0 fusion.63
  1978.3 291.8 %fusion.82 = bf16[16,256,4096]{2,1,0:T(8,128)(2,1)} fusion(bf16[16,256,8192]{2,1,0:T(8,128)(2,1)} %all-gather.2.cloned.1.call-done, bf16[8192,4096]{1,0:T(8,128)(2,1)} %param.15), kind=kOutput, calls=%fused_computation.103 | convolution fusion | flops 274894684160 | bytes 167772160 | tf_op jit(solution)/shard_map/dot_general | solution.py:31
  2270.1 45.2 fusion.108
  2315.3 23.1 copy_bitcast_fusion
  2338.4 30.0 fusion.87
  2368.4 15.3 fusion.79
  2383.7 27.9 fusion.103
  2411.6 0.0 copy-done.4
  2411.6 23.0 copy.32
  2434.6 22.7 copy.13
  2457.3 54.6 pad_maximum_fusion
  2511.9 0.0 copy-done.3
  2511.9 2810.4 %while.27 = (s32[]{:T(128)}, bf16[2,16,256,32,128]{4,2,3,1,0:T(8,128)(2,1)}, f32[16,32,1,128]{3,1,0,2:T(8,128)}, f32[16,32,1,128]{3,1,0,2:T(8,128)}, f32[16,32,1...) while((s32[]{:T(128)}, ...), condition=%wide.region_13.14_spmd, body=%wide.region_4.13_spmd.sunk | while | flops 8758099968 | bytes 986710528 | solution.py:110
  2512.1 0.0 collective-permute-start
  2512.2 722.0 %collective-permute-done = bf16[2,16,256,32,128]{4,2,3,1,0:T(8,128)(2,1)} collective-permute-done((bf16[2,16,256,32,128]{4,2,3,1,0:T(8,128)(2,1)}, bf16[2,16,256,32,128]{4,2,3,1,0:T(8,128)(2,1)}, u32[]{:S(2)}, u32[]{:S(2)}) %collective-permute-start) | collective-permute-done | bytes 67108896 | tf_op jit(solution)/shard_map/while/body/eval_jaxpr/ppermute | solution.py:104
  3234.2 114.6 %conditional.2 = (f32[16,32,1,128]{3,1,0,2:T(8,128)}, f32[16,32,1,128]{3,1,0,2:T(8,128)}, f32[16,32,1,128,128]{4,3,1,0,2:T(8,128)}, f32[16,32,1,128]{3,1,0,2:T(8...) conditional(s32[]{:T(128)} %convert_element_type.151, ...), branch_computations={%region_5.7_spmd, %region_8.12_spmd} | conditional | flops 8758099968 | bytes 583532736 | solution.py:106
  3234.2 38.8 bitcast_reduce_fusion
  3273.0 0.1 fusion.18
  3273.0 21.2 fusion.2
  3294.2 0.2 bitcast_add_fusion.1
  3294.4 54.4 bitcast_add_fusion
  3348.8 44.4 copy.76
  3393.2 85.0 %collective-permute-start = (bf16[2,16,256,32,128]{4,2,3,1,0:T(8,128)(2,1)}, bf16[2,16,256,32,128]{4,2,3,1,0:T(8,128)(2,1)}, u32[]{:S(2)}, u32[]{:S(2)}) collective-permute-start(bf16[2,16,256,32,128]{4,2,3,1,0:T(8,128)(2,1)} %get-tuple-element.529), channel_id=1, source_target_pairs={{0,1},{1,2},{2,3},{3,0},{4,5},{5,6},{6,7},{7,4}} | collective-permute-start | bytes 201326592 | tf_op jit(solution)/shard_map/while/body/eval_jaxpr/ppermute | solution.py:104
  3478.2 720.5 %collective-permute-done = bf16[2,16,256,32,128]{4,2,3,1,0:T(8,128)(2,1)} collective-permute-done((bf16[2,16,256,32,128]{4,2,3,1,0:T(8,128)(2,1)}, bf16[2,16,256,32,128]{4,2,3,1,0:T(8,128)(2,1)}, u32[]{:S(2)}, u32[]{:S(2)}) %collective-permute-start) | collective-permute-done | bytes 67108896 | tf_op jit(solution)/shard_map/while/body/eval_jaxpr/ppermute | solution.py:104
  4198.7 114.6 %conditional.2 = (f32[16,32,1,128]{3,1,0,2:T(8,128)}, f32[16,32,1,128]{3,1,0,2:T(8,128)}, f32[16,32,1,128,128]{4,3,1,0,2:T(8,128)}, f32[16,32,1,128]{3,1,0,2:T(8...) conditional(s32[]{:T(128)} %convert_element_type.151, ...), branch_computations={%region_5.7_spmd, %region_8.12_spmd} | conditional | flops 8758099968 | bytes 583532736 | solution.py:106
  4198.7 38.8 bitcast_reduce_fusion
  4237.4 0.1 fusion.18
  4237.5 21.2 fusion.2
  4258.7 0.2 bitcast_add_fusion.1
  4258.9 54.4 bitcast_add_fusion
  4313.3 44.4 copy.76
  4357.7 1.6 collective-permute-start
  4359.3 803.9 %collective-permute-done = bf16[2,16,256,32,128]{4,2,3,1,0:T(8,128)(2,1)} collective-permute-done((bf16[2,16,256,32,128]{4,2,3,1,0:T(8,128)(2,1)}, bf16[2,16,256,32,128]{4,2,3,1,0:T(8,128)(2,1)}, u32[]{:S(2)}, u32[]{:S(2)}) %collective-permute-start) | collective-permute-done | bytes 67108896 | tf_op jit(solution)/shard_map/while/body/eval_jaxpr/ppermute | solution.py:104
  5163.1 114.6 %conditional.2 = (f32[16,32,1,128]{3,1,0,2:T(8,128)}, f32[16,32,1,128]{3,1,0,2:T(8,128)}, f32[16,32,1,128,128]{4,3,1,0,2:T(8,128)}, f32[16,32,1,128]{3,1,0,2:T(8...) conditional(s32[]{:T(128)} %convert_element_type.151, ...), branch_computations={%region_5.7_spmd, %region_8.12_spmd} | conditional | flops 8758099968 | bytes 583532736 | solution.py:106
  5163.2 38.8 bitcast_reduce_fusion
  5201.9 0.1 fusion.18
  5202.0 21.2 fusion.2
  5223.2 0.2 bitcast_add_fusion.1
  5223.4 54.4 bitcast_add_fusion
  5277.8 44.4 copy.76
  5322.4 33.0 divide_convert_fusion
  5355.3 290.5 %convolution_bitcast_fusion = f32[16,256,8192]{2,1,0:T(8,128)} fusion(bf16[32,128,8192,1]{2,1,0,3:T(8,128)(2,1)} %bitcast.57, bf16[16,32,1,128,128]{4,3,1,0,2:T(8,128)(2,1)} %get-tuple-element.420, bf16[16,32,1,128,128]{4,3,1,0,2:T(8,128)(2,1)} %get-tuple-element.421), kind=kOutput, calls=%fused_computation.61 | convolution fusion | flops 274945015808 | bytes 234881024 | tf_op jit(solution)/shard_map/bhgqd,hgde->bqe/dot_general | solution.py:72
  5645.9 0.0 reduce-scatter.2.cloned.1.call-update
  5645.9 1528.6 %reduce-scatter.2.cloned.1.call-done = f32[16,128,8192]{2,1,0:T(8,128)} async-done(((f32[16,256,8192]{2,1,0:T(8,128)}), f32[16,128,8192]{2,1,0:T(8,128)}) %reduce-scatter.2.cloned.1.call-update) | async-done | bytes 67108880 | tf_op jit(solution)/shard_map/reduce_scatter | solution.py:113
  7174.4 42.7 add_convert_fusion
  (24 shorter events, 0.1 us)
Async XLA Ops:
  6.5 8.9 copy-start.15
  6.5 0.8 copy-start.14
  6.5 768.3 %all-gather.2.cloned.1.call-start = ((), (), s32[]{:S(2)}) async-start(), calls=%async_computation.1 | async-start | bytes 100663296 | tf_op jit(solution)/shard_map/all_gather | solution.py:81
  7.3 7167.2 %reduce-scatter.2.cloned.1.call-start = ((), (), s32[]{:S(2)}) async-start(), calls=%async_computation.2 | async-start | bytes 201326592 | tf_op jit(solution)/shard_map/reduce_scatter | solution.py:113
  1535.5 88.0 %copy-start.7 = (f32[16,256,64]{2,1,0:T(8,128)S(1)}, f32[16,256,64]{2,1,0:T(8,128)}, u32[]{:S(2)}) copy-start(f32[16,256,64]{2,1,0:T(8,128)} %get-tuple-element.412) | copy-start | bytes 3145732
  1535.5 88.0 %copy-start.8 = (f32[16,256,64]{2,1,0:T(8,128)S(1)}, f32[16,256,64]{2,1,0:T(8,128)}, u32[]{:S(2)}) copy-start(f32[16,256,64]{2,1,0:T(8,128)} %get-tuple-element.413) | copy-start | bytes 3145732
  1779.5 118.8 %copy-start.12 = (pred[16,128,256]{1,2,0:T(8,128)(4,1)S(1)}, pred[16,128,256]{1,2,0:T(8,128)(4,1)}, u32[]{:S(2)}) copy-start(pred[16,128,256]{1,2,0:T(8,128)(4,1)} %broadcast_compare_fusion) | copy-start | bytes 1572868
  1956.3 22.1 copy-start.2
  1978.3 291.8 %copy-start.13 = (pred[16,128,256]{1,2,0:T(8,128)(4,1)S(1)}, pred[16,128,256]{1,2,0:T(8,128)(4,1)}, u32[]{:S(2)}) copy-start(pred[16,128,256]{1,2,0:T(8,128)(4,1)} %broadcast_compare_fusion) | copy-start | bytes 1572868
  2315.3 23.1 copy-start.11
  2368.4 43.2 copy-start.4
  2457.3 54.6 copy-start.3
  2457.3 54.6 copy-start.6
  2512.1 722.1 %collective-permute-start = (bf16[2,16,256,32,128]{4,2,3,1,0:T(8,128)(2,1)}, bf16[2,16,256,32,128]{4,2,3,1,0:T(8,128)(2,1)}, u32[]{:S(2)}, u32[]{:S(2)}) collective-permute-start(bf16[2,16,256,32,128]{4,2,3,1,0:T(8,128)(2,1)} %get-tuple-element.529), channel_id=1, source_target_pairs={{0,1},{1,2},{2,3},{3,0},{4,5},{5,6},{6,7},{7,4}} | collective-permute-start | bytes 201326592 | tf_op jit(solution)/shard_map/while/body/eval_jaxpr/ppermute | solution.py:104
  3393.2 805.4 %collective-permute-start = (bf16[2,16,256,32,128]{4,2,3,1,0:T(8,128)(2,1)}, bf16[2,16,256,32,128]{4,2,3,1,0:T(8,128)(2,1)}, u32[]{:S(2)}, u32[]{:S(2)}) collective-permute-start(bf16[2,16,256,32,128]{4,2,3,1,0:T(8,128)(2,1)} %get-tuple-element.529), channel_id=1, source_target_pairs={{0,1},{1,2},{2,3},{3,0},{4,5},{5,6},{6,7},{7,4}} | collective-permute-start | bytes 201326592 | tf_op jit(solution)/shard_map/while/body/eval_jaxpr/ppermute | solution.py:104
  4357.7 805.5 %collective-permute-start = (bf16[2,16,256,32,128]{4,2,3,1,0:T(8,128)(2,1)}, bf16[2,16,256,32,128]{4,2,3,1,0:T(8,128)(2,1)}, u32[]{:S(2)}, u32[]{:S(2)}) collective-permute-start(bf16[2,16,256,32,128]{4,2,3,1,0:T(8,128)(2,1)} %get-tuple-element.529), channel_id=1, source_target_pairs={{0,1},{1,2},{2,3},{3,0},{4,5},{5,6},{6,7},{7,4}} | collective-permute-start | bytes 201326592 | tf_op jit(solution)/shard_map/while/body/eval_jaxpr/ppermute | solution.py:104
Sparse Core Ops, SparseCore 0:
  8.9 765.9 all-gather.1
  5646.0 1528.3 reduce-scatter.1
where the time goes:
time: 7230 us; the launch traced here: 7220 us
  waiting for transfers between devices  4530 us (63%)
  matrix products  1610 us (22%)
  other arithmetic  518 us (7%)
  local copies, waits for them, and re-layouts  466 us (6%)
  starting transfers between devices  86.6 us (1%)
    ppermute x3, waiting for transfers between devices, kv_step(): kv_blk = lax.ppermute(kv_blk, 'cp', send_pairs)  2250 us
    reduce_scatter x1, waiting for transfers between devices, local_fn(): y_rows = lax.psum_scatter(partial_y, 'tp', scatter_dimension=1, tiled=True)  1530 us
    all_gather x1, waiting for transfers between devices, local_fn(): x_pair = lax.all_gather(x_rows, 'tp', axis=1, tiled=True)  751 us
    dot_general x1, matrix products, project_heads(): jnp.dot(x_rows, w_key, preferred_element_type=jnp.float32)  292 us
    dot_general x1, matrix products, project_heads(): jnp.dot(x_rows, w_query, preferred_element_type=jnp.float32)  292 us
    dot_general x1, matrix products, project_heads(): jnp.dot(x_rows, w_value, preferred_element_type=jnp.float32)  292 us
    dot_general x1, matrix products, project_out(): jnp.einsum('bhgqd,hgde->bqe', attn_out, w_out_heads, preferred_element_ty...  290 us
    another operation x2, other arithmetic  238 us
  transfers between devices with their start and end apart: 5, of which 5 were waited for; matrix products, arithmetic and copies ran while one was open for 0% of the time, Pallas kernels for 0%

commit v1 on v0

v1 whole, which is shorter than its diff:
```python
import functools
import math
import jax
import jax.numpy as jnp
from jax import lax
from jax.experimental import pallas as pl
from jax.experimental.pallas import tpu as pltpu
from jax.sharding import PartitionSpec as P

HEAD_DIM = 128
ROPE_BASE = 500000
Q_TILE = 256
STEP_HEADS = 2
EXP_SCALE = math.log2(math.e) / math.sqrt(HEAD_DIM)
W_PIECES = 2


def rope_tables(pos_vals):
    inv_freq = jnp.asarray([ROPE_BASE ** (-2.0 * freq_idx / HEAD_DIM) for freq_idx in range(HEAD_DIM // 2)], dtype=jnp.float32)
    angles = pos_vals.astype(jnp.float32)[..., None] * inv_freq
    cos_t, sin_t = jnp.cos(angles), jnp.sin(angles)
    return jnp.concatenate([cos_t, cos_t], axis=-1), jnp.concatenate([-sin_t, sin_t], axis=-1)


def attend_kernel(place_ref, q_ref, k_ref, v_ref, cos_ref, sin_ref, o_ref, q_seq, k_seq, v_seq):
    n_rows = q_ref.shape[0]
    n_chunks = place_ref.shape[1]
    chunk = n_rows // n_chunks
    n_heads = q_ref.shape[1] // HEAD_DIM
    for m in range(n_chunks):
        src = slice(m * chunk, (m + 1) * chunk)
        dst = pl.ds(pl.multiple_of(place_ref[0, m] * chunk, chunk), chunk)
        cos_t, sin_t = cos_ref[src, :], sin_ref[src, :]
        for h in range(n_heads):
            cols = slice(h * HEAD_DIM, (h + 1) * HEAD_DIM)
            for in_ref, out_ref in ((q_ref, q_seq), (k_ref, k_seq)):
                vals = in_ref[src, cols].astype(jnp.float32)
                out_ref[dst, cols] = (vals * cos_t + pltpu.roll(vals, HEAD_DIM // 2, 1) * sin_t).astype(jnp.bfloat16)
        v_seq[dst, :] = v_ref[src, :]
    tile = min(Q_TILE, n_rows)
    below = lax.broadcasted_iota(jnp.int32, (tile, tile), 1) <= lax.broadcasted_iota(jnp.int32, (tile, tile), 0)
    contract_last = (((1,), (1,)), ((), ()))
    for j in range(n_rows // tile):
        for h in range(n_heads):
            cols = slice(h * HEAD_DIM, (h + 1) * HEAD_DIM)
            here = slice(j * tile, (j + 1) * tile)
            q_tile = q_seq[here, cols]
            s_diag = lax.dot_general(q_tile, k_seq[here, cols], contract_last, preferred_element_type=jnp.float32)
            s_diag = jnp.where(below, s_diag, -jnp.inf)
            row_max = jnp.max(s_diag, axis=1, keepdims=True)
            if j:
                s_prev = lax.dot_general(q_tile, k_seq[:j * tile, cols], contract_last, preferred_element_type=jnp.float32)
                row_max = jnp.maximum(row_max, jnp.max(s_prev, axis=1, keepdims=True))
            p_diag = jnp.exp2((s_diag - row_max) * EXP_SCALE)
            row_sum = jnp.sum(p_diag, axis=1, keepdims=True)
            acc = jnp.dot(p_diag.astype(jnp.bfloat16), v_seq[here, cols], preferred_element_type=jnp.float32)
            if j:
                p_prev = jnp.exp2((s_prev - row_max) * EXP_SCALE)
                row_sum = row_sum + jnp.sum(p_prev, axis=1, keepdims=True)
                acc = acc + jnp.dot(p_prev.astype(jnp.bfloat16), v_seq[:j * tile, cols], preferred_element_type=jnp.float32)
            out = (acc / row_sum).astype(jnp.bfloat16)
            for part in range(tile // chunk):
                dst = pl.ds(pl.multiple_of(place_ref[1, j * (tile // chunk) + part] * chunk, chunk), chunk)
                o_ref[dst, cols] = out[part * chunk:(part + 1) * chunk]


def attend(place, q, k, v, cos_t, sin_t):
    n_rows, width = q.shape
    step_w = STEP_HEADS * HEAD_DIM
    head_spec = pl.BlockSpec((n_rows, step_w), lambda g, place_ref: (0, g))
    table_spec = pl.BlockSpec((n_rows, HEAD_DIM), lambda g, place_ref: (0, 0))
    flops = 2 * n_rows * n_rows * width
    return pl.pallas_call(
        attend_kernel,
        out_shape=jax.ShapeDtypeStruct((n_rows, width), jnp.bfloat16),
        grid_spec=pltpu.PrefetchScalarGridSpec(
            num_scalar_prefetch=1, grid=(width // step_w,),
            in_specs=[head_spec] * 3 + [table_spec] * 2, out_specs=head_spec,
            scratch_shapes=[pltpu.VMEM((n_rows, step_w), jnp.bfloat16)] * 3),
        compiler_params=pltpu.CompilerParams(dimension_semantics=('arbitrary',), vmem_limit_bytes=48 * 2 ** 20),
        cost_estimate=pl.CostEstimate(flops=8 * flops, bytes_accessed=8 * n_rows * width, transcendentals=n_rows * n_rows * width // HEAD_DIM),
        name='attend',
    )(place, q, k, v, cos_t, sin_t)


def out_kernel(n_w, n_peers, tp_size, cp_ref, *refs):
    w_refs, pieces = refs[:n_w], refs[n_w:n_w + n_peers]
    x_ref = refs[n_w + n_peers]
    y_ref, o_all, sems = refs[-3:]
    chunk, width = pieces[0].shape
    cp_i = cp_ref[0]
    cp_size = n_peers // tp_size
    part_w = width // cp_size

    @pl.when(pl.program_id(0) == 0)
    def _():
        copies = []
        for m, piece in enumerate(pieces):
            mc, mt = m // tp_size, m % tp_size
            rows = pl.ds(pl.multiple_of((cp_i ^ mc) * chunk, chunk), chunk)
            if mt == 0:
                copies.append((piece, o_all.at[rows, pl.ds(0, width)]))
                continue
            for part in range(cp_size):
                cols = pl.ds(pl.multiple_of((cp_i ^ part) * part_w, part_w), part_w)
                copies.append((piece.at[:, cols], o_all.at[rows, pl.ds(width + part * part_w, part_w)]))
        copies = [pltpu.make_async_copy(src, dst, sems.at[n]) for n, (src, dst) in enumerate(copies)]
        for copy in copies:
            copy.start()
        for copy in copies:
            copy.wait()

    first, acc = 0, None
    for w_ref in w_refs:
        depth = w_ref.shape[0]
        term = jnp.dot(o_all[:, first:first + depth], w_ref[...], preferred_element_type=jnp.float32)
        acc = term if acc is None else acc + term
        first += depth
    y_ref[...] = (x_ref[...].astype(jnp.float32) + acc).astype(jnp.bfloat16)


def out_project(cp_i, w_parts, pieces, x_flat, y_buf, s, tp_size, n_tile=512):
    chunk, width = pieces[0].shape
    n_rows = chunk * len(pieces) // tp_size
    depth = width * tp_size
    dim = x_flat.shape[1]
    n_tile = min(n_tile, dim)
    any_spec = pl.BlockSpec(memory_space=pl.ANY)
    row_spec = pl.BlockSpec((n_rows, n_tile), lambda g, cp_ref: (s, g))
    operands = [*w_parts, *pieces, x_flat]
    in_specs = [pl.BlockSpec((w.shape[0], n_tile), lambda g, cp_ref: (0, g)) for w in w_parts] + [any_spec] * len(pieces) + [row_spec]
    aliases = {}
    if y_buf is not None:
        aliases = {1 + len(operands): 0}
        operands.append(y_buf)
        in_specs.append(any_spec)
    return pl.pallas_call(
        functools.partial(out_kernel, len(w_parts), len(pieces), tp_size),
        out_shape=jax.ShapeDtypeStruct(x_flat.shape, jnp.bfloat16),
        grid_spec=pltpu.PrefetchScalarGridSpec(
            num_scalar_prefetch=1, grid=(dim // n_tile,), in_specs=in_specs, out_specs=row_spec,
            scratch_shapes=[pltpu.VMEM((n_rows, depth), jnp.bfloat16), pltpu.SemaphoreType.DMA((len(pieces) * len(pieces),))]),
        input_output_aliases=aliases,
        compiler_params=pltpu.CompilerParams(dimension_semantics=('arbitrary',), vmem_limit_bytes=48 * 2 ** 20),
        cost_estimate=pl.CostEstimate(flops=2 * n_rows * depth * dim, bytes_accessed=2 * depth * dim + 2 * n_rows * (depth + 2 * dim), transcendentals=0),
        name='out_project',
    )(cp_i, *operands)


def solution(mesh):
    cp_size, tp_size = mesh.shape['cp'], mesh.shape['tp']
    n_peers = cp_size * tp_size
    row_spec = P('data', ('cp', 'tp'))

    def swap(vals, m):
        if not m:
            return vals
        mc, mt = m // tp_size, m % tp_size
        pairs = [(t * cp_size + c, (t ^ mt) * cp_size + (c ^ mc)) for t in range(tp_size) for c in range(cp_size)]
        return lax.ppermute(vals, ('tp', 'cp'), pairs)

    def local_fn(x_rows, pos_rows, w_query, w_key, w_value, w_out):
        n_seqs, chunk, dim = x_rows.shape
        n_own = n_seqs // cp_size
        cp_i, tp_i = lax.axis_index('cp'), lax.axis_index('tp')
        me = cp_i * tp_size + tp_i
        peers = me ^ jnp.arange(n_peers, dtype=jnp.int32)
        peer_cp, peer_tp = peers // tp_size, peers % tp_size
        block_of = jnp.where(peer_tp == 0, peer_cp, 2 * cp_size - 1 - peer_cp)
        chunk_of = jnp.argmax(block_of[None, :] == jnp.arange(n_peers, dtype=jnp.int32)[:, None], axis=1).astype(jnp.int32)
        place = jnp.stack([block_of, chunk_of]).astype(jnp.int32)
        pos_all = lax.all_gather(pos_rows, ('tp', 'cp'), axis=0, tiled=False)
        pos_all = jnp.take(pos_all, peer_tp * cp_size + peer_cp, axis=0)

        def seq_of(s, mc):
            return s * cp_size + (cp_i ^ mc)

        seq_x = []
        for s in range(n_own):
            outgoing = [lax.dynamic_index_in_dim(x_rows, seq_of(s, mc), 0, keepdims=False) for mc in range(cp_size)]
            seq_x.append([swap(outgoing[m // tp_size], m) for m in range(n_peers)])

        q_rows = w_out.shape[0] // cp_size
        piece_rows = q_rows // W_PIECES
        w_got = [[None] * W_PIECES for _ in range(cp_size)]
        for p in range(W_PIECES):
            mine = lax.dynamic_slice_in_dim(w_out, cp_i * q_rows + p * piece_rows, piece_rows, 0)
            w_got[0][p] = swap(mine, 1)
            w_got[1][p] = swap(w_got[0][p], tp_size)
            w_got[2][p] = swap(w_got[0][p], 2 * tp_size)
            w_got[3][p] = swap(w_got[2][p], tp_size)
        w_parts = [w_out] + [piece for part in w_got for piece in part]

        o_got = []
        for s in range(n_own):
            x_seq = jnp.concatenate(seq_x[s], axis=0)
            pos_seq = lax.dynamic_index_in_dim(pos_all, seq_of(s, 0), 1, keepdims=False).reshape(-1)
            cos_t, sin_t = rope_tables(pos_seq)
            q, k, v = [jnp.dot(x_seq, w, preferred_element_type=jnp.float32).astype(jnp.bfloat16) for w in (w_query, w_key, w_value)]
            o = attend(place, q, k, v, cos_t, sin_t)
            o_got.append([swap(o[m * chunk:(m + 1) * chunk], m) for m in range(n_peers)])

        x_flat = x_rows.reshape(n_seqs * chunk, dim)
        y = None
        for s in range(n_own):
            y = out_project(cp_i.reshape(1).astype(jnp.int32), w_parts, o_got[s], x_flat, y, s, tp_size)
        return y.reshape(n_seqs, chunk, dim)


    return jax.shard_map(local_fn, mesh=mesh,
                         in_specs=(row_spec, row_spec, P(None, 'tp'), P(None, 'tp'), P(None, 'tp'), P('tp', None)),
                         out_specs=row_spec, check_vma=False)
```

time: 7230 us -> 2550 us (0.35)
  waiting for transfers between devices: 4530 us -> 674 us
  matrix products: 1610 us -> 958 us
  Pallas kernels: 0 us -> 574 us
  other arithmetic: 518 us -> 14.9 us
  local copies, waits for them, and re-layouts: 466 us -> 133 us
  blocking collectives: 5.68 us -> 131 us
    ppermute x3 -> x64, waiting for transfers between devices: 2250 us -> 674 us  [swap(): return lax.ppermute(vals, ('tp', 'cp'), pairs)]
    reduce_scatter x1 -> x0, waiting for transfers between devices: 1530 us -> none  [local_fn(): y_rows = lax.psum_scatter(partial_y, 'tp', scatter_dimension=1, tiled=True)]
    all_gather x1 -> x0, waiting for transfers between devices: 751 us -> none  [local_fn(): x_pair = lax.all_gather(x_rows, 'tp', axis=1, tiled=True)]
    dot_general x14 -> x12, matrix products: 1610 us -> 958 us  [local_fn(): jnp.dot(x_seq, w, preferred_element_type=jnp.float32).astype(jnp.bfloat16)]
    pallas_call x0 -> x8, Pallas kernels: none -> 574 us  [the longest x4 326 us: out_project(): pl.pallas_call(functools.partial(out_kernel, len(w_parts), len(pieces), t...]
    another operation x3 -> x2, other arithmetic: 292 us -> 0.71 us  [the longest x1 0.7 us: local_fn(): jnp.argmax(block_of[None, :] == jnp.arange(n_peers, dtype=jnp.int32)[:, N...]
    slice x3 -> x4, local copies, waits for them, and re-layouts: 176 us -> 20.9 us  [local_fn(): o[m * chunk:(m + 1) * chunk]]
    while x6 -> x0, local copies, waits for them, and re-layouts: 133 us -> none
  transfers between devices with their start and end apart: 5 -> 64, of which waited for: 5 -> 20; matrix products, arithmetic and copies ran while one was open for 0% -> 43% of each run, Pallas kernels for 0% -> 19%
where the time goes in v1:
time: 2550 us
  matrix products  958 us (38%)
  waiting for transfers between devices  674 us (26%)
  Pallas kernels  574 us (23%)
  local copies, waits for them, and re-layouts  133 us (5%)
  blocking collectives  131 us (5%)
  starting transfers between devices  58.8 us (2%)
    dot_general x12, matrix products, local_fn(): jnp.dot(x_seq, w, preferred_element_type=jnp.float32).astype(jnp.bfloat16)  958 us
    ppermute x64, waiting for transfers between devices, swap(): return lax.ppermute(vals, ('tp', 'cp'), pairs)  674 us
    pallas_call x4, Pallas kernels, out_project(): pl.pallas_call(functools.partial(out_kernel, len(w_parts), len(pieces), t...  326 us
    pallas_call x4, Pallas kernels, attend(): pl.pallas_call(attend_kernel, out_shape=jax.ShapeDtypeStruct((n_rows, wid...  248 us
    all_gather x1, blocking collectives, local_fn(): pos_all = lax.all_gather(pos_rows, ('tp', 'cp'), axis=0, tiled=False)  131 us
    unnamed x67, local copies, waits for them, and re-layouts  77.6 us
    ppermute x64, starting transfers between devices, swap(): return lax.ppermute(vals, ('tp', 'cp'), pairs)  58.8 us
  transfers between devices with their start and end apart: 64, of which 20 were waited for; matrix products, arithmetic and copies ran while one was open for 43% of the time, Pallas kernels for 19%

profile of v1, /device:TPU:0, one launch (start us, length us, event | category | flops | bytes accessed | tf_op | source)
XLA Modules:
  0.0 2545.1 jit_solution(6083253956175805725)
XLA Ops:
  0.0 16.4 dynamic-slice_bitcast_fusion
  21.4 8.2 constant_dynamic-update-slice_fusion.31
  31.6 131.3 %all-gather = s32[128,128]{1,0:T(8,128)S(1)} all-gather(s32[16,128]{1,0:T(8,128)S(1)} %copy-done.12), channel_id=2, replica_groups=mesh['data'=1,'tp'=2,'cp'=4] {'tp','cp'}, dimensions={0}, use_global_device_ids=true | all-gather | bytes 73728 | tf_op jit(solution)/shard_map/all_gather | solution.py:172
  163.6 9.7 fusion.3
  178.0 11.9 constant_dynamic-slice_fusion.4
  190.3 3.1 constant_dynamic-update-slice_fusion.6
  198.2 3.1 constant_dynamic-update-slice_fusion.4
  202.9 3.1 constant_dynamic-update-slice_fusion.3
  206.6 3.1 constant_dynamic-update-slice_fusion.2
  209.7 28.5 %collective-permute-done.13 = bf16[128,8192]{1,0:T(8,128)(2,1)S(1)} collective-permute-done((bf16[128,8192]{1,0:T(8,128)(2,1)S(1)}, bf16[128,8192]{1,0:T(8,128)(2,1)S(1)}, u32[]{:S(2)}, u32[]{:S(2)}) %collective-permute-start.13) | collective-permute-done | bytes 2097184 | tf_op jit(solution)/shard_map/ppermute | solution.py:160
  239.9 43.3 %collective-permute-done.14 = bf16[128,8192]{1,0:T(8,128)(2,1)S(1)} collective-permute-done((bf16[128,8192]{1,0:T(8,128)(2,1)S(1)}, bf16[128,8192]{1,0:T(8,128)(2,1)S(1)}, u32[]{:S(2)}, u32[]{:S(2)}) %collective-permute-start.14) | collective-permute-done | bytes 2097184 | tf_op jit(solution)/shard_map/ppermute | solution.py:160
  286.2 79.7 %convolution_convert_fusion.11.q_ref = bf16[1024,4096]{1,0:T(8,128)(2,1)} fusion(bf16[1024,8192]{1,0:T(8,128)(2,1)} %constant_dynamic-update-slice_fusion, bf16[8192,4096]{1,0:T(8,128)(2,1)} %param.12), kind=kOutput, calls=%fused_computation.12 | convolution fusion | flops 68723671040 | bytes 92274688 | tf_op jit(solution)/shard_map/dot_general | solution.py:199
  365.9 80.0 %convolution_convert_fusion.10.k_ref = bf16[1024,4096]{1,0:T(8,128)(2,1)} fusion(bf16[1024,8192]{1,0:T(8,128)(2,1)} %constant_dynamic-update-slice_fusion, bf16[8192,4096]{1,0:T(8,128)(2,1)} %param.13), kind=kOutput, calls=%fused_computation.11 | convolution fusion | flops 68723671040 | bytes 92274688 | tf_op jit(solution)/shard_map/dot_general | solution.py:199
  445.9 3.1 constant_dynamic-update-slice_fusion.14
  450.7 3.1 constant_dynamic-update-slice_fusion.13
  453.8 3.2 constant_dynamic-update-slice_fusion.12
  462.3 3.2 constant_dynamic-update-slice_fusion.10
  465.5 28.3 %collective-permute-done.27 = bf16[128,8192]{1,0:T(8,128)(2,1)S(1)} collective-permute-done((bf16[128,8192]{1,0:T(8,128)(2,1)S(1)}, bf16[128,8192]{1,0:T(8,128)(2,1)S(1)}, u32[]{:S(2)}, u32[]{:S(2)}) %collective-permute-start.27) | collective-permute-done | bytes 2097184 | tf_op jit(solution)/shard_map/ppermute | solution.py:160
  495.3 43.5 %collective-permute-done.28 = bf16[128,8192]{1,0:T(8,128)(2,1)S(1)} collective-permute-done((bf16[128,8192]{1,0:T(8,128)(2,1)S(1)}, bf16[128,8192]{1,0:T(8,128)(2,1)S(1)}, u32[]{:S(2)}, u32[]{:S(2)}) %collective-permute-start.28) | collective-permute-done | bytes 2097184 | tf_op jit(solution)/shard_map/ppermute | solution.py:160
  541.7 79.7 %convolution_convert_fusion.8.q_ref = bf16[1024,4096]{1,0:T(8,128)(2,1)} fusion(bf16[1024,8192]{1,0:T(8,128)(2,1)} %constant_dynamic-update-slice_fusion.8, bf16[8192,4096]{1,0:T(8,128)(2,1)} %param.12), kind=kOutput, calls=%fused_computation.9 | convolution fusion | flops 68723671040 | bytes 92274688 | tf_op jit(solution)/shard_map/dot_general | solution.py:199
  621.4 80.1 %convolution_convert_fusion.7.k_ref = bf16[1024,4096]{1,0:T(8,128)(2,1)} fusion(bf16[1024,8192]{1,0:T(8,128)(2,1)} %constant_dynamic-update-slice_fusion.8, bf16[8192,4096]{1,0:T(8,128)(2,1)} %param.13), kind=kOutput, calls=%fused_computation.8 | convolution fusion | flops 68723671040 | bytes 92274688 | tf_op jit(solution)/shard_map/dot_general | solution.py:199
  701.5 79.6 %convolution_convert_fusion.9.v_ref = bf16[1024,4096]{1,0:T(8,128)(2,1)} fusion(bf16[1024,8192]{1,0:T(8,128)(2,1)} %constant_dynamic-update-slice_fusion, bf16[8192,4096]{1,0:T(8,128)(2,1)} %param.14), kind=kOutput, calls=%fused_computation.10 | convolution fusion | flops 68723671040 | bytes 92274688 | tf_op jit(solution)/shard_map/dot_general | solution.py:199
  781.1 80.0 %convolution_convert_fusion.6.v_ref = bf16[1024,4096]{1,0:T(8,128)(2,1)} fusion(bf16[1024,8192]{1,0:T(8,128)(2,1)} %constant_dynamic-update-slice_fusion.8, bf16[8192,4096]{1,0:T(8,128)(2,1)} %param.14), kind=kOutput, calls=%fused_computation.7 | convolution fusion | flops 68723671040 | bytes 92274688 | tf_op jit(solution)/shard_map/dot_general | solution.py:199
  861.2 3.1 constant_dynamic-update-slice_fusion.22
  866.0 3.1 constant_dynamic-update-slice_fusion.21
  869.1 3.2 constant_dynamic-update-slice_fusion.20
  873.9 3.1 constant_dynamic-update-slice_fusion.19
  877.5 3.2 constant_dynamic-update-slice_fusion.18
  880.7 28.3 %collective-permute-done.41 = bf16[128,8192]{1,0:T(8,128)(2,1)S(1)} collective-permute-done((bf16[128,8192]{1,0:T(8,128)(2,1)S(1)}, bf16[128,8192]{1,0:T(8,128)(2,1)S(1)}, u32[]{:S(2)}, u32[]{:S(2)}) %collective-permute-start.41) | collective-permute-done | bytes 2097184 | tf_op jit(solution)/shard_map/ppermute | solution.py:160
  910.6 43.5 %collective-permute-done.42 = bf16[128,8192]{1,0:T(8,128)(2,1)S(1)} collective-permute-done((bf16[128,8192]{1,0:T(8,128)(2,1)S(1)}, bf16[128,8192]{1,0:T(8,128)(2,1)S(1)}, u32[]{:S(2)}, u32[]{:S(2)}) %collective-permute-start.42) | collective-permute-done | bytes 2097184 | tf_op jit(solution)/shard_map/ppermute | solution.py:160
  957.0 79.6 %convolution_convert_fusion.5.q_ref = bf16[1024,4096]{1,0:T(8,128)(2,1)} fusion(bf16[1024,8192]{1,0:T(8,128)(2,1)} %constant_dynamic-update-slice_fusion.16, bf16[8192,4096]{1,0:T(8,128)(2,1)} %param.12), kind=kOutput, calls=%fused_computation.6 | convolution fusion | flops 68723671040 | bytes 92274688 | tf_op jit(solution)/shard_map/dot_general | solution.py:199
  1036.6 79.8 %convolution_convert_fusion.4.k_ref = bf16[1024,4096]{1,0:T(8,128)(2,1)} fusion(bf16[1024,8192]{1,0:T(8,128)(2,1)} %constant_dynamic-update-slice_fusion.16, bf16[8192,4096]{1,0:T(8,128)(2,1)} %param.13), kind=kOutput, calls=%fused_computation.5 | convolution fusion | flops 68723671040 | bytes 92274688 | tf_op jit(solution)/shard_map/dot_general | solution.py:199
  1116.4 79.8 %convolution_convert_fusion.3.v_ref = bf16[1024,4096]{1,0:T(8,128)(2,1)} fusion(bf16[1024,8192]{1,0:T(8,128)(2,1)} %constant_dynamic-update-slice_fusion.16, bf16[8192,4096]{1,0:T(8,128)(2,1)} %param.14), kind=kOutput, calls=%fused_computation.4 | convolution fusion | flops 68723671040 | bytes 92274688 | tf_op jit(solution)/shard_map/dot_general | solution.py:199
  1196.3 3.1 constant_dynamic-update-slice_fusion.30
  1201.1 3.1 constant_dynamic-update-slice_fusion.29
  1205.7 3.1 constant_dynamic-update-slice_fusion.28
  1209.3 3.1 constant_dynamic-update-slice_fusion.27
  1212.4 3.1 constant_dynamic-update-slice_fusion.26
  1215.5 28.7 %collective-permute-done.55 = bf16[128,8192]{1,0:T(8,128)(2,1)S(1)} collective-permute-done((bf16[128,8192]{1,0:T(8,128)(2,1)S(1)}, bf16[128,8192]{1,0:T(8,128)(2,1)S(1)}, u32[]{:S(2)}, u32[]{:S(2)}) %collective-permute-start.55) | collective-permute-done | bytes 2097184 | tf_op jit(solution)/shard_map/ppermute | solution.py:160
  1245.7 42.2 %collective-permute-done.56 = bf16[128,8192]{1,0:T(8,128)(2,1)S(1)} collective-permute-done((bf16[128,8192]{1,0:T(8,128)(2,1)S(1)}, bf16[128,8192]{1,0:T(8,128)(2,1)S(1)}, u32[]{:S(2)}, u32[]{:S(2)}) %collective-permute-start.56) | collective-permute-done | bytes 2097184 | tf_op jit(solution)/shard_map/ppermute | solution.py:160
  1289.4 80.1 %convolution_convert_fusion.2.q_ref = bf16[1024,4096]{1,0:T(8,128)(2,1)} fusion(bf16[1024,8192]{1,0:T(8,128)(2,1)} %constant_dynamic-update-slice_fusion.24, bf16[8192,4096]{1,0:T(8,128)(2,1)} %param.12), kind=kOutput, calls=%fused_computation.3 | convolution fusion | flops 68723671040 | bytes 92274688 | tf_op jit(solution)/shard_map/dot_general | solution.py:199
  1369.4 79.7 %convolution_convert_fusion.1.k_ref = bf16[1024,4096]{1,0:T(8,128)(2,1)} fusion(bf16[1024,8192]{1,0:T(8,128)(2,1)} %constant_dynamic-update-slice_fusion.24, bf16[8192,4096]{1,0:T(8,128)(2,1)} %param.13), kind=kOutput, calls=%fused_computation.2 | convolution fusion | flops 68723671040 | bytes 92274688 | tf_op jit(solution)/shard_map/dot_general | solution.py:199
  1449.2 61.4 %attend.4 = bf16[1024,4096]{1,0:T(8,128)(2,1)} custom-call(s32[2,8]{1,0:T(2,128)S(1)} %pad_add_fusion.place_ref, bf16[1024,4096]{1,0:T(8,128)(2,1)} %convolution_convert_fusion.11.q_ref, bf16[1024,4096]{1,0:T(8,128)(2,1)} %convolution_convert_fusion.10.k_ref, bf16[1024,4096]{1,0:T(8,128)(2,1)} %convolution_convert_fusion.9.v_ref, ...), custom_call_target="tpu_custom_call" | custom-call | flops 68719476736 | bytes 33554432 | tf_op jit(solution)/shard_map/attend/pallas_call | solution.py:73
  1510.6 5.9 fusion.14
  1518.5 62.2 %attend.5 = bf16[1024,4096]{1,0:T(8,128)(2,1)} custom-call(s32[2,8]{1,0:T(2,128)S(1)} %pad_add_fusion.place_ref, bf16[1024,4096]{1,0:T(8,128)(2,1)} %convolution_convert_fusion.8.q_ref, bf16[1024,4096]{1,0:T(8,128)(2,1)} %convolution_convert_fusion.7.k_ref, bf16[1024,4096]{1,0:T(8,128)(2,1)} %convolution_convert_fusion.6.v_ref, ...), custom_call_target="tpu_custom_call" | custom-call | flops 68719476736 | bytes 33554432 | tf_op jit(solution)/shard_map/attend/pallas_call | solution.py:73
  1580.7 5.9 fusion.13
  1586.7 79.9 %convolution_convert_fusion.v_ref = bf16[1024,4096]{1,0:T(8,128)(2,1)} fusion(bf16[1024,8192]{1,0:T(8,128)(2,1)} %constant_dynamic-update-slice_fusion.24, bf16[8192,4096]{1,0:T(8,128)(2,1)} %param.14), kind=kOutput, calls=%fused_computation.1 | convolution fusion | flops 68723671040 | bytes 92274688 | tf_op jit(solution)/shard_map/dot_general | solution.py:199
  1668.6 62.1 %attend.6 = bf16[1024,4096]{1,0:T(8,128)(2,1)} custom-call(s32[2,8]{1,0:T(2,128)S(1)} %pad_add_fusion.place_ref, bf16[1024,4096]{1,0:T(8,128)(2,1)} %convolution_convert_fusion.5.q_ref, bf16[1024,4096]{1,0:T(8,128)(2,1)} %convolution_convert_fusion.4.k_ref, bf16[1024,4096]{1,0:T(8,128)(2,1)} %convolution_convert_fusion.3.v_ref, ...), custom_call_target="tpu_custom_call" | custom-call | flops 68719476736 | bytes 33554432 | tf_op jit(solution)/shard_map/attend/pallas_call | solution.py:73
  1730.7 5.2 fusion.12
  1738.0 62.4 %attend.7 = bf16[1024,4096]{1,0:T(8,128)(2,1)} custom-call(s32[2,8]{1,0:T(2,128)S(1)} %pad_add_fusion.place_ref, bf16[1024,4096]{1,0:T(8,128)(2,1)} %convolution_convert_fusion.2.q_ref, bf16[1024,4096]{1,0:T(8,128)(2,1)} %convolution_convert_fusion.1.k_ref, bf16[1024,4096]{1,0:T(8,128)(2,1)} %convolution_convert_fusion.v_ref, ...), custom_call_target="tpu_custom_call" | custom-call | flops 68719476736 | bytes 33554432 | tf_op jit(solution)/shard_map/attend/pallas_call | solution.py:73
  1801.1 49.1 %collective-permute-done.4.refs_5_ = bf16[512,8192]{1,0:T(8,128)(2,1)} collective-permute-done((bf16[512,8192]{1,0:T(8,128)(2,1)}, bf16[512,8192]{1,0:T(8,128)(2,1)}, u32[]{:S(2)}, u32[]{:S(2)}) %collective-permute-start.4) | collective-permute-done | bytes 8388640 | tf_op jit(solution)/shard_map/ppermute | solution.py:160
  1850.2 179.3 %collective-permute-done.5.refs_6_ = bf16[512,8192]{1,0:T(8,128)(2,1)} collective-permute-done((bf16[512,8192]{1,0:T(8,128)(2,1)}, bf16[512,8192]{1,0:T(8,128)(2,1)}, u32[]{:S(2)}, u32[]{:S(2)}) %collective-permute-start.5) | collective-permute-done | bytes 8388640 | tf_op jit(solution)/shard_map/ppermute | solution.py:160
  2029.5 3.9 fusion.11
  2035.2 23.9 collective-permute-done.57.refs_10_
  2063.1 23.7 collective-permute-done.59.refs_12_
  2088.2 23.8 collective-permute-done.60.refs_13_
  2114.6 22.7 collective-permute-done.61.refs_14_
  2137.3 25.4 collective-permute-done.62.refs_15_
  2163.3 25.5 %collective-permute-done.63.refs_16_ = bf16[128,4096]{1,0:T(8,128)(2,1)S(1)} collective-permute-done((bf16[128,4096]{1,0:T(8,128)(2,1)S(1)}, bf16[128,4096]{1,0:T(8,128)(2,1)S(1)}, u32[]{:S(2)}, u32[]{:S(2)}) %collective-permute-start.63) | collective-permute-done | bytes 1048608 | tf_op jit(solution)/shard_map/ppermute | solution.py:160
  2196.0 81.1 %out_project.4.refs_18_ = bf16[2048,8192]{1,0:T(8,128)(2,1)} custom-call(s32[1]{0:T(128)} %bitcast.cp_ref, bf16[4096,8192]{1,0:T(8,128)(2,1)} %refs_0_.7, bf16[512,8192]{1,0:T(8,128)(2,1)} %collective-permute-done.refs_1_, bf16[512,8192]{1,0:T(8,128)(2,1)} %collective-permute-done.1.refs_2_, bf16[512,8192]{1,0:T(8,128)(2,1)} %copy-done.14, ...), custom_call_target="tpu_custom_call" | custom-call | flops 68719476736 | bytes 159383552 | tf_op jit(solution)/shard_map/out_project/pallas_call | solution.py:137
  2284.6 81.3 %out_project.5.refs_18_ = bf16[2048,8192]{1,0:T(8,128)(2,1)} custom-call(s32[1]{0:T(128)} %bitcast.cp_ref, bf16[4096,8192]{1,0:T(8,128)(2,1)} %refs_0_.7, bf16[512,8192]{1,0:T(8,128)(2,1)} %collective-permute-done.refs_1_, bf16[512,8192]{1,0:T(8,128)(2,1)} %collective-permute-done.1.refs_2_, ...), custom_call_target="tpu_custom_call", output_to_operand_aliasing={{}: (19, {})} | custom-call | flops 68719476736 | bytes 159383552 | tf_op jit(solution)/shard_map/out_project/pallas_call | solution.py:137
  2374.5 81.7 %out_project.6.refs_18_ = bf16[2048,8192]{1,0:T(8,128)(2,1)} custom-call(s32[1]{0:T(128)} %bitcast.cp_ref, bf16[4096,8192]{1,0:T(8,128)(2,1)} %refs_0_.7, bf16[512,8192]{1,0:T(8,128)(2,1)} %collective-permute-done.refs_1_, bf16[512,8192]{1,0:T(8,128)(2,1)} %collective-permute-done.1.refs_2_, ...), custom_call_target="tpu_custom_call", output_to_operand_aliasing={{}: (19, {})} | custom-call | flops 68719476736 | bytes 159383552 | tf_op jit(solution)/shard_map/out_project/pallas_call | solution.py:137
  2456.2 6.6 collective-permute-done.21.refs_16_
  2462.8 81.7 %out_project.7 = bf16[2048,8192]{1,0:T(8,128)(2,1)} custom-call(s32[1]{0:T(128)} %bitcast.cp_ref, bf16[4096,8192]{1,0:T(8,128)(2,1)} %refs_0_.7, bf16[512,8192]{1,0:T(8,128)(2,1)} %collective-permute-done.refs_1_, bf16[512,8192]{1,0:T(8,128)(2,1)} %collective-permute-done.1.refs_2_, bf16[512,8192]{1,0:T(8,128)(2,1)} %copy-done.14, ...), custom_call_target="tpu_custom_call", output_to_operand_aliasing={{}: (19, {})} | custom-call | flops 68719476736 | bytes 159383552 | tf_op jit(solution)/shard_map/out_project/pallas_call | solution.py:137
  (177 shorter events, 91.6 us)
Async XLA Ops:
  16.4 177.1 %collective-permute-start.9 = (bf16[128,8192]{1,0:T(8,128)(2,1)}, bf16[128,8192]{1,0:T(8,128)(2,1)}, u32[]{:S(2)}, u32[]{:S(2)}) collective-permute-start(bf16[128,8192]{1,0:T(8,128)(2,1)} %get-tuple-element.27), channel_id=1, source_target_pairs={{0,1},{1,0},{2,3},{3,2},{4,5},{5,4},{6,7},{7,6}} | collective-permute-start | bytes 6291464 | tf_op jit(solution)/shard_map/ppermute | solution.py:160
  17.2 180.9 %collective-permute-start.10 = (bf16[128,8192]{1,0:T(8,128)(2,1)}, bf16[128,8192]{1,0:T(8,128)(2,1)}, u32[]{:S(2)}, u32[]{:S(2)}) collective-permute-start(bf16[128,8192]{1,0:T(8,128)(2,1)} %get-tuple-element.27), channel_id=1, source_target_pairs={{0,5},{1,4},{2,7},{3,6},{4,1},{5,0},{6,3},{7,2}} | collective-permute-start | bytes 6291464 | tf_op jit(solution)/shard_map/ppermute | solution.py:160
  19.9 181.4 %collective-permute-start.11 = (bf16[128,8192]{1,0:T(8,128)(2,1)}, bf16[128,8192]{1,0:T(8,128)(2,1)}, u32[]{:S(2)}, u32[]{:S(2)}) collective-permute-start(bf16[128,8192]{1,0:T(8,128)(2,1)} %get-tuple-element.26), channel_id=1, source_target_pairs={{0,2},{1,3},{2,0},{3,1},{4,6},{5,7},{6,4},{7,5}} | collective-permute-start | bytes 6291464 | tf_op jit(solution)/shard_map/ppermute | solution.py:160
  21.3 184.7 %collective-permute-start.12 = (bf16[128,8192]{1,0:T(8,128)(2,1)}, bf16[128,8192]{1,0:T(8,128)(2,1)}, u32[]{:S(2)}, u32[]{:S(2)}) collective-permute-start(bf16[128,8192]{1,0:T(8,128)(2,1)} %get-tuple-element.26), channel_id=1, source_target_pairs={{0,6},{1,7},{2,4},{3,5},{4,2},{5,3},{6,0},{7,1}} | collective-permute-start | bytes 6291464 | tf_op jit(solution)/shard_map/ppermute | solution.py:160
  29.5 160.8 %collective-permute-start.8 = (bf16[128,8192]{1,0:T(8,128)(2,1)}, bf16[128,8192]{1,0:T(8,128)(2,1)}, u32[]{:S(2)}, u32[]{:S(2)}) collective-permute-start(bf16[128,8192]{1,0:T(8,128)(2,1)} %get-tuple-element.34), channel_id=1, source_target_pairs={{0,4},{1,5},{2,6},{3,7},{4,0},{5,1},{6,2},{7,3}} | collective-permute-start | bytes 6291464 | tf_op jit(solution)/shard_map/ppermute | solution.py:160
  190.3 47.9 %collective-permute-start.13 = (bf16[128,8192]{1,0:T(8,128)(2,1)S(1)}, bf16[128,8192]{1,0:T(8,128)(2,1)S(1)}, u32[]{:S(2)}, u32[]{:S(2)}) collective-permute-start(bf16[128,8192]{1,0:T(8,128)(2,1)S(1)} %get-tuple-element.25), channel_id=1, source_target_pairs={{0,3},{1,2},{2,1},{3,0},{4,7},{5,6},{6,5},{7,4}} | collective-permute-start | bytes 6291464 | tf_op jit(solution)/shard_map/ppermute | solution.py:160
  193.4 89.7 %collective-permute-start.14 = (bf16[128,8192]{1,0:T(8,128)(2,1)S(1)}, bf16[128,8192]{1,0:T(8,128)(2,1)S(1)}, u32[]{:S(2)}, u32[]{:S(2)}) collective-permute-start(bf16[128,8192]{1,0:T(8,128)(2,1)S(1)} %get-tuple-element.25), channel_id=1, source_target_pairs={{0,7},{1,6},{2,5},{3,4},{4,3},{5,2},{6,1},{7,0}} | collective-permute-start | bytes 6291464 | tf_op jit(solution)/shard_map/ppermute | solution.py:160
  198.2 250.8 %collective-permute-start.23 = (bf16[128,8192]{1,0:T(8,128)(2,1)}, bf16[128,8192]{1,0:T(8,128)(2,1)}, u32[]{:S(2)}, u32[]{:S(2)}) collective-permute-start(bf16[128,8192]{1,0:T(8,128)(2,1)} %get-tuple-element.24), channel_id=1, source_target_pairs={{0,1},{1,0},{2,3},{3,2},{4,5},{5,4},{6,7},{7,6}} | collective-permute-start | bytes 6291464 | tf_op jit(solution)/shard_map/ppermute | solution.py:160
  201.3 252.5 %collective-permute-start.24 = (bf16[128,8192]{1,0:T(8,128)(2,1)}, bf16[128,8192]{1,0:T(8,128)(2,1)}, u32[]{:S(2)}, u32[]{:S(2)}) collective-permute-start(bf16[128,8192]{1,0:T(8,128)(2,1)} %get-tuple-element.24), channel_id=1, source_target_pairs={{0,5},{1,4},{2,7},{3,6},{4,1},{5,0},{6,3},{7,2}} | collective-permute-start | bytes 6291464 | tf_op jit(solution)/shard_map/ppermute | solution.py:160
  206.0 251.0 %collective-permute-start.25 = (bf16[128,8192]{1,0:T(8,128)(2,1)}, bf16[128,8192]{1,0:T(8,128)(2,1)}, u32[]{:S(2)}, u32[]{:S(2)}) collective-permute-start(bf16[128,8192]{1,0:T(8,128)(2,1)} %get-tuple-element.23), channel_id=1, source_target_pairs={{0,2},{1,3},{2,0},{3,1},{4,6},{5,7},{6,4},{7,5}} | collective-permute-start | bytes 6291464 | tf_op jit(solution)/shard_map/ppermute | solution.py:160
  238.2 223.5 %collective-permute-start.26 = (bf16[128,8192]{1,0:T(8,128)(2,1)}, bf16[128,8192]{1,0:T(8,128)(2,1)}, u32[]{:S(2)}, u32[]{:S(2)}) collective-permute-start(bf16[128,8192]{1,0:T(8,128)(2,1)} %get-tuple-element.23), channel_id=1, source_target_pairs={{0,6},{1,7},{2,4},{3,5},{4,2},{5,3},{6,0},{7,1}} | collective-permute-start | bytes 6291464 | tf_op jit(solution)/shard_map/ppermute | solution.py:160
  283.2 162.7 %collective-permute-start.22 = (bf16[128,8192]{1,0:T(8,128)(2,1)}, bf16[128,8192]{1,0:T(8,128)(2,1)}, u32[]{:S(2)}, u32[]{:S(2)}) collective-permute-start(bf16[128,8192]{1,0:T(8,128)(2,1)} %get-tuple-element.32), channel_id=1, source_target_pairs={{0,4},{1,5},{2,6},{3,7},{4,0},{5,1},{6,2},{7,3}} | collective-permute-start | bytes 6291464 | tf_op jit(solution)/shard_map/ppermute | solution.py:160
  445.9 47.9 %collective-permute-start.27 = (bf16[128,8192]{1,0:T(8,128)(2,1)S(1)}, bf16[128,8192]{1,0:T(8,128)(2,1)S(1)}, u32[]{:S(2)}, u32[]{:S(2)}) collective-permute-start(bf16[128,8192]{1,0:T(8,128)(2,1)S(1)} %copy-done.2), channel_id=1, source_target_pairs={{0,3},{1,2},{2,1},{3,0},{4,7},{5,6},{6,5},{7,4}} | collective-permute-start | bytes 6291464 | tf_op jit(solution)/shard_map/ppermute | solution.py:160
  449.0 89.7 %collective-permute-start.28 = (bf16[128,8192]{1,0:T(8,128)(2,1)S(1)}, bf16[128,8192]{1,0:T(8,128)(2,1)S(1)}, u32[]{:S(2)}, u32[]{:S(2)}) collective-permute-start(bf16[128,8192]{1,0:T(8,128)(2,1)S(1)} %copy-done.2), channel_id=1, source_target_pairs={{0,7},{1,6},{2,5},{3,4},{4,3},{5,2},{6,1},{7,0}} | collective-permute-start | bytes 6291464 | tf_op jit(solution)/shard_map/ppermute | solution.py:160
  453.8 410.5 %collective-permute-start.37 = (bf16[128,8192]{1,0:T(8,128)(2,1)}, bf16[128,8192]{1,0:T(8,128)(2,1)}, u32[]{:S(2)}, u32[]{:S(2)}) collective-permute-start(bf16[128,8192]{1,0:T(8,128)(2,1)} %get-tuple-element.21), channel_id=1, source_target_pairs={{0,1},{1,0},{2,3},{3,2},{4,5},{5,4},{6,7},{7,6}} | collective-permute-start | bytes 6291464 | tf_op jit(solution)/shard_map/ppermute | solution.py:160
  457.0 412.1 %collective-permute-start.38 = (bf16[128,8192]{1,0:T(8,128)(2,1)}, bf16[128,8192]{1,0:T(8,128)(2,1)}, u32[]{:S(2)}, u32[]{:S(2)}) collective-permute-start(bf16[128,8192]{1,0:T(8,128)(2,1)} %get-tuple-element.21), channel_id=1, source_target_pairs={{0,5},{1,4},{2,7},{3,6},{4,1},{5,0},{6,3},{7,2}} | collective-permute-start | bytes 6291464 | tf_op jit(solution)/shard_map/ppermute | solution.py:160
  461.7 410.6 %collective-permute-start.39 = (bf16[128,8192]{1,0:T(8,128)(2,1)}, bf16[128,8192]{1,0:T(8,128)(2,1)}, u32[]{:S(2)}, u32[]{:S(2)}) collective-permute-start(bf16[128,8192]{1,0:T(8,128)(2,1)} %get-tuple-element.20), channel_id=1, source_target_pairs={{0,2},{1,3},{2,0},{3,1},{4,6},{5,7},{6,4},{7,5}} | collective-permute-start | bytes 6291464 | tf_op jit(solution)/shard_map/ppermute | solution.py:160
  493.8 383.2 %collective-permute-start.40 = (bf16[128,8192]{1,0:T(8,128)(2,1)}, bf16[128,8192]{1,0:T(8,128)(2,1)}, u32[]{:S(2)}, u32[]{:S(2)}) collective-permute-start(bf16[128,8192]{1,0:T(8,128)(2,1)} %get-tuple-element.20), channel_id=1, source_target_pairs={{0,6},{1,7},{2,4},{3,5},{4,2},{5,3},{6,0},{7,1}} | collective-permute-start | bytes 6291464 | tf_op jit(solution)/shard_map/ppermute | solution.py:160
  538.7 322.4 %collective-permute-start.36 = (bf16[128,8192]{1,0:T(8,128)(2,1)}, bf16[128,8192]{1,0:T(8,128)(2,1)}, u32[]{:S(2)}, u32[]{:S(2)}) collective-permute-start(bf16[128,8192]{1,0:T(8,128)(2,1)} %get-tuple-element.30), channel_id=1, source_target_pairs={{0,4},{1,5},{2,6},{3,7},{4,0},{5,1},{6,2},{7,3}} | collective-permute-start | bytes 6291464 | tf_op jit(solution)/shard_map/ppermute | solution.py:160
  861.1 47.9 %collective-permute-start.41 = (bf16[128,8192]{1,0:T(8,128)(2,1)S(1)}, bf16[128,8192]{1,0:T(8,128)(2,1)S(1)}, u32[]{:S(2)}, u32[]{:S(2)}) collective-permute-start(bf16[128,8192]{1,0:T(8,128)(2,1)S(1)} %copy-done.1), channel_id=1, source_target_pairs={{0,3},{1,2},{2,1},{3,0},{4,7},{5,6},{6,5},{7,4}} | collective-permute-start | bytes 6291464 | tf_op jit(solution)/shard_map/ppermute | solution.py:160
  864.3 89.7 %collective-permute-start.42 = (bf16[128,8192]{1,0:T(8,128)(2,1)S(1)}, bf16[128,8192]{1,0:T(8,128)(2,1)S(1)}, u32[]{:S(2)}, u32[]{:S(2)}) collective-permute-start(bf16[128,8192]{1,0:T(8,128)(2,1)S(1)} %copy-done.1), channel_id=1, source_target_pairs={{0,7},{1,6},{2,5},{3,4},{4,3},{5,2},{6,1},{7,0}} | collective-permute-start | bytes 6291464 | tf_op jit(solution)/shard_map/ppermute | solution.py:160
  869.1 330.3 %collective-permute-start.51 = (bf16[128,8192]{1,0:T(8,128)(2,1)}, bf16[128,8192]{1,0:T(8,128)(2,1)}, u32[]{:S(2)}, u32[]{:S(2)}) collective-permute-start(bf16[128,8192]{1,0:T(8,128)(2,1)} %get-tuple-element.18), channel_id=1, source_target_pairs={{0,1},{1,0},{2,3},{3,2},{4,5},{5,4},{6,7},{7,6}} | collective-permute-start | bytes 6291464 | tf_op jit(solution)/shard_map/ppermute | solution.py:160
  872.3 331.9 %collective-permute-start.52 = (bf16[128,8192]{1,0:T(8,128)(2,1)}, bf16[128,8192]{1,0:T(8,128)(2,1)}, u32[]{:S(2)}, u32[]{:S(2)}) collective-permute-start(bf16[128,8192]{1,0:T(8,128)(2,1)} %get-tuple-element.18), channel_id=1, source_target_pairs={{0,5},{1,4},{2,7},{3,6},{4,1},{5,0},{6,3},{7,2}} | collective-permute-start | bytes 6291464 | tf_op jit(solution)/shard_map/ppermute | solution.py:160
  877.0 331.8 %collective-permute-start.53 = (bf16[128,8192]{1,0:T(8,128)(2,1)}, bf16[128,8192]{1,0:T(8,128)(2,1)}, u32[]{:S(2)}, u32[]{:S(2)}) collective-permute-start(bf16[128,8192]{1,0:T(8,128)(2,1)} %get-tuple-element.28), channel_id=1, source_target_pairs={{0,2},{1,3},{2,0},{3,1},{4,6},{5,7},{6,4},{7,5}} | collective-permute-start | bytes 6291464 | tf_op jit(solution)/shard_map/ppermute | solution.py:160
  909.1 303.3 %collective-permute-start.54 = (bf16[128,8192]{1,0:T(8,128)(2,1)}, bf16[128,8192]{1,0:T(8,128)(2,1)}, u32[]{:S(2)}, u32[]{:S(2)}) collective-permute-start(bf16[128,8192]{1,0:T(8,128)(2,1)} %get-tuple-element.28), channel_id=1, source_target_pairs={{0,6},{1,7},{2,4},{3,5},{4,2},{5,3},{6,0},{7,1}} | collective-permute-start | bytes 6291464 | tf_op jit(solution)/shard_map/ppermute | solution.py:160
  954.0 242.3 %collective-permute-start.50 = (bf16[128,8192]{1,0:T(8,128)(2,1)}, bf16[128,8192]{1,0:T(8,128)(2,1)}, u32[]{:S(2)}, u32[]{:S(2)}) collective-permute-start(bf16[128,8192]{1,0:T(8,128)(2,1)} %get-tuple-element.8), channel_id=1, source_target_pairs={{0,4},{1,5},{2,6},{3,7},{4,0},{5,1},{6,2},{7,3}} | collective-permute-start | bytes 6291464 | tf_op jit(solution)/shard_map/ppermute | solution.py:160
  1196.3 47.9 %collective-permute-start.55 = (bf16[128,8192]{1,0:T(8,128)(2,1)S(1)}, bf16[128,8192]{1,0:T(8,128)(2,1)S(1)}, u32[]{:S(2)}, u32[]{:S(2)}) collective-permute-start(bf16[128,8192]{1,0:T(8,128)(2,1)S(1)} %copy-done), channel_id=1, source_target_pairs={{0,3},{1,2},{2,1},{3,0},{4,7},{5,6},{6,5},{7,4}} | collective-permute-start | bytes 6291464 | tf_op jit(solution)/shard_map/ppermute | solution.py:160
  1199.4 88.5 %collective-permute-start.56 = (bf16[128,8192]{1,0:T(8,128)(2,1)S(1)}, bf16[128,8192]{1,0:T(8,128)(2,1)S(1)}, u32[]{:S(2)}, u32[]{:S(2)}) collective-permute-start(bf16[128,8192]{1,0:T(8,128)(2,1)S(1)} %copy-done), channel_id=1, source_target_pairs={{0,7},{1,6},{2,5},{3,4},{4,3},{5,2},{6,1},{7,0}} | collective-permute-start | bytes 6291464 | tf_op jit(solution)/shard_map/ppermute | solution.py:160
  1204.2 462.4 %collective-permute-start = (bf16[512,8192]{1,0:T(8,128)(2,1)}, bf16[512,8192]{1,0:T(8,128)(2,1)}, u32[]{:S(2)}, u32[]{:S(2)}) collective-permute-start(bf16[512,8192]{1,0:T(8,128)(2,1)} %get-tuple-element.16), channel_id=1, source_target_pairs={{0,4},{1,5},{2,6},{3,7},{4,0},{5,1},{6,2},{7,3}} | collective-permute-start | bytes 25165832 | tf_op jit(solution)/shard_map/ppermute | solution.py:160
  1208.8 459.2 %collective-permute-start.1 = (bf16[512,8192]{1,0:T(8,128)(2,1)}, bf16[512,8192]{1,0:T(8,128)(2,1)}, u32[]{:S(2)}, u32[]{:S(2)}) collective-permute-start(bf16[512,8192]{1,0:T(8,128)(2,1)} %get-tuple-element.15), channel_id=1, source_target_pairs={{0,4},{1,5},{2,6},{3,7},{4,0},{5,1},{6,2},{7,3}} | collective-permute-start | bytes 25165832 | tf_op jit(solution)/shard_map/ppermute | solution.py:160
  1516.5 219.4 %collective-permute-start.15 = (bf16[128,4096]{1,0:T(8,128)(2,1)}, bf16[128,4096]{1,0:T(8,128)(2,1)}, u32[]{:S(2)}, u32[]{:S(2)}) collective-permute-start(bf16[128,4096]{1,0:T(8,128)(2,1)} %get-tuple-element.65), channel_id=1, source_target_pairs={{0,4},{1,5},{2,6},{3,7},{4,0},{5,1},{6,2},{7,3}} | collective-permute-start | bytes 3145736 | tf_op jit(solution)/shard_map/ppermute | solution.py:160
  1518.5 217.5 %collective-permute-start.16 = (bf16[128,4096]{1,0:T(8,128)(2,1)}, bf16[128,4096]{1,0:T(8,128)(2,1)}, u32[]{:S(2)}, u32[]{:S(2)}) collective-permute-start(bf16[128,4096]{1,0:T(8,128)(2,1)} %get-tuple-element.64), channel_id=1, source_target_pairs={{0,1},{1,0},{2,3},{3,2},{4,5},{5,4},{6,7},{7,6}} | collective-permute-start | bytes 3145736 | tf_op jit(solution)/shard_map/ppermute | solution.py:160
  1586.6 213.8 %collective-permute-start.29 = (bf16[128,4096]{1,0:T(8,128)(2,1)}, bf16[128,4096]{1,0:T(8,128)(2,1)}, u32[]{:S(2)}, u32[]{:S(2)}) collective-permute-start(bf16[128,4096]{1,0:T(8,128)(2,1)} %get-tuple-element.57), channel_id=1, source_target_pairs={{0,4},{1,5},{2,6},{3,7},{4,0},{5,1},{6,2},{7,3}} | collective-permute-start | bytes 3145736 | tf_op jit(solution)/shard_map/ppermute | solution.py:160
  1666.6 183.6 %collective-permute-start.4 = (bf16[512,8192]{1,0:T(8,128)(2,1)}, bf16[512,8192]{1,0:T(8,128)(2,1)}, u32[]{:S(2)}, u32[]{:S(2)}) collective-permute-start(bf16[512,8192]{1,0:T(8,128)(2,1)} %collective-permute-done.refs_1_), channel_id=1, source_target_pairs={{0,2},{1,3},{2,0},{3,1},{4,6},{5,7},{6,4},{7,5}} | collective-permute-start | bytes 25165832 | tf_op jit(solution)/shard_map/ppermute | solution.py:160
  1668.0 361.5 %collective-permute-start.5 = (bf16[512,8192]{1,0:T(8,128)(2,1)}, bf16[512,8192]{1,0:T(8,128)(2,1)}, u32[]{:S(2)}, u32[]{:S(2)}) collective-permute-start(bf16[512,8192]{1,0:T(8,128)(2,1)} %collective-permute-done.1.refs_2_), channel_id=1, source_target_pairs={{0,2},{1,3},{2,0},{3,1},{4,6},{5,7},{6,4},{7,5}} | collective-permute-start | bytes 25165832 | tf_op jit(solution)/shard_map/ppermute | solution.py:160
  1735.9 64.6 %collective-permute-start.30 = (bf16[128,4096]{1,0:T(8,128)(2,1)S(1)}, bf16[128,4096]{1,0:T(8,128)(2,1)S(1)}, u32[]{:S(2)}, u32[]{:S(2)}) collective-permute-start(bf16[128,4096]{1,0:T(8,128)(2,1)S(1)} %copy-done.11), channel_id=1, source_target_pairs={{0,1},{1,0},{2,3},{3,2},{4,5},{5,4},{6,7},{7,6}} | collective-permute-start | bytes 3145736 | tf_op jit(solution)/shard_map/ppermute | solution.py:160
  1736.0 64.9 %collective-permute-start.43 = (bf16[128,4096]{1,0:T(8,128)(2,1)S(1)}, bf16[128,4096]{1,0:T(8,128)(2,1)S(1)}, u32[]{:S(2)}, u32[]{:S(2)}) collective-permute-start(bf16[128,4096]{1,0:T(8,128)(2,1)S(1)} %get-tuple-element.49), channel_id=1, source_target_pairs={{0,4},{1,5},{2,6},{3,7},{4,0},{5,1},{6,2},{7,3}} | collective-permute-start | bytes 3145736 | tf_op jit(solution)/shard_map/ppermute | solution.py:160
  1800.4 233.0 %collective-permute-start.44 = (bf16[128,4096]{1,0:T(8,128)(2,1)S(1)}, bf16[128,4096]{1,0:T(8,128)(2,1)S(1)}, u32[]{:S(2)}, u32[]{:S(2)}) collective-permute-start(bf16[128,4096]{1,0:T(8,128)(2,1)S(1)} %get-tuple-element.48), channel_id=1, source_target_pairs={{0,1},{1,0},{2,3},{3,2},{4,5},{5,4},{6,7},{7,6}} | collective-permute-start | bytes 3145736 | tf_op jit(solution)/shard_map/ppermute | solution.py:160
  1800.6 389.7 %collective-permute-start.2 = (bf16[512,8192]{1,0:T(8,128)(2,1)}, bf16[512,8192]{1,0:T(8,128)(2,1)S(1)}, u32[]{:S(2)}, u32[]{:S(2)}) collective-permute-start(bf16[512,8192]{1,0:T(8,128)(2,1)} %collective-permute-done.refs_1_), channel_id=1, source_target_pairs={{0,1},{1,0},{2,3},{3,2},{4,5},{5,4},{6,7},{7,6}} | collective-permute-start | bytes 25165832 | tf_op jit(solution)/shard_map/ppermute | solution.py:160
  1800.9 389.5 %collective-permute-start.3 = (bf16[512,8192]{1,0:T(8,128)(2,1)}, bf16[512,8192]{1,0:T(8,128)(2,1)S(1)}, u32[]{:S(2)}, u32[]{:S(2)}) collective-permute-start(bf16[512,8192]{1,0:T(8,128)(2,1)} %collective-permute-done.1.refs_2_), channel_id=1, source_target_pairs={{0,1},{1,0},{2,3},{3,2},{4,5},{5,4},{6,7},{7,6}} | collective-permute-start | bytes 25165832 | tf_op jit(solution)/shard_map/ppermute | solution.py:160
  1850.2 342.8 %collective-permute-start.6 = (bf16[512,8192]{1,0:T(8,128)(2,1)}, bf16[512,8192]{1,0:T(8,128)(2,1)}, u32[]{:S(2)}, u32[]{:S(2)}) collective-permute-start(bf16[512,8192]{1,0:T(8,128)(2,1)} %collective-permute-done.4.refs_5_), channel_id=1, source_target_pairs={{0,1},{1,0},{2,3},{3,2},{4,5},{5,4},{6,7},{7,6}} | collective-permute-start | bytes 25165832 | tf_op jit(solution)/shard_map/ppermute | solution.py:160
  2029.5 163.5 %collective-permute-start.7 = (bf16[512,8192]{1,0:T(8,128)(2,1)}, bf16[512,8192]{1,0:T(8,128)(2,1)}, u32[]{:S(2)}, u32[]{:S(2)}) collective-permute-start(bf16[512,8192]{1,0:T(8,128)(2,1)} %collective-permute-done.5.refs_6_), channel_id=1, source_target_pairs={{0,1},{1,0},{2,3},{3,2},{4,5},{5,4},{6,7},{7,6}} | collective-permute-start | bytes 25165832 | tf_op jit(solution)/shard_map/ppermute | solution.py:160
  2033.4 25.6 %collective-permute-start.57 = (bf16[128,4096]{1,0:T(8,128)(2,1)S(1)}, bf16[128,4096]{1,0:T(8,128)(2,1)S(1)}, u32[]{:S(2)}, u32[]{:S(2)}) collective-permute-start(bf16[128,4096]{1,0:T(8,128)(2,1)S(1)} %get-tuple-element.41), channel_id=1, source_target_pairs={{0,4},{1,5},{2,6},{3,7},{4,0},{5,1},{6,2},{7,3}} | collective-permute-start | bytes 3145736 | tf_op jit(solution)/shard_map/ppermute | solution.py:160
  2059.0 2.7 collective-permute-start.58
  2061.7 25.1 collective-permute-start.59
  2086.8 25.2 collective-permute-start.60
  2112.0 25.2 collective-permute-start.61
  2137.3 25.4 collective-permute-start.62
  2162.7 26.1 %collective-permute-start.63 = (bf16[128,4096]{1,0:T(8,128)(2,1)S(1)}, bf16[128,4096]{1,0:T(8,128)(2,1)S(1)}, u32[]{:S(2)}, u32[]{:S(2)}) collective-permute-start(bf16[128,4096]{1,0:T(8,128)(2,1)S(1)} %get-tuple-element.35), channel_id=1, source_target_pairs={{0,7},{1,6},{2,5},{3,4},{4,3},{5,2},{6,1},{7,0}} | collective-permute-start | bytes 3145736 | tf_op jit(solution)/shard_map/ppermute | solution.py:160
  2188.8 88.3 %collective-permute-start.45 = (bf16[128,4096]{1,0:T(8,128)(2,1)}, bf16[128,4096]{1,0:T(8,128)(2,1)S(1)}, u32[]{:S(2)}, u32[]{:S(2)}) collective-permute-start(bf16[128,4096]{1,0:T(8,128)(2,1)} %get-tuple-element.47), channel_id=1, source_target_pairs={{0,5},{1,4},{2,7},{3,6},{4,1},{5,0},{6,3},{7,2}} | collective-permute-start | bytes 3145736 | tf_op jit(solution)/shard_map/ppermute | solution.py:160
  2190.2 87.9 %collective-permute-start.46 = (bf16[128,4096]{1,0:T(8,128)(2,1)}, bf16[128,4096]{1,0:T(8,128)(2,1)S(1)}, u32[]{:S(2)}, u32[]{:S(2)}) collective-permute-start(bf16[128,4096]{1,0:T(8,128)(2,1)} %get-tuple-element.46), channel_id=1, source_target_pairs={{0,2},{1,3},{2,0},{3,1},{4,6},{5,7},{6,4},{7,5}} | collective-permute-start | bytes 3145736 | tf_op jit(solution)/shard_map/ppermute | solution.py:160
  2190.4 87.7 %collective-permute-start.47 = (bf16[128,4096]{1,0:T(8,128)(2,1)}, bf16[128,4096]{1,0:T(8,128)(2,1)}, u32[]{:S(2)}, u32[]{:S(2)}) collective-permute-start(bf16[128,4096]{1,0:T(8,128)(2,1)} %get-tuple-element.45), channel_id=1, source_target_pairs={{0,6},{1,7},{2,4},{3,5},{4,2},{5,3},{6,0},{7,1}} | collective-permute-start | bytes 3145736 | tf_op jit(solution)/shard_map/ppermute | solution.py:160
  2193.0 87.6 %collective-permute-start.48 = (bf16[128,4096]{1,0:T(8,128)(2,1)S(1)}, bf16[128,4096]{1,0:T(8,128)(2,1)}, u32[]{:S(2)}, u32[]{:S(2)}) collective-permute-start(bf16[128,4096]{1,0:T(8,128)(2,1)S(1)} %get-tuple-element.44), channel_id=1, source_target_pairs={{0,3},{1,2},{2,1},{3,0},{4,7},{5,6},{6,5},{7,4}} | collective-permute-start | bytes 3145736 | tf_op jit(solution)/shard_map/ppermute | solution.py:160
  2193.0 90.1 %collective-permute-start.49 = (bf16[128,4096]{1,0:T(8,128)(2,1)S(1)}, bf16[128,4096]{1,0:T(8,128)(2,1)}, u32[]{:S(2)}, u32[]{:S(2)}) collective-permute-start(bf16[128,4096]{1,0:T(8,128)(2,1)S(1)} %get-tuple-element.43), channel_id=1, source_target_pairs={{0,7},{1,6},{2,5},{3,4},{4,3},{5,2},{6,1},{7,0}} | collective-permute-start | bytes 3145736 | tf_op jit(solution)/shard_map/ppermute | solution.py:160
  2277.1 88.8 %collective-permute-start.31 = (bf16[128,4096]{1,0:T(8,128)(2,1)}, bf16[128,4096]{1,0:T(8,128)(2,1)S(1)}, u32[]{:S(2)}, u32[]{:S(2)}) collective-permute-start(bf16[128,4096]{1,0:T(8,128)(2,1)} %get-tuple-element.55), channel_id=1, source_target_pairs={{0,5},{1,4},{2,7},{3,6},{4,1},{5,0},{6,3},{7,2}} | collective-permute-start | bytes 3145736 | tf_op jit(solution)/shard_map/ppermute | solution.py:160
  2278.1 88.2 %collective-permute-start.32 = (bf16[128,4096]{1,0:T(8,128)(2,1)}, bf16[128,4096]{1,0:T(8,128)(2,1)S(1)}, u32[]{:S(2)}, u32[]{:S(2)}) collective-permute-start(bf16[128,4096]{1,0:T(8,128)(2,1)} %get-tuple-element.54), channel_id=1, source_target_pairs={{0,2},{1,3},{2,0},{3,1},{4,6},{5,7},{6,4},{7,5}} | collective-permute-start | bytes 3145736 | tf_op jit(solution)/shard_map/ppermute | solution.py:160
  2278.1 89.7 %collective-permute-start.33 = (bf16[128,4096]{1,0:T(8,128)(2,1)}, bf16[128,4096]{1,0:T(8,128)(2,1)}, u32[]{:S(2)}, u32[]{:S(2)}) collective-permute-start(bf16[128,4096]{1,0:T(8,128)(2,1)} %get-tuple-element.53), channel_id=1, source_target_pairs={{0,6},{1,7},{2,4},{3,5},{4,2},{5,3},{6,0},{7,1}} | collective-permute-start | bytes 3145736 | tf_op jit(solution)/shard_map/ppermute | solution.py:160
  2280.6 88.4 %collective-permute-start.34 = (bf16[128,4096]{1,0:T(8,128)(2,1)}, bf16[128,4096]{1,0:T(8,128)(2,1)}, u32[]{:S(2)}, u32[]{:S(2)}) collective-permute-start(bf16[128,4096]{1,0:T(8,128)(2,1)} %get-tuple-element.52), channel_id=1, source_target_pairs={{0,3},{1,2},{2,1},{3,0},{4,7},{5,6},{6,5},{7,4}} | collective-permute-start | bytes 3145736 | tf_op jit(solution)/shard_map/ppermute | solution.py:160
  2283.1 89.9 %collective-permute-start.35 = (bf16[128,4096]{1,0:T(8,128)(2,1)}, bf16[128,4096]{1,0:T(8,128)(2,1)}, u32[]{:S(2)}, u32[]{:S(2)}) collective-permute-start(bf16[128,4096]{1,0:T(8,128)(2,1)} %get-tuple-element.51), channel_id=1, source_target_pairs={{0,7},{1,6},{2,5},{3,4},{4,3},{5,2},{6,1},{7,0}} | collective-permute-start | bytes 3145736 | tf_op jit(solution)/shard_map/ppermute | solution.py:160
  2365.9 90.3 %collective-permute-start.17 = (bf16[128,4096]{1,0:T(8,128)(2,1)S(1)}, bf16[128,4096]{1,0:T(8,128)(2,1)S(1)}, u32[]{:S(2)}, u32[]{:S(2)}) collective-permute-start(bf16[128,4096]{1,0:T(8,128)(2,1)S(1)} %copy-done.10), channel_id=1, source_target_pairs={{0,5},{1,4},{2,7},{3,6},{4,1},{5,0},{6,3},{7,2}} | collective-permute-start | bytes 3145736 | tf_op jit(solution)/shard_map/ppermute | solution.py:160
  2366.3 89.9 %collective-permute-start.18 = (bf16[128,4096]{1,0:T(8,128)(2,1)S(1)}, bf16[128,4096]{1,0:T(8,128)(2,1)S(1)}, u32[]{:S(2)}, u32[]{:S(2)}) collective-permute-start(bf16[128,4096]{1,0:T(8,128)(2,1)S(1)} %copy-done.9), channel_id=1, source_target_pairs={{0,2},{1,3},{2,0},{3,1},{4,6},{5,7},{6,4},{7,5}} | collective-permute-start | bytes 3145736 | tf_op jit(solution)/shard_map/ppermute | solution.py:160
  2367.8 88.4 %collective-permute-start.19 = (bf16[128,4096]{1,0:T(8,128)(2,1)S(1)}, bf16[128,4096]{1,0:T(8,128)(2,1)S(1)}, u32[]{:S(2)}, u32[]{:S(2)}) collective-permute-start(bf16[128,4096]{1,0:T(8,128)(2,1)S(1)} %copy-done.8), channel_id=1, source_target_pairs={{0,6},{1,7},{2,4},{3,5},{4,2},{5,3},{6,0},{7,1}} | collective-permute-start | bytes 3145736 | tf_op jit(solution)/shard_map/ppermute | solution.py:160
  2369.0 87.2 %collective-permute-start.20 = (bf16[128,4096]{1,0:T(8,128)(2,1)S(1)}, bf16[128,4096]{1,0:T(8,128)(2,1)S(1)}, u32[]{:S(2)}, u32[]{:S(2)}) collective-permute-start(bf16[128,4096]{1,0:T(8,128)(2,1)S(1)} %copy-done.7), channel_id=1, source_target_pairs={{0,3},{1,2},{2,1},{3,0},{4,7},{5,6},{6,5},{7,4}} | collective-permute-start | bytes 3145736 | tf_op jit(solution)/shard_map/ppermute | solution.py:160
  2373.0 89.8 %collective-permute-start.21 = (bf16[128,4096]{1,0:T(8,128)(2,1)S(1)}, bf16[128,4096]{1,0:T(8,128)(2,1)}, u32[]{:S(2)}, u32[]{:S(2)}) collective-permute-start(bf16[128,4096]{1,0:T(8,128)(2,1)S(1)} %copy-done.6), channel_id=1, source_target_pairs={{0,7},{1,6},{2,5},{3,4},{4,3},{5,2},{6,1},{7,0}} | collective-permute-start | bytes 3145736 | tf_op jit(solution)/shard_map/ppermute | solution.py:160
  (21 other events, 979.4 us)

commit v2 on v1

v2 whole, which is shorter than its diff:
```python
import functools
import math
import jax
import jax.numpy as jnp
from jax import lax
from jax.experimental import pallas as pl
from jax.experimental.pallas import tpu as pltpu
from jax.sharding import PartitionSpec as P

HEAD_DIM = 128
ROPE_BASE = 500000
Q_TILE = 256
STEP_HEADS = 2
EXP_SCALE = math.log2(math.e) / math.sqrt(HEAD_DIM)
W_PIECES = 2
QKV_TILE = 512
OUT_TILE = 512
CP_SIZE = 4
OWN = 4
NEAR = (0, 2)


def rope_tables(pos_vals):
    inv_freq = jnp.asarray([ROPE_BASE ** (-2.0 * freq_idx / HEAD_DIM) for freq_idx in range(HEAD_DIM // 2)], dtype=jnp.float32)
    angles = pos_vals.astype(jnp.float32)[..., None] * inv_freq
    cos_t, sin_t = jnp.cos(angles), jnp.sin(angles)
    return jnp.concatenate([cos_t, cos_t], axis=-1), jnp.concatenate([-sin_t, sin_t], axis=-1)


def attend_kernel(sources, place_ref, *refs):
    n_chunks = place_ref.shape[1]
    qkv_refs, (cos_ref, sin_ref) = refs[:6], refs[6:8]
    o_refs, (q_seq, k_seq, v_seq, o_seq) = refs[8:8 + n_chunks], refs[8 + n_chunks:]
    n_rows, step_w = q_seq.shape
    chunk = n_rows // n_chunks
    heads = [slice(h * HEAD_DIM, (h + 1) * HEAD_DIM) for h in range(step_w // HEAD_DIM)]
    for m, (which, first) in enumerate(sources):
        q_ref, k_ref, v_ref = qkv_refs[which::2]
        src, tab = slice(first, first + chunk), slice(m * chunk, (m + 1) * chunk)
        dst = pl.ds(pl.multiple_of(place_ref[0, m] * chunk, chunk), chunk)
        cos_t, sin_t = cos_ref[tab, :], sin_ref[tab, :]
        for cols in heads:
            for in_ref, out_ref in ((q_ref, q_seq), (k_ref, k_seq)):
                vals = in_ref[src, cols].astype(jnp.float32)
                out_ref[dst, cols] = (vals * cos_t + pltpu.roll(vals, HEAD_DIM // 2, 1) * sin_t).astype(jnp.bfloat16)
        v_seq[dst, :] = v_ref[src, :]
    tile = min(Q_TILE, n_rows)
    below = lax.broadcasted_iota(jnp.int32, (tile, tile), 1) <= lax.broadcasted_iota(jnp.int32, (tile, tile), 0)
    contract_last = (((1,), (1,)), ((), ()))
    for j in range(n_rows // tile):
        for cols in heads:
            here = slice(j * tile, (j + 1) * tile)
            q_tile = q_seq[here, cols]
            s_diag = lax.dot_general(q_tile, k_seq[here, cols], contract_last, preferred_element_type=jnp.float32)
            s_diag = jnp.where(below, s_diag, -jnp.inf)
            row_max = jnp.max(s_diag, axis=1, keepdims=True)
            if j:
                s_prev = lax.dot_general(q_tile, k_seq[:j * tile, cols], contract_last, preferred_element_type=jnp.float32)
                row_max = jnp.maximum(row_max, jnp.max(s_prev, axis=1, keepdims=True))
            p_diag = jnp.exp2((s_diag - row_max) * EXP_SCALE)
            row_sum = jnp.sum(p_diag, axis=1, keepdims=True)
            acc = jnp.dot(p_diag.astype(jnp.bfloat16), v_seq[here, cols], preferred_element_type=jnp.float32)
            if j:
                p_prev = jnp.exp2((s_prev - row_max) * EXP_SCALE)
                row_sum = row_sum + jnp.sum(p_prev, axis=1, keepdims=True)
                acc = acc + jnp.dot(p_prev.astype(jnp.bfloat16), v_seq[:j * tile, cols], preferred_element_type=jnp.float32)
            o_seq[here, cols] = (acc / row_sum).astype(jnp.bfloat16)
    for m, o_ref in enumerate(o_refs):
        o_ref[...] = o_seq[pl.ds(pl.multiple_of(place_ref[0, m] * chunk, chunk), chunk), :]


def attend(place, qkv_near, qkv_far, s, near, cos_t, sin_t):
    n_rows, n_peers = cos_t.shape[0], place.shape[1]
    chunk = n_rows // n_peers
    width = qkv_far.shape[1] // 3
    step_w = STEP_HEADS * HEAD_DIM
    steps = width // step_w
    near_rows = len(near) * chunk
    far = [m for m in range(n_peers) if m not in near]
    sources = [(0, near.index(m) * chunk) if m in near else (1, far.index(m) * chunk) for m in range(n_peers)]
    qkv_specs = []
    for part in range(3):
        qkv_specs.append(pl.BlockSpec((near_rows, step_w), lambda g, place_ref, part=part: (s, part * steps + g)))
        qkv_specs.append(pl.BlockSpec((len(far) * chunk, step_w), lambda g, place_ref, part=part: (0, part * steps + g)))
    table_spec = pl.BlockSpec((n_rows, HEAD_DIM), lambda g, place_ref: (0, 0))
    out_spec = pl.BlockSpec((chunk, step_w), lambda g, place_ref: (0, g))
    flops = 2 * n_rows * n_rows * width
    return pl.pallas_call(
        functools.partial(attend_kernel, sources),
        out_shape=[jax.ShapeDtypeStruct((chunk, width), jnp.bfloat16)] * n_peers,
        grid_spec=pltpu.PrefetchScalarGridSpec(
            num_scalar_prefetch=1, grid=(steps,),
            in_specs=qkv_specs + [table_spec] * 2, out_specs=[out_spec] * n_peers,
            scratch_shapes=[pltpu.VMEM((n_rows, step_w), jnp.bfloat16)] * 4),
        compiler_params=pltpu.CompilerParams(dimension_semantics=('arbitrary',), vmem_limit_bytes=48 * 2 ** 20),
        cost_estimate=pl.CostEstimate(flops=4 * flops, bytes_accessed=8 * n_rows * width, transcendentals=n_rows * n_rows * width // HEAD_DIM // 2),
        name='attend',
    )(place, *[qkv_near, qkv_far] * 3, cos_t, sin_t)


def fetch_all(copies, sems):
    copies = [pltpu.make_async_copy(src, dst, sems.at[n]) for n, (src, dst) in enumerate(copies)]
    for copy in copies:
        copy.start()
    return copies


def qkv_kernel(n_rows_in, picks, cp_ref, *refs):
    rows_in, w_refs = refs[:n_rows_in], refs[n_rows_in:n_rows_in + 3]
    out_ref, x_all, w_buf, w_sems, x_sems = refs[n_rows_in + 3:]
    step, last = pl.program_id(0), pl.num_programs(0) - 1
    n_tile = w_buf.shape[2]
    per_w = w_refs[0].shape[1] // n_tile

    def fetch(index, act):
        slot = lax.rem(index, 2)
        for part, w_ref in enumerate(w_refs):
            @pl.when(lax.div(index, per_w) == part)
            def _():
                cols = pl.ds(pl.multiple_of((index - part * per_w) * n_tile, n_tile), n_tile)
                getattr(pltpu.make_async_copy(w_ref.at[:, cols], w_buf.at[slot], w_sems.at[slot]), act)()

    @pl.when(step == 0)
    def _():
        fetch(step, 'start')
        copies = []
        first = 0
        for which, index in picks:
            src = rows_in[which]
            if index is not None:
                src = src.at[index * CP_SIZE + cp_ref[0]] if index < OWN else src.at[index - OWN]
            chunk = src.shape[0]
            copies.append((src, x_all.at[pl.ds(first, chunk), :]))
            first += chunk
        for copy in fetch_all(copies, x_sems):
            copy.wait()

    @pl.when(step < last)
    def _():
        fetch(step + 1, 'start')

    fetch(step, 'wait')
    out_ref[...] = jnp.dot(x_all[...], w_buf[lax.rem(step, 2)], preferred_element_type=jnp.float32).astype(jnp.bfloat16)


def project(cp_i, rows_in, picks, chunk, weights, n_tile=QKV_TILE):
    dim, width = weights[0].shape
    n_tile = min(n_tile, width)
    n_rows = len(picks) * chunk
    any_spec = pl.BlockSpec(memory_space=pl.ANY)
    return pl.pallas_call(
        functools.partial(qkv_kernel, len(rows_in), picks),
        out_shape=jax.ShapeDtypeStruct((n_rows, 3 * width), jnp.bfloat16),
        grid_spec=pltpu.PrefetchScalarGridSpec(
            num_scalar_prefetch=1, grid=(3 * width // n_tile,), in_specs=[any_spec] * (len(rows_in) + 3),
            out_specs=pl.BlockSpec((n_rows, n_tile), lambda g, cp_ref: (0, g)),
            scratch_shapes=[pltpu.VMEM((n_rows, dim), jnp.bfloat16), pltpu.VMEM((2, dim, n_tile), jnp.bfloat16),
                            pltpu.SemaphoreType.DMA((2,)), pltpu.SemaphoreType.DMA((len(picks),))]),
        compiler_params=pltpu.CompilerParams(dimension_semantics=('arbitrary',), vmem_limit_bytes=58 * 2 ** 20),
        cost_estimate=pl.CostEstimate(flops=6 * n_rows * dim * width, bytes_accessed=6 * dim * width + 2 * n_rows * (dim + 3 * width), transcendentals=0),
        name='project',
    )(cp_i, *rows_in, *weights)


def out_kernel(n_w, placed, part_w, cp_ref, *refs):
    w_refs, pieces = refs[:n_w], refs[n_w:n_w + len(placed)]
    add_ref = refs[n_w + len(placed)]
    out_ref, o_all, sems = refs[-3:]
    chunk, width = pieces[0].shape
    cp_i = cp_ref[0]

    @pl.when(pl.program_id(0) == 0)
    def _():
        copies = []
        for piece, (group, mc, first, split) in zip(pieces, placed):
            rows = pl.ds(pl.multiple_of((group * CP_SIZE + (cp_i ^ mc)) * chunk, chunk), chunk)
            if not split:
                copies.append((piece, o_all.at[rows, pl.ds(first, width)]))
                continue
            for part in range(CP_SIZE):
                cols = pl.ds(pl.multiple_of((cp_i ^ part) * part_w, part_w), part_w)
                copies.append((piece.at[:, cols], o_all.at[rows, pl.ds(first + part * part_w, part_w)]))
        for copy in fetch_all(copies, sems):
            copy.wait()

    first, acc = 0, None
    for w_ref in w_refs:
        depth = w_ref.shape[0]
        term = jnp.dot(o_all[:, first:first + depth], w_ref[...], preferred_element_type=jnp.float32)
        acc = term if acc is None else acc + term
        first += depth
    out_ref[...] = (add_ref[...].astype(jnp.float32) + acc).astype(out_ref.dtype)


def out_project(cp_i, w_parts, pieces, placed, addend, out_type, row_block, buf=None, n_tile=OUT_TILE):
    chunk, width = pieces[0].shape
    depth = sum(w.shape[0] for w in w_parts)
    n_rows = chunk * len(pieces) * width // depth
    dim = addend.shape[1]
    n_tile = min(n_tile, dim)
    any_spec = pl.BlockSpec(memory_space=pl.ANY)
    row_spec = pl.BlockSpec((n_rows, n_tile), lambda g, cp_ref: (row_block, g))
    operands = [*w_parts, *pieces, addend]
    in_specs = [pl.BlockSpec((w.shape[0], n_tile), lambda g, cp_ref: (0, g)) for w in w_parts] + [any_spec] * len(pieces) + [row_spec]
    aliases = {}
    if buf is not None:
        aliases = {1 + len(operands): 0}
        operands.append(buf)
        in_specs.append(any_spec)
    return pl.pallas_call(
        functools.partial(out_kernel, len(w_parts), placed, width // CP_SIZE),
        out_shape=out_type,
        grid_spec=pltpu.PrefetchScalarGridSpec(
            num_scalar_prefetch=1, grid=(dim // n_tile,), in_specs=in_specs, out_specs=row_spec,
            scratch_shapes=[pltpu.VMEM((n_rows, depth), jnp.bfloat16), pltpu.SemaphoreType.DMA((CP_SIZE * len(pieces),))]),
        input_output_aliases=aliases,
        compiler_params=pltpu.CompilerParams(dimension_semantics=('arbitrary',), vmem_limit_bytes=52 * 2 ** 20),
        cost_estimate=pl.CostEstimate(flops=2 * n_rows * depth * dim, bytes_accessed=2 * depth * dim + 2 * n_rows * (depth + 2 * dim), transcendentals=0),
        name='out_project',
    )(cp_i, *operands)


def solution(mesh):
    cp_size, tp_size = mesh.shape['cp'], mesh.shape['tp']
    n_peers = cp_size * tp_size
    row_spec = P('data', ('cp', 'tp'))

    def swap(vals, m):
        if not m:
            return vals
        mc, mt = m // tp_size, m % tp_size
        pairs = [(t * cp_size + c, (t ^ mt) * cp_size + (c ^ mc)) for t in range(tp_size) for c in range(cp_size)]
        return lax.ppermute(vals, ('tp', 'cp'), pairs)

    def local_fn(x_rows, pos_rows, w_query, w_key, w_value, w_out):
        n_seqs, chunk, dim = x_rows.shape
        n_own = n_seqs // cp_size
        cp_i, tp_i = lax.axis_index('cp'), lax.axis_index('tp')
        me = cp_i * tp_size + tp_i
        peers = me ^ jnp.arange(n_peers, dtype=jnp.int32)
        peer_cp, peer_tp = peers // tp_size, peers % tp_size
        block_of = jnp.where(peer_tp == 0, peer_cp, 2 * cp_size - 1 - peer_cp)
        chunk_of = jnp.argmax(block_of[None, :] == jnp.arange(n_peers, dtype=jnp.int32)[:, None], axis=1).astype(jnp.int32)
        place = jnp.stack([block_of, chunk_of]).astype(jnp.int32)
        pos_all = lax.all_gather(pos_rows, ('tp', 'cp'), axis=0, tiled=False)
        pos_all = jnp.take(pos_all, peer_tp * cp_size + peer_cp, axis=0)
        cp_ref = cp_i.reshape(1).astype(jnp.int32)
        weights = (w_query, w_key, w_value)
        far = [m for m in range(n_peers) if m not in NEAR]

        def seq_of(s, mc):
            return s * cp_size + (cp_i ^ mc)

        def rows_for(s, mc):
            return lax.dynamic_index_in_dim(x_rows, seq_of(s, mc), 0, keepdims=False)

        near_got = swap(jnp.stack([rows_for(s, 1) for s in range(n_own)]), NEAR[1])
        far_got = []
        for s in range(n_own):
            outgoing = [rows_for(s, mc) for mc in range(cp_size)]
            far_got.append([swap(outgoing[m // tp_size], m) for m in far])

        q_rows = w_out.shape[0] // cp_size
        piece_rows = q_rows // W_PIECES
        w_got = [[None] * W_PIECES for _ in range(cp_size)]
        for p in range(W_PIECES):
            mine = lax.dynamic_slice_in_dim(w_out, cp_i * q_rows + p * piece_rows, piece_rows, 0)
            w_got[0][p] = swap(mine, 1)
            w_got[1][p] = swap(w_got[0][p], tp_size)
            w_got[2][p] = swap(w_got[0][p], 2 * tp_size)
            w_got[3][p] = swap(w_got[2][p], tp_size)
        w_other = [piece for part in w_got for piece in part]

        picks = tuple(pick for s in range(n_own) for pick in ((0, s), (1, OWN + s)))
        qkv_near = project(cp_ref, [x_rows, near_got], picks, chunk, weights)
        o_got = []
        for s in range(n_own):
            pos_seq = lax.dynamic_index_in_dim(pos_all, seq_of(s, 0), 1, keepdims=False).reshape(-1)
            cos_t, sin_t = rope_tables(pos_seq)
            qkv_far = project(cp_ref, far_got[s], tuple((n, None) for n in range(len(far))), chunk, weights)
            o = attend(place, qkv_near, qkv_far, s, NEAR, cos_t, sin_t)
            got = []
            for m in range(n_peers):
                got.append(swap(o[m], m))
            o_got.append(got)

        x_flat = x_rows.reshape(n_seqs * chunk, dim)
        early = n_own - 1
        width = w_out.shape[0]
        y_type = jax.ShapeDtypeStruct(x_flat.shape, jnp.bfloat16)
        part_type = jax.ShapeDtypeStruct((early * cp_size * chunk, dim), jnp.float32)
        placed = [(s, mc, 0, False) for s in range(early) for mc in range(cp_size)]
        partial = out_project(cp_ref, [w_out], [o_got[s][mc * tp_size] for s, mc, _, _ in placed], placed, x_flat, part_type, 0)
        placed = [(s, mc, 0, True) for s in range(early) for mc in range(cp_size)]
        y = out_project(cp_ref, w_other, [o_got[s][mc * tp_size + 1] for s, mc, _, _ in placed], placed, partial, y_type, 0)
        placed = [(0, m // tp_size, (m % tp_size) * width, bool(m % tp_size)) for m in range(n_peers)]
        y = out_project(cp_ref, [w_out] + w_other, o_got[early], placed, x_flat, y_type, early, y)
        return y.reshape(n_seqs, chunk, dim)


    return jax.shard_map(local_fn, mesh=mesh,
                         in_specs=(row_spec, row_spec, P(None, 'tp'), P(None, 'tp'), P(None, 'tp'), P('tp', None)),
                         out_specs=row_spec, check_vma=False)
```

time: 2550 us -> 2350 us (0.922)
  matrix products: 958 us -> 0 us
  Pallas kernels: 574 us -> 1470 us
  local copies, waits for them, and re-layouts: 133 us -> 43.1 us
  waiting for transfers between devices: 674 us -> 608 us
    dot_general x12 -> x0, matrix products: 958 us -> none  [local_fn(): jnp.dot(x_seq, w, preferred_element_type=jnp.float32).astype(jnp.bfloat16)]
    pallas_call x8 -> x12, Pallas kernels: 574 us -> 1470 us  [the longest x5 896 us: project(): pl.pallas_call(functools.partial(qkv_kernel, len(rows_in), picks), out_sh...]
    unnamed x67 -> x96, local copies, waits for them, and re-layouts: 77.6 us -> 8.3 us
    ppermute x64 -> x61, waiting for transfers between devices: 674 us -> 608 us  [swap(): return lax.ppermute(vals, ('tp', 'cp'), pairs)]
    ppermute x64 -> x61, starting transfers between devices: 58.8 us -> 65.1 us  [swap(): return lax.ppermute(vals, ('tp', 'cp'), pairs)]
  transfers between devices with their start and end apart: 64 -> 61, of which waited for: 20 -> 15; matrix products, arithmetic and copies ran while one was open for 43% -> 1% of each run, Pallas kernels for 19% -> 59%
where the time goes in v2:
time: 2350 us; the launch traced here: 2340 us
  Pallas kernels  1470 us (63%)
  waiting for transfers between devices  608 us (26%)
  blocking collectives  139 us (6%)
  starting transfers between devices  65.1 us (3%)
  local copies, waits for them, and re-layouts  43.1 us (2%)
    pallas_call x5, Pallas kernels, project(): pl.pallas_call(functools.partial(qkv_kernel, len(rows_in), picks), out_sh...  896 us
    ppermute x61, waiting for transfers between devices, swap(): return lax.ppermute(vals, ('tp', 'cp'), pairs)  608 us
    pallas_call x3, Pallas kernels, out_project(): pl.pallas_call(functools.partial(out_kernel, len(w_parts), placed, width...  318 us
    pallas_call x4, Pallas kernels, attend(): pl.pallas_call(functools.partial(attend_kernel, sources), out_shape=[jax....  256 us
    all_gather x1, blocking collectives, local_fn(): pos_all = lax.all_gather(pos_rows, ('tp', 'cp'), axis=0, tiled=False)  139 us
    ppermute x61, starting transfers between devices, swap(): return lax.ppermute(vals, ('tp', 'cp'), pairs)  65.1 us
  transfers between devices with their start and end apart: 61, of which 15 were waited for; matrix products, arithmetic and copies ran while one was open for 1% of the time, Pallas kernels for 59%

profile of v2, /device:TPU:0, one launch (start us, length us, event | category | flops | bytes accessed | tf_op | source)
XLA Modules:
  0.0 2342.1 jit_solution(14085599522241285049)
XLA Ops:
  0.0 22.6 dynamic-slice_bitcast_fusion
  22.7 3.3 collective-permute-start.11
  26.0 1.5 collective-permute-start.12
  28.1 2.6 collective-permute-start.13
  30.7 139.2 %all-gather = s32[128,128]{1,0:T(8,128)S(1)} all-gather(s32[16,128]{1,0:T(8,128)S(1)} %copy-done.16), channel_id=2, replica_groups=mesh['data'=1,'tp'=2,'cp'=4] {'tp','cp'}, dimensions={0}, use_global_device_ids=true | all-gather | bytes 73728 | tf_op jit(solution)/shard_map/all_gather | solution.py:245
  171.4 7.5 fusion.3
  180.5 1.5 collective-permute-start.22
  182.0 1.3 collective-permute-start.23
  183.3 5.7 pad_maximum_fusion
  189.0 11.6 constant_dynamic-slice_fusion.8
  200.6 1.5 collective-permute-start.24
  202.7 26.7 %collective-permute-done.14.refs_5_ = bf16[128,8192]{1,0:T(8,128)(2,1)S(1)} collective-permute-done((bf16[128,8192]{1,0:T(8,128)(2,1)}, bf16[128,8192]{1,0:T(8,128)(2,1)S(1)}, u32[]{:S(2)}, u32[]{:S(2)}) %collective-permute-start.14) | collective-permute-done | bytes 2097184 | tf_op jit(solution)/shard_map/ppermute | solution.py:233
  229.5 44.7 %collective-permute-done.22.refs_0_ = bf16[128,8192]{1,0:T(8,128)(2,1)S(1)} collective-permute-done((bf16[128,8192]{1,0:T(8,128)(2,1)S(1)}, bf16[128,8192]{1,0:T(8,128)(2,1)S(1)}, u32[]{:S(2)}, u32[]{:S(2)}) %collective-permute-start.22) | collective-permute-done | bytes 2097184 | tf_op jit(solution)/shard_map/ppermute | solution.py:233
  274.2 1.5 collective-permute-start.27
  275.7 88.4 %collective-permute-done.23.refs_1_ = bf16[128,8192]{1,0:T(8,128)(2,1)S(1)} collective-permute-done((bf16[128,8192]{1,0:T(8,128)(2,1)S(1)}, bf16[128,8192]{1,0:T(8,128)(2,1)S(1)}, u32[]{:S(2)}, u32[]{:S(2)}) %collective-permute-start.23) | collective-permute-done | bytes 2097184 | tf_op jit(solution)/shard_map/ppermute | solution.py:233
  364.1 1.3 copy-done.19
  365.4 1.4 collective-permute-start.32
  366.8 168.5 %project.6.refs_1_.refs_3_.refs_5_ = bf16[768,12288]{1,0:T(8,128)(2,1)} custom-call(s32[1]{0:T(128)} %bitcast.cp_ref, bf16[128,8192]{1,0:T(8,128)(2,1)} %collective-permute-done.9.refs_0_, bf16[128,8192]{1,0:T(8,128)(2,1)} %collective-permute-done.10.refs_1_, bf16[128,8192]{1,0:T(8,128)(2,1)} %collective-permute-done.11.refs_2_, ...), custom_call_target="tpu_custom_call" | custom-call | flops 154618822656 | bytes 232783872 | tf_op jit(solution)/shard_map/project/pallas_call | solution.py:151
  536.0 1.4 collective-permute-start.35
  537.4 2.6 collective-permute-start.37
  540.0 168.6 %project.7.refs_1_.refs_3_.refs_5_ = bf16[768,12288]{1,0:T(8,128)(2,1)} custom-call(s32[1]{0:T(128)} %bitcast.cp_ref, bf16[128,8192]{1,0:T(8,128)(2,1)} %copy-done.18, bf16[128,8192]{1,0:T(8,128)(2,1)} %copy-done.19, bf16[128,8192]{1,0:T(8,128)(2,1)} %collective-permute-done.24.refs_2_, bf16[128,8192]{1,0:T(8,128)(2,1)} %collective-permute-done.25.refs_3_, ...), custom_call_target="tpu_custom_call" | custom-call | flops 154618822656 | bytes 232783872 | tf_op jit(solution)/shard_map/project/pallas_call | solution.py:151
  709.5 1.1 collective-permute-start.1
  710.9 1.4 collective-permute-start.42
  712.3 4.7 collective-permute-done.37.refs_5_
  716.9 1.9 collective-permute-start.43
  718.9 168.5 %project.8.refs_1_.refs_3_.refs_5_ = bf16[768,12288]{1,0:T(8,128)(2,1)} custom-call(s32[1]{0:T(128)} %bitcast.cp_ref, bf16[128,8192]{1,0:T(8,128)(2,1)} %collective-permute-done.32.refs_0_, bf16[128,8192]{1,0:T(8,128)(2,1)} %collective-permute-done.33.refs_1_, bf16[128,8192]{1,0:T(8,128)(2,1)} %collective-permute-done.34.refs_2_, ...), custom_call_target="tpu_custom_call" | custom-call | flops 154618822656 | bytes 232783872 | tf_op jit(solution)/shard_map/project/pallas_call | solution.py:151
  887.9 221.5 %project.5.refs_0_.refs_2_.refs_4_ = bf16[1024,12288]{1,0:T(8,128)(2,1)} custom-call(s32[1]{0:T(128)} %bitcast.cp_ref, bf16[16,128,8192]{2,1,0:T(8,128)(2,1)} %refs_0_.3, bf16[4,128,8192]{2,1,0:T(8,128)(2,1)} %collective-permute-done.8.refs_1_, bf16[8192,4096]{1,0:T(8,128)(2,1)} %refs_6_.7, bf16[8192,4096]{1,0:T(8,128)(2,1)} %refs_7_.7, ...), custom_call_target="tpu_custom_call" | custom-call | flops 206158430208 | bytes 243269632 | tf_op jit(solution)/shard_map/project/pallas_call | solution.py:151
  1109.4 64.5 %attend.4 = (bf16[128,4096]{1,0:T(8,128)(2,1)S(1)}, bf16[128,4096]{1,0:T(8,128)(2,1)S(1)}, bf16[128,4096]{1,0:T(8,128)(2,1)S(1)}, bf16[128,4096]{1,0:T(8,128)(2,...) custom-call(s32[2,8]{1,0:T(2,128)S(1)} %pad_add_fusion.place_ref, ...), custom_call_target="tpu_custom_call" | custom-call | flops 34359738368 | bytes 33554432 | tf_op jit(solution)/shard_map/attend/pallas_call | solution.py:88
  1174.0 1.6 collective-permute-start.45
  1175.6 2.5 collective-permute-start.47
  1178.1 63.9 %attend.5 = (bf16[128,4096]{1,0:T(8,128)(2,1)S(1)}, bf16[128,4096]{1,0:T(8,128)(2,1)S(1)}, bf16[128,4096]{1,0:T(8,128)(2,1)S(1)}, bf16[128,4096]{1,0:T(8,128)(2,...) custom-call(s32[2,8]{1,0:T(2,128)S(1)} %pad_add_fusion.place_ref, ...), custom_call_target="tpu_custom_call" | custom-call | flops 34359738368 | bytes 33554432 | tf_op jit(solution)/shard_map/attend/pallas_call | solution.py:88
  1243.7 22.8 collective-permute-done.46.refs_4_
  1267.5 42.5 %collective-permute-done.47.refs_5_ = bf16[128,8192]{1,0:T(8,128)(2,1)} collective-permute-done((bf16[128,8192]{1,0:T(8,128)(2,1)S(1)}, bf16[128,8192]{1,0:T(8,128)(2,1)}, u32[]{:S(2)}, u32[]{:S(2)}) %collective-permute-start.47) | collective-permute-done | bytes 2097184 | tf_op jit(solution)/shard_map/ppermute | solution.py:233
  1310.0 1.4 collective-permute-start.28
  1311.4 1.5 collective-permute-start.29
  1312.9 63.7 %attend.6 = (bf16[128,4096]{1,0:T(8,128)(2,1)S(1)}, bf16[128,4096]{1,0:T(8,128)(2,1)}, bf16[128,4096]{1,0:T(8,128)(2,1)S(1)}, bf16[128,4096]{1,0:T(8,128)(2,1)},...) custom-call(s32[2,8]{1,0:T(2,128)S(1)} %pad_add_fusion.place_ref, ...), custom_call_target="tpu_custom_call" | custom-call | flops 34359738368 | bytes 33554432 | tf_op jit(solution)/shard_map/attend/pallas_call | solution.py:88
  1378.6 1.8 collective-permute-start.30
  1380.5 1.3 collective-permute-start.38
  1382.7 1.2 collective-permute-start.4
  1384.7 168.8 %project.9.refs_1_.refs_3_.refs_5_ = bf16[768,12288]{1,0:T(8,128)(2,1)} custom-call(s32[1]{0:T(128)} %bitcast.cp_ref, bf16[128,8192]{1,0:T(8,128)(2,1)} %collective-permute-done.42.refs_0_, bf16[128,8192]{1,0:T(8,128)(2,1)} %collective-permute-done.43.refs_1_, bf16[128,8192]{1,0:T(8,128)(2,1)} %collective-permute-done.44.refs_2_, ...), custom_call_target="tpu_custom_call" | custom-call | flops 154618822656 | bytes 232783872 | tf_op jit(solution)/shard_map/project/pallas_call | solution.py:151
  1554.4 1.8 collective-permute-start.40
  1556.8 64.2 %attend.7 = (bf16[128,4096]{1,0:T(8,128)(2,1)S(1)}, bf16[128,4096]{1,0:T(8,128)(2,1)S(1)}, bf16[128,4096]{1,0:T(8,128)(2,1)S(1)}, bf16[128,4096]{1,0:T(8,128)(2,...) custom-call(s32[2,8]{1,0:T(2,128)S(1)} %pad_add_fusion.place_ref, ...), custom_call_target="tpu_custom_call" | custom-call | flops 34359738368 | bytes 33554432 | tf_op jit(solution)/shard_map/attend/pallas_call | solution.py:88
  1622.0 1.3 collective-permute-start.48
  1623.3 186.9 %collective-permute-done.40.refs_14_ = bf16[128,4096]{1,0:T(8,128)(2,1)S(1)} collective-permute-done((bf16[128,4096]{1,0:T(8,128)(2,1)}, bf16[128,4096]{1,0:T(8,128)(2,1)S(1)}, u32[]{:S(2)}, u32[]{:S(2)}) %collective-permute-start.40) | collective-permute-done | bytes 1048608 | tf_op jit(solution)/shard_map/ppermute | solution.py:233
  1810.3 19.7 collective-permute-done.41.refs_15_
  1830.0 2.0 collective-permute-start.50
  1832.9 43.2 %collective-permute-done.49.refs_17_ = bf16[128,4096]{1,0:T(8,128)(2,1)S(1)} collective-permute-done((bf16[128,4096]{1,0:T(8,128)(2,1)S(1)}, bf16[128,4096]{1,0:T(8,128)(2,1)S(1)}, u32[]{:S(2)}, u32[]{:S(2)}) %collective-permute-start.49) | collective-permute-done | bytes 1048608 | tf_op jit(solution)/shard_map/ppermute | solution.py:233
  1876.1 1.5 collective-permute-start.53
  1878.3 23.8 %collective-permute-done.53.refs_3_ = bf16[128,4096]{1,0:T(8,128)(2,1)S(1)} collective-permute-done((bf16[128,4096]{1,0:T(8,128)(2,1)S(1)}, bf16[128,4096]{1,0:T(8,128)(2,1)S(1)}, u32[]{:S(2)}, u32[]{:S(2)}) %collective-permute-start.53) | collective-permute-done | bytes 1048608 | tf_op jit(solution)/shard_map/ppermute | solution.py:233
  1902.1 1.5 collective-permute-start.56
  1903.7 20.0 collective-permute-done.54.refs_4_
  1923.6 1.9 collective-permute-start.57
  1925.6 21.5 collective-permute-done.56.refs_7_
  1947.1 1.5 collective-permute-start.59
  1948.6 20.1 collective-permute-done.57.refs_8_
  1968.7 1.8 collective-permute-start.60
  1971.1 20.9 collective-permute-done.59.refs_11_
  1992.0 21.6 collective-permute-done.60.refs_12_
  2015.4 118.1 %out_project.3.refs_20_ = f32[1536,8192]{1,0:T(8,128)} custom-call(s32[1]{0:T(128)} %bitcast.cp_ref, bf16[4096,8192]{1,0:T(8,128)(2,1)} %refs_0_.5, bf16[128,4096]{1,0:T(8,128)(2,1)S(1)} %get-tuple-element.59.refs_1_, bf16[128,4096]{1,0:T(8,128)(2,1)} %copy-done.35, bf16[128,4096]{1,0:T(8,128)(2,1)} %copy-done.36, bf16[128,4096]{1,0:T(8,128)(2,1)} %copy-done.37, ...), custom_call_target="tpu_custom_call" | custom-call | flops 103079215104 | bytes 130023424 | tf_op jit(solution)/shard_map/out_project/pallas_call | solution.py:210
  2133.6 1.3 collective-permute-start.17
  2134.9 1.3 collective-permute-start.18
  2137.8 1.8 collective-permute-start.21
  2139.6 118.3 %out_project.4.refs_18_ = bf16[2048,8192]{1,0:T(8,128)(2,1)} custom-call(s32[1]{0:T(128)} %bitcast.cp_ref, bf16[512,8192]{1,0:T(8,128)(2,1)} %collective-permute-done.refs_0_.refs_1_, bf16[512,8192]{1,0:T(8,128)(2,1)} %collective-permute-done.1.refs_1_.refs_2_, bf16[512,8192]{1,0:T(8,128)(2,1)} %collective-permute-done.2.refs_2_.refs_3_, ...), custom_call_target="tpu_custom_call" | custom-call | flops 103079215104 | bytes 130023424 | tf_op jit(solution)/shard_map/out_project/pallas_call | solution.py:210
  2259.9 82.0 %out_project.5 = bf16[2048,8192]{1,0:T(8,128)(2,1)} custom-call(s32[1]{0:T(128)} %bitcast.cp_ref, bf16[4096,8192]{1,0:T(8,128)(2,1)} %refs_0_.5, bf16[512,8192]{1,0:T(8,128)(2,1)} %collective-permute-done.refs_0_.refs_1_, bf16[512,8192]{1,0:T(8,128)(2,1)} %collective-permute-done.1.refs_1_.refs_2_, ...), custom_call_target="tpu_custom_call", output_to_operand_aliasing={{}: (19, {})} | custom-call | flops 68719476736 | bytes 159383552 | tf_op jit(solution)/shard_map/out_project/pallas_call | solution.py:210
  (185 shorter events, 22.9 us)
Async XLA Ops:
  22.7 159.3 %collective-permute-start.11 = (bf16[128,8192]{1,0:T(8,128)(2,1)}, bf16[128,8192]{1,0:T(8,128)(2,1)}, u32[]{:S(2)}, u32[]{:S(2)}) collective-permute-start(bf16[128,8192]{1,0:T(8,128)(2,1)} %get-tuple-element.82), channel_id=1, source_target_pairs={{0,2},{1,3},{2,0},{3,1},{4,6},{5,7},{6,4},{7,5}} | collective-permute-start | bytes 6291464 | tf_op jit(solution)/shard_map/ppermute | solution.py:233
  26.0 174.6 %collective-permute-start.12 = (bf16[128,8192]{1,0:T(8,128)(2,1)}, bf16[128,8192]{1,0:T(8,128)(2,1)}, u32[]{:S(2)}, u32[]{:S(2)}) collective-permute-start(bf16[128,8192]{1,0:T(8,128)(2,1)} %get-tuple-element.82), channel_id=1, source_target_pairs={{0,6},{1,7},{2,4},{3,5},{4,2},{5,3},{6,0},{7,1}} | collective-permute-start | bytes 6291464 | tf_op jit(solution)/shard_map/ppermute | solution.py:233
  27.5 152.8 %collective-permute-start.9 = (bf16[128,8192]{1,0:T(8,128)(2,1)}, bf16[128,8192]{1,0:T(8,128)(2,1)}, u32[]{:S(2)}, u32[]{:S(2)}) collective-permute-start(bf16[128,8192]{1,0:T(8,128)(2,1)} %get-tuple-element.83), channel_id=1, source_target_pairs={{0,4},{1,5},{2,6},{3,7},{4,0},{5,1},{6,2},{7,3}} | collective-permute-start | bytes 6291464 | tf_op jit(solution)/shard_map/ppermute | solution.py:233
  27.5 152.9 %collective-permute-start.10 = (bf16[128,8192]{1,0:T(8,128)(2,1)}, bf16[128,8192]{1,0:T(8,128)(2,1)}, u32[]{:S(2)}, u32[]{:S(2)}) collective-permute-start(bf16[128,8192]{1,0:T(8,128)(2,1)} %bitcast.3), channel_id=1, source_target_pairs={{0,5},{1,4},{2,7},{3,6},{4,1},{5,0},{6,3},{7,2}} | collective-permute-start | bytes 6291464 | tf_op jit(solution)/shard_map/ppermute | solution.py:233
  28.1 174.0 %collective-permute-start.13 = (bf16[128,8192]{1,0:T(8,128)(2,1)}, bf16[128,8192]{1,0:T(8,128)(2,1)}, u32[]{:S(2)}, u32[]{:S(2)}) collective-permute-start(bf16[128,8192]{1,0:T(8,128)(2,1)} %get-tuple-element.81), channel_id=1, source_target_pairs={{0,3},{1,2},{2,1},{3,0},{4,7},{5,6},{6,5},{7,4}} | collective-permute-start | bytes 6291464 | tf_op jit(solution)/shard_map/ppermute | solution.py:233
  180.3 49.1 %collective-permute-start.14 = (bf16[128,8192]{1,0:T(8,128)(2,1)}, bf16[128,8192]{1,0:T(8,128)(2,1)S(1)}, u32[]{:S(2)}, u32[]{:S(2)}) collective-permute-start(bf16[128,8192]{1,0:T(8,128)(2,1)} %get-tuple-element.81), channel_id=1, source_target_pairs={{0,7},{1,6},{2,5},{3,4},{4,3},{5,2},{6,1},{7,0}} | collective-permute-start | bytes 6291464 | tf_op jit(solution)/shard_map/ppermute | solution.py:233
  180.5 93.7 %collective-permute-start.22 = (bf16[128,8192]{1,0:T(8,128)(2,1)S(1)}, bf16[128,8192]{1,0:T(8,128)(2,1)S(1)}, u32[]{:S(2)}, u32[]{:S(2)}) collective-permute-start(bf16[128,8192]{1,0:T(8,128)(2,1)S(1)} %copy-done.15), channel_id=1, source_target_pairs={{0,4},{1,5},{2,6},{3,7},{4,0},{5,1},{6,2},{7,3}} | collective-permute-start | bytes 6291464 | tf_op jit(solution)/shard_map/ppermute | solution.py:233
  182.0 182.1 %collective-permute-start.23 = (bf16[128,8192]{1,0:T(8,128)(2,1)S(1)}, bf16[128,8192]{1,0:T(8,128)(2,1)S(1)}, u32[]{:S(2)}, u32[]{:S(2)}) collective-permute-start(bf16[128,8192]{1,0:T(8,128)(2,1)S(1)} %bitcast.43), channel_id=1, source_target_pairs={{0,5},{1,4},{2,7},{3,6},{4,1},{5,0},{6,3},{7,2}} | collective-permute-start | bytes 6291464 | tf_op jit(solution)/shard_map/ppermute | solution.py:233
  200.6 334.7 %collective-permute-start.24 = (bf16[128,8192]{1,0:T(8,128)(2,1)}, bf16[128,8192]{1,0:T(8,128)(2,1)}, u32[]{:S(2)}, u32[]{:S(2)}) collective-permute-start(bf16[128,8192]{1,0:T(8,128)(2,1)} %get-tuple-element.79), channel_id=1, source_target_pairs={{0,2},{1,3},{2,0},{3,1},{4,6},{5,7},{6,4},{7,5}} | collective-permute-start | bytes 6291464 | tf_op jit(solution)/shard_map/ppermute | solution.py:233
  202.1 333.9 %collective-permute-start.25 = (bf16[128,8192]{1,0:T(8,128)(2,1)}, bf16[128,8192]{1,0:T(8,128)(2,1)}, u32[]{:S(2)}, u32[]{:S(2)}) collective-permute-start(bf16[128,8192]{1,0:T(8,128)(2,1)} %get-tuple-element.79), channel_id=1, source_target_pairs={{0,6},{1,7},{2,4},{3,5},{4,2},{5,3},{6,0},{7,1}} | collective-permute-start | bytes 6291464 | tf_op jit(solution)/shard_map/ppermute | solution.py:233
  229.4 308.0 %collective-permute-start.26 = (bf16[128,8192]{1,0:T(8,128)(2,1)}, bf16[128,8192]{1,0:T(8,128)(2,1)}, u32[]{:S(2)}, u32[]{:S(2)}) collective-permute-start(bf16[128,8192]{1,0:T(8,128)(2,1)} %get-tuple-element.78), channel_id=1, source_target_pairs={{0,3},{1,2},{2,1},{3,0},{4,7},{5,6},{6,5},{7,4}} | collective-permute-start | bytes 6291464 | tf_op jit(solution)/shard_map/ppermute | solution.py:233
  274.2 263.2 %collective-permute-start.27 = (bf16[128,8192]{1,0:T(8,128)(2,1)}, bf16[128,8192]{1,0:T(8,128)(2,1)}, u32[]{:S(2)}, u32[]{:S(2)}) collective-permute-start(bf16[128,8192]{1,0:T(8,128)(2,1)} %get-tuple-element.78), channel_id=1, source_target_pairs={{0,7},{1,6},{2,5},{3,4},{4,3},{5,2},{6,1},{7,0}} | collective-permute-start | bytes 6291464 | tf_op jit(solution)/shard_map/ppermute | solution.py:233
  365.4 174.6 %collective-permute-start.32 = (bf16[128,8192]{1,0:T(8,128)(2,1)}, bf16[128,8192]{1,0:T(8,128)(2,1)}, u32[]{:S(2)}, u32[]{:S(2)}) collective-permute-start(bf16[128,8192]{1,0:T(8,128)(2,1)} %get-tuple-element.77), channel_id=1, source_target_pairs={{0,4},{1,5},{2,6},{3,7},{4,0},{5,1},{6,2},{7,3}} | collective-permute-start | bytes 6291464 | tf_op jit(solution)/shard_map/ppermute | solution.py:233
  535.3 174.3 %collective-permute-start.34 = (bf16[128,8192]{1,0:T(8,128)(2,1)}, bf16[128,8192]{1,0:T(8,128)(2,1)}, u32[]{:S(2)}, u32[]{:S(2)}) collective-permute-start(bf16[128,8192]{1,0:T(8,128)(2,1)} %get-tuple-element.76), channel_id=1, source_target_pairs={{0,2},{1,3},{2,0},{3,1},{4,6},{5,7},{6,4},{7,5}} | collective-permute-start | bytes 6291464 | tf_op jit(solution)/shard_map/ppermute | solution.py:233
  536.0 174.7 %collective-permute-start.35 = (bf16[128,8192]{1,0:T(8,128)(2,1)}, bf16[128,8192]{1,0:T(8,128)(2,1)}, u32[]{:S(2)}, u32[]{:S(2)}) collective-permute-start(bf16[128,8192]{1,0:T(8,128)(2,1)} %get-tuple-element.76), channel_id=1, source_target_pairs={{0,6},{1,7},{2,4},{3,5},{4,2},{5,3},{6,0},{7,1}} | collective-permute-start | bytes 6291464 | tf_op jit(solution)/shard_map/ppermute | solution.py:233
  537.4 173.4 %collective-permute-start.36 = (bf16[128,8192]{1,0:T(8,128)(2,1)}, bf16[128,8192]{1,0:T(8,128)(2,1)}, u32[]{:S(2)}, u32[]{:S(2)}) collective-permute-start(bf16[128,8192]{1,0:T(8,128)(2,1)} %get-tuple-element.75), channel_id=1, source_target_pairs={{0,3},{1,2},{2,1},{3,0},{4,7},{5,6},{6,5},{7,4}} | collective-permute-start | bytes 6291464 | tf_op jit(solution)/shard_map/ppermute | solution.py:233
  537.4 179.5 %collective-permute-start.37 = (bf16[128,8192]{1,0:T(8,128)(2,1)}, bf16[128,8192]{1,0:T(8,128)(2,1)}, u32[]{:S(2)}, u32[]{:S(2)}) collective-permute-start(bf16[128,8192]{1,0:T(8,128)(2,1)} %get-tuple-element.75), channel_id=1, source_target_pairs={{0,7},{1,6},{2,5},{3,4},{4,3},{5,2},{6,1},{7,0}} | collective-permute-start | bytes 6291464 | tf_op jit(solution)/shard_map/ppermute | solution.py:233
  540.0 168.6 %collective-permute-start.33 = (bf16[128,8192]{1,0:T(8,128)(2,1)}, bf16[128,8192]{1,0:T(8,128)(2,1)}, u32[]{:S(2)}, u32[]{:S(2)}) collective-permute-start(bf16[128,8192]{1,0:T(8,128)(2,1)} %bitcast.42), channel_id=1, source_target_pairs={{0,5},{1,4},{2,7},{3,6},{4,1},{5,0},{6,3},{7,2}} | collective-permute-start | bytes 6291464 | tf_op jit(solution)/shard_map/ppermute | solution.py:233
  708.6 602.8 %collective-permute-start = (bf16[512,8192]{1,0:T(8,128)(2,1)}, bf16[512,8192]{1,0:T(8,128)(2,1)}, u32[]{:S(2)}, u32[]{:S(2)}) collective-permute-start(bf16[512,8192]{1,0:T(8,128)(2,1)} %get-tuple-element.72), channel_id=1, source_target_pairs={{0,4},{1,5},{2,6},{3,7},{4,0},{5,1},{6,2},{7,3}} | collective-permute-start | bytes 25165832 | tf_op jit(solution)/shard_map/ppermute | solution.py:233
  709.5 669.1 %collective-permute-start.1 = (bf16[512,8192]{1,0:T(8,128)(2,1)}, bf16[512,8192]{1,0:T(8,128)(2,1)}, u32[]{:S(2)}, u32[]{:S(2)}) collective-permute-start(bf16[512,8192]{1,0:T(8,128)(2,1)} %get-tuple-element.71), channel_id=1, source_target_pairs={{0,4},{1,5},{2,6},{3,7},{4,0},{5,1},{6,2},{7,3}} | collective-permute-start | bytes 25165832 | tf_op jit(solution)/shard_map/ppermute | solution.py:233
  710.7 176.6 %collective-permute-start.8 = (bf16[4,128,8192]{2,1,0:T(8,128)(2,1)}, bf16[4,128,8192]{2,1,0:T(8,128)(2,1)}, u32[]{:S(2)}, u32[]{:S(2)}) collective-permute-start(bf16[4,128,8192]{2,1,0:T(8,128)(2,1)} %pad_maximum_fusion), channel_id=1, source_target_pairs={{0,1},{1,0},{2,3},{3,2},{4,5},{5,4},{6,7},{7,6}} | collective-permute-start | bytes 25165832 | tf_op jit(solution)/shard_map/ppermute | solution.py:233
  710.9 463.1 %collective-permute-start.42 = (bf16[128,8192]{1,0:T(8,128)(2,1)}, bf16[128,8192]{1,0:T(8,128)(2,1)}, u32[]{:S(2)}, u32[]{:S(2)}) collective-permute-start(bf16[128,8192]{1,0:T(8,128)(2,1)} %get-tuple-element.74), channel_id=1, source_target_pairs={{0,4},{1,5},{2,6},{3,7},{4,0},{5,1},{6,2},{7,3}} | collective-permute-start | bytes 6291464 | tf_op jit(solution)/shard_map/ppermute | solution.py:233
  716.9 458.6 %collective-permute-start.43 = (bf16[128,8192]{1,0:T(8,128)(2,1)}, bf16[128,8192]{1,0:T(8,128)(2,1)}, u32[]{:S(2)}, u32[]{:S(2)}) collective-permute-start(bf16[128,8192]{1,0:T(8,128)(2,1)} %bitcast.41), channel_id=1, source_target_pairs={{0,5},{1,4},{2,7},{3,6},{4,1},{5,0},{6,3},{7,2}} | collective-permute-start | bytes 6291464 | tf_op jit(solution)/shard_map/ppermute | solution.py:233
  887.3 288.2 %collective-permute-start.44 = (bf16[128,8192]{1,0:T(8,128)(2,1)}, bf16[128,8192]{1,0:T(8,128)(2,1)}, u32[]{:S(2)}, u32[]{:S(2)}) collective-permute-start(bf16[128,8192]{1,0:T(8,128)(2,1)} %get-tuple-element.88), channel_id=1, source_target_pairs={{0,2},{1,3},{2,0},{3,1},{4,6},{5,7},{6,4},{7,5}} | collective-permute-start | bytes 6291464 | tf_op jit(solution)/shard_map/ppermute | solution.py:233
  1174.0 69.0 %collective-permute-start.45 = (bf16[128,8192]{1,0:T(8,128)(2,1)S(1)}, bf16[128,8192]{1,0:T(8,128)(2,1)}, u32[]{:S(2)}, u32[]{:S(2)}) collective-permute-start(bf16[128,8192]{1,0:T(8,128)(2,1)S(1)} %copy-done.14), channel_id=1, source_target_pairs={{0,6},{1,7},{2,4},{3,5},{4,2},{5,3},{6,0},{7,1}} | collective-permute-start | bytes 6291464 | tf_op jit(solution)/shard_map/ppermute | solution.py:233
  1175.6 91.0 %collective-permute-start.46 = (bf16[128,8192]{1,0:T(8,128)(2,1)S(1)}, bf16[128,8192]{1,0:T(8,128)(2,1)}, u32[]{:S(2)}, u32[]{:S(2)}) collective-permute-start(bf16[128,8192]{1,0:T(8,128)(2,1)S(1)} %copy-done.13), channel_id=1, source_target_pairs={{0,3},{1,2},{2,1},{3,0},{4,7},{5,6},{6,5},{7,4}} | collective-permute-start | bytes 6291464 | tf_op jit(solution)/shard_map/ppermute | solution.py:233
  1175.6 134.4 %collective-permute-start.47 = (bf16[128,8192]{1,0:T(8,128)(2,1)S(1)}, bf16[128,8192]{1,0:T(8,128)(2,1)}, u32[]{:S(2)}, u32[]{:S(2)}) collective-permute-start(bf16[128,8192]{1,0:T(8,128)(2,1)S(1)} %copy-done.13), channel_id=1, source_target_pairs={{0,7},{1,6},{2,5},{3,4},{4,3},{5,2},{6,1},{7,0}} | collective-permute-start | bytes 6291464 | tf_op jit(solution)/shard_map/ppermute | solution.py:233
  1243.0 137.4 %collective-permute-start.15 = (bf16[128,4096]{1,0:T(8,128)(2,1)S(1)}, bf16[128,4096]{1,0:T(8,128)(2,1)S(1)}, u32[]{:S(2)}, u32[]{:S(2)}) collective-permute-start(bf16[128,4096]{1,0:T(8,128)(2,1)S(1)} %get-tuple-element.40), channel_id=1, source_target_pairs={{0,4},{1,5},{2,6},{3,7},{4,0},{5,1},{6,2},{7,3}} | collective-permute-start | bytes 3145736 | tf_op jit(solution)/shard_map/ppermute | solution.py:233
  1266.5 113.9 %collective-permute-start.16 = (bf16[128,4096]{1,0:T(8,128)(2,1)S(1)}, bf16[128,4096]{1,0:T(8,128)(2,1)S(1)}, u32[]{:S(2)}, u32[]{:S(2)}) collective-permute-start(bf16[128,4096]{1,0:T(8,128)(2,1)S(1)} %get-tuple-element.41), channel_id=1, source_target_pairs={{0,1},{1,0},{2,3},{3,2},{4,5},{5,4},{6,7},{7,6}} | collective-permute-start | bytes 3145736 | tf_op jit(solution)/shard_map/ppermute | solution.py:233
  1310.0 71.7 %collective-permute-start.28 = (bf16[128,4096]{1,0:T(8,128)(2,1)S(1)}, bf16[128,4096]{1,0:T(8,128)(2,1)S(1)}, u32[]{:S(2)}, u32[]{:S(2)}) collective-permute-start(bf16[128,4096]{1,0:T(8,128)(2,1)S(1)} %get-tuple-element.47), channel_id=1, source_target_pairs={{0,4},{1,5},{2,6},{3,7},{4,0},{5,1},{6,2},{7,3}} | collective-permute-start | bytes 3145736 | tf_op jit(solution)/shard_map/ppermute | solution.py:233
  1311.4 72.4 %collective-permute-start.29 = (bf16[128,4096]{1,0:T(8,128)(2,1)S(1)}, bf16[128,4096]{1,0:T(8,128)(2,1)}, u32[]{:S(2)}, u32[]{:S(2)}) collective-permute-start(bf16[128,4096]{1,0:T(8,128)(2,1)S(1)} %get-tuple-element.48), channel_id=1, source_target_pairs={{0,5},{1,4},{2,7},{3,6},{4,1},{5,0},{6,3},{7,2}} | collective-permute-start | bytes 3145736 | tf_op jit(solution)/shard_map/ppermute | solution.py:233
  1378.6 175.0 %collective-permute-start.30 = (bf16[128,4096]{1,0:T(8,128)(2,1)}, bf16[128,4096]{1,0:T(8,128)(2,1)}, u32[]{:S(2)}, u32[]{:S(2)}) collective-permute-start(bf16[128,4096]{1,0:T(8,128)(2,1)} %get-tuple-element.49), channel_id=1, source_target_pairs={{0,6},{1,7},{2,4},{3,5},{4,2},{5,3},{6,0},{7,1}} | collective-permute-start | bytes 3145736 | tf_op jit(solution)/shard_map/ppermute | solution.py:233
  1380.5 173.9 %collective-permute-start.31 = (bf16[128,4096]{1,0:T(8,128)(2,1)}, bf16[128,4096]{1,0:T(8,128)(2,1)}, u32[]{:S(2)}, u32[]{:S(2)}) collective-permute-start(bf16[128,4096]{1,0:T(8,128)(2,1)} %get-tuple-element.50), channel_id=1, source_target_pairs={{0,7},{1,6},{2,5},{3,4},{4,3},{5,2},{6,1},{7,0}} | collective-permute-start | bytes 3145736 | tf_op jit(solution)/shard_map/ppermute | solution.py:233
  1380.5 175.7 %collective-permute-start.38 = (bf16[128,4096]{1,0:T(8,128)(2,1)}, bf16[128,4096]{1,0:T(8,128)(2,1)}, u32[]{:S(2)}, u32[]{:S(2)}) collective-permute-start(bf16[128,4096]{1,0:T(8,128)(2,1)} %get-tuple-element.51), channel_id=1, source_target_pairs={{0,4},{1,5},{2,6},{3,7},{4,0},{5,1},{6,2},{7,3}} | collective-permute-start | bytes 3145736 | tf_op jit(solution)/shard_map/ppermute | solution.py:233
  1382.7 632.0 %collective-permute-start.4 = (bf16[512,8192]{1,0:T(8,128)(2,1)}, bf16[512,8192]{1,0:T(8,128)(2,1)}, u32[]{:S(2)}, u32[]{:S(2)}) collective-permute-start(bf16[512,8192]{1,0:T(8,128)(2,1)} %collective-permute-done.refs_0_.refs_1_), channel_id=1, source_target_pairs={{0,2},{1,3},{2,0},{3,1},{4,6},{5,7},{6,4},{7,5}} | collective-permute-start | bytes 25165832 | tf_op jit(solution)/shard_map/ppermute | solution.py:233
  1383.9 630.9 %collective-permute-start.5 = (bf16[512,8192]{1,0:T(8,128)(2,1)}, bf16[512,8192]{1,0:T(8,128)(2,1)}, u32[]{:S(2)}, u32[]{:S(2)}) collective-permute-start(bf16[512,8192]{1,0:T(8,128)(2,1)} %collective-permute-done.1.refs_1_.refs_2_), channel_id=1, source_target_pairs={{0,2},{1,3},{2,0},{3,1},{4,6},{5,7},{6,4},{7,5}} | collective-permute-start | bytes 25165832 | tf_op jit(solution)/shard_map/ppermute | solution.py:233
  1553.6 68.4 %collective-permute-start.39 = (bf16[128,4096]{1,0:T(8,128)(2,1)}, bf16[128,4096]{1,0:T(8,128)(2,1)S(1)}, u32[]{:S(2)}, u32[]{:S(2)}) collective-permute-start(bf16[128,4096]{1,0:T(8,128)(2,1)} %get-tuple-element.52), channel_id=1, source_target_pairs={{0,5},{1,4},{2,7},{3,6},{4,1},{5,0},{6,3},{7,2}} | collective-permute-start | bytes 3145736 | tf_op jit(solution)/shard_map/ppermute | solution.py:233
  1554.4 255.9 %collective-permute-start.40 = (bf16[128,4096]{1,0:T(8,128)(2,1)}, bf16[128,4096]{1,0:T(8,128)(2,1)S(1)}, u32[]{:S(2)}, u32[]{:S(2)}) collective-permute-start(bf16[128,4096]{1,0:T(8,128)(2,1)} %get-tuple-element.53), channel_id=1, source_target_pairs={{0,6},{1,7},{2,4},{3,5},{4,2},{5,3},{6,0},{7,1}} | collective-permute-start | bytes 3145736 | tf_op jit(solution)/shard_map/ppermute | solution.py:233
  1556.2 273.8 %collective-permute-start.41 = (bf16[128,4096]{1,0:T(8,128)(2,1)}, bf16[128,4096]{1,0:T(8,128)(2,1)S(1)}, u32[]{:S(2)}, u32[]{:S(2)}) collective-permute-start(bf16[128,4096]{1,0:T(8,128)(2,1)} %get-tuple-element.54), channel_id=1, source_target_pairs={{0,7},{1,6},{2,5},{3,4},{4,3},{5,2},{6,1},{7,0}} | collective-permute-start | bytes 3145736 | tf_op jit(solution)/shard_map/ppermute | solution.py:233
  1556.8 320.9 %copy-start.8 = (bf16[128,4096]{1,0:T(8,128)(2,1)S(1)}, bf16[128,4096]{1,0:T(8,128)(2,1)}, u32[]{:S(2)}) copy-start(bf16[128,4096]{1,0:T(8,128)(2,1)} %copy-done.7) | copy-start | bytes 3145732
  1622.0 511.5 %copy-start.27 = (bf16[128,4096]{1,0:T(8,128)(2,1)}, bf16[128,4096]{1,0:T(8,128)(2,1)S(1)}, u32[]{:S(2)}) copy-start(bf16[128,4096]{1,0:T(8,128)(2,1)S(1)} %collective-permute-done.39.refs_13_) | copy-start | bytes 3145732
  1622.0 210.0 %collective-permute-start.48 = (bf16[128,4096]{1,0:T(8,128)(2,1)S(1)}, bf16[128,4096]{1,0:T(8,128)(2,1)S(1)}, u32[]{:S(2)}, u32[]{:S(2)}) collective-permute-start(bf16[128,4096]{1,0:T(8,128)(2,1)S(1)} %get-tuple-element.55), channel_id=1, source_target_pairs={{0,4},{1,5},{2,6},{3,7},{4,0},{5,1},{6,2},{7,3}} | collective-permute-start | bytes 3145736 | tf_op jit(solution)/shard_map/ppermute | solution.py:233
  1810.3 323.3 %copy-start.28 = (bf16[128,4096]{1,0:T(8,128)(2,1)}, bf16[128,4096]{1,0:T(8,128)(2,1)S(1)}, u32[]{:S(2)}) copy-start(bf16[128,4096]{1,0:T(8,128)(2,1)S(1)} %collective-permute-done.40.refs_14_) | copy-start | bytes 3145732
  1810.3 65.8 %collective-permute-start.49 = (bf16[128,4096]{1,0:T(8,128)(2,1)S(1)}, bf16[128,4096]{1,0:T(8,128)(2,1)S(1)}, u32[]{:S(2)}, u32[]{:S(2)}) collective-permute-start(bf16[128,4096]{1,0:T(8,128)(2,1)S(1)} %get-tuple-element.56), channel_id=1, source_target_pairs={{0,5},{1,4},{2,7},{3,6},{4,1},{5,0},{6,3},{7,2}} | collective-permute-start | bytes 3145736 | tf_op jit(solution)/shard_map/ppermute | solution.py:233
  1830.0 47.6 %collective-permute-start.50 = (bf16[128,4096]{1,0:T(8,128)(2,1)}, bf16[128,4096]{1,0:T(8,128)(2,1)S(1)}, u32[]{:S(2)}, u32[]{:S(2)}) collective-permute-start(bf16[128,4096]{1,0:T(8,128)(2,1)} %get-tuple-element.57), channel_id=1, source_target_pairs={{0,6},{1,7},{2,4},{3,5},{4,2},{5,3},{6,0},{7,1}} | collective-permute-start | bytes 3145736 | tf_op jit(solution)/shard_map/ppermute | solution.py:233
  1832.0 45.7 %collective-permute-start.52 = (bf16[128,4096]{1,0:T(8,128)(2,1)S(1)}, bf16[128,4096]{1,0:T(8,128)(2,1)S(1)}, u32[]{:S(2)}, u32[]{:S(2)}) collective-permute-start(bf16[128,4096]{1,0:T(8,128)(2,1)S(1)} %copy-done.6), channel_id=1, source_target_pairs={{0,1},{1,0},{2,3},{3,2},{4,5},{5,4},{6,7},{7,6}} | collective-permute-start | bytes 3145736 | tf_op jit(solution)/shard_map/ppermute | solution.py:233
  1876.1 26.0 %collective-permute-start.53 = (bf16[128,4096]{1,0:T(8,128)(2,1)S(1)}, bf16[128,4096]{1,0:T(8,128)(2,1)S(1)}, u32[]{:S(2)}, u32[]{:S(2)}) collective-permute-start(bf16[128,4096]{1,0:T(8,128)(2,1)S(1)} %copy-done.31), channel_id=1, source_target_pairs={{0,2},{1,3},{2,0},{3,1},{4,6},{5,7},{6,4},{7,5}} | collective-permute-start | bytes 3145736 | tf_op jit(solution)/shard_map/ppermute | solution.py:233
  1877.6 46.0 %collective-permute-start.54 = (bf16[128,4096]{1,0:T(8,128)(2,1)S(1)}, bf16[128,4096]{1,0:T(8,128)(2,1)S(1)}, u32[]{:S(2)}, u32[]{:S(2)}) collective-permute-start(bf16[128,4096]{1,0:T(8,128)(2,1)S(1)} %copy-done.30), channel_id=1, source_target_pairs={{0,3},{1,2},{2,1},{3,0},{4,7},{5,6},{6,5},{7,4}} | collective-permute-start | bytes 3145736 | tf_op jit(solution)/shard_map/ppermute | solution.py:233
  1877.7 47.9 %collective-permute-start.55 = (bf16[128,4096]{1,0:T(8,128)(2,1)S(1)}, bf16[128,4096]{1,0:T(8,128)(2,1)S(1)}, u32[]{:S(2)}, u32[]{:S(2)}) collective-permute-start(bf16[128,4096]{1,0:T(8,128)(2,1)S(1)} %copy-done.8), channel_id=1, source_target_pairs={{0,1},{1,0},{2,3},{3,2},{4,5},{5,4},{6,7},{7,6}} | collective-permute-start | bytes 3145736 | tf_op jit(solution)/shard_map/ppermute | solution.py:233
  1902.1 44.9 %collective-permute-start.56 = (bf16[128,4096]{1,0:T(8,128)(2,1)}, bf16[128,4096]{1,0:T(8,128)(2,1)S(1)}, u32[]{:S(2)}, u32[]{:S(2)}) collective-permute-start(bf16[128,4096]{1,0:T(8,128)(2,1)} %get-tuple-element.65), channel_id=1, source_target_pairs={{0,2},{1,3},{2,0},{3,1},{4,6},{5,7},{6,4},{7,5}} | collective-permute-start | bytes 3145736 | tf_op jit(solution)/shard_map/ppermute | solution.py:233
  1923.6 45.0 %collective-permute-start.57 = (bf16[128,4096]{1,0:T(8,128)(2,1)}, bf16[128,4096]{1,0:T(8,128)(2,1)S(1)}, u32[]{:S(2)}, u32[]{:S(2)}) collective-permute-start(bf16[128,4096]{1,0:T(8,128)(2,1)} %get-tuple-element.66), channel_id=1, source_target_pairs={{0,3},{1,2},{2,1},{3,0},{4,7},{5,6},{6,5},{7,4}} | collective-permute-start | bytes 3145736 | tf_op jit(solution)/shard_map/ppermute | solution.py:233
  1925.6 44.9 %collective-permute-start.58 = (bf16[128,4096]{1,0:T(8,128)(2,1)S(1)}, bf16[128,4096]{1,0:T(8,128)(2,1)S(1)}, u32[]{:S(2)}, u32[]{:S(2)}) collective-permute-start(bf16[128,4096]{1,0:T(8,128)(2,1)S(1)} %get-tuple-element.68), channel_id=1, source_target_pairs={{0,1},{1,0},{2,3},{3,2},{4,5},{5,4},{6,7},{7,6}} | collective-permute-start | bytes 3145736 | tf_op jit(solution)/shard_map/ppermute | solution.py:233
  1947.1 44.9 %collective-permute-start.59 = (bf16[128,4096]{1,0:T(8,128)(2,1)}, bf16[128,4096]{1,0:T(8,128)(2,1)S(1)}, u32[]{:S(2)}, u32[]{:S(2)}) collective-permute-start(bf16[128,4096]{1,0:T(8,128)(2,1)} %get-tuple-element.69), channel_id=1, source_target_pairs={{0,2},{1,3},{2,0},{3,1},{4,6},{5,7},{6,4},{7,5}} | collective-permute-start | bytes 3145736 | tf_op jit(solution)/shard_map/ppermute | solution.py:233
  1968.7 44.9 %collective-permute-start.60 = (bf16[128,4096]{1,0:T(8,128)(2,1)}, bf16[128,4096]{1,0:T(8,128)(2,1)S(1)}, u32[]{:S(2)}, u32[]{:S(2)}) collective-permute-start(bf16[128,4096]{1,0:T(8,128)(2,1)} %get-tuple-element.70), channel_id=1, source_target_pairs={{0,3},{1,2},{2,1},{3,0},{4,7},{5,6},{6,5},{7,4}} | collective-permute-start | bytes 3145736 | tf_op jit(solution)/shard_map/ppermute | solution.py:233
  1970.5 163.1 %collective-permute-start.51 = (bf16[128,4096]{1,0:T(8,128)(2,1)}, bf16[128,4096]{1,0:T(8,128)(2,1)}, u32[]{:S(2)}, u32[]{:S(2)}) collective-permute-start(bf16[128,4096]{1,0:T(8,128)(2,1)} %get-tuple-element.58), channel_id=1, source_target_pairs={{0,7},{1,6},{2,5},{3,4},{4,3},{5,2},{6,1},{7,0}} | collective-permute-start | bytes 3145736 | tf_op jit(solution)/shard_map/ppermute | solution.py:233
  1992.0 142.9 %collective-permute-start.2 = (bf16[512,8192]{1,0:T(8,128)(2,1)}, bf16[512,8192]{1,0:T(8,128)(2,1)}, u32[]{:S(2)}, u32[]{:S(2)}) collective-permute-start(bf16[512,8192]{1,0:T(8,128)(2,1)} %collective-permute-done.refs_0_.refs_1_), channel_id=1, source_target_pairs={{0,1},{1,0},{2,3},{3,2},{4,5},{5,4},{6,7},{7,6}} | collective-permute-start | bytes 25165832 | tf_op jit(solution)/shard_map/ppermute | solution.py:233
  2013.6 122.6 %collective-permute-start.3 = (bf16[512,8192]{1,0:T(8,128)(2,1)}, bf16[512,8192]{1,0:T(8,128)(2,1)}, u32[]{:S(2)}, u32[]{:S(2)}) collective-permute-start(bf16[512,8192]{1,0:T(8,128)(2,1)} %collective-permute-done.1.refs_1_.refs_2_), channel_id=1, source_target_pairs={{0,1},{1,0},{2,3},{3,2},{4,5},{5,4},{6,7},{7,6}} | collective-permute-start | bytes 25165832 | tf_op jit(solution)/shard_map/ppermute | solution.py:233
  2014.7 122.4 %collective-permute-start.6 = (bf16[512,8192]{1,0:T(8,128)(2,1)}, bf16[512,8192]{1,0:T(8,128)(2,1)}, u32[]{:S(2)}, u32[]{:S(2)}) collective-permute-start(bf16[512,8192]{1,0:T(8,128)(2,1)} %collective-permute-done.4.refs_4_.refs_5_), channel_id=1, source_target_pairs={{0,1},{1,0},{2,3},{3,2},{4,5},{5,4},{6,7},{7,6}} | collective-permute-start | bytes 25165832 | tf_op jit(solution)/shard_map/ppermute | solution.py:233
  2014.8 123.0 %collective-permute-start.7 = (bf16[512,8192]{1,0:T(8,128)(2,1)}, bf16[512,8192]{1,0:T(8,128)(2,1)}, u32[]{:S(2)}, u32[]{:S(2)}) collective-permute-start(bf16[512,8192]{1,0:T(8,128)(2,1)} %collective-permute-done.5.refs_5_.refs_6_), channel_id=1, source_target_pairs={{0,1},{1,0},{2,3},{3,2},{4,5},{5,4},{6,7},{7,6}} | collective-permute-start | bytes 25165832 | tf_op jit(solution)/shard_map/ppermute | solution.py:233
  2133.6 124.3 %collective-permute-start.17 = (bf16[128,4096]{1,0:T(8,128)(2,1)S(1)}, bf16[128,4096]{1,0:T(8,128)(2,1)S(1)}, u32[]{:S(2)}, u32[]{:S(2)}) collective-permute-start(bf16[128,4096]{1,0:T(8,128)(2,1)S(1)} %copy-done.1), channel_id=1, source_target_pairs={{0,5},{1,4},{2,7},{3,6},{4,1},{5,0},{6,3},{7,2}} | collective-permute-start | bytes 3145736 | tf_op jit(solution)/shard_map/ppermute | solution.py:233
  2134.9 123.1 %collective-permute-start.18 = (bf16[128,4096]{1,0:T(8,128)(2,1)S(1)}, bf16[128,4096]{1,0:T(8,128)(2,1)S(1)}, u32[]{:S(2)}, u32[]{:S(2)}) collective-permute-start(bf16[128,4096]{1,0:T(8,128)(2,1)S(1)} %copy-done.24), channel_id=1, source_target_pairs={{0,2},{1,3},{2,0},{3,1},{4,6},{5,7},{6,4},{7,5}} | collective-permute-start | bytes 3145736 | tf_op jit(solution)/shard_map/ppermute | solution.py:233
  2136.2 121.7 %collective-permute-start.19 = (bf16[128,4096]{1,0:T(8,128)(2,1)S(1)}, bf16[128,4096]{1,0:T(8,128)(2,1)S(1)}, u32[]{:S(2)}, u32[]{:S(2)}) collective-permute-start(bf16[128,4096]{1,0:T(8,128)(2,1)S(1)} %copy-done.23), channel_id=1, source_target_pairs={{0,6},{1,7},{2,4},{3,5},{4,2},{5,3},{6,0},{7,1}} | collective-permute-start | bytes 3145736 | tf_op jit(solution)/shard_map/ppermute | solution.py:233
  2137.1 120.9 %collective-permute-start.20 = (bf16[128,4096]{1,0:T(8,128)(2,1)S(1)}, bf16[128,4096]{1,0:T(8,128)(2,1)S(1)}, u32[]{:S(2)}, u32[]{:S(2)}) collective-permute-start(bf16[128,4096]{1,0:T(8,128)(2,1)S(1)} %copy-done.22), channel_id=1, source_target_pairs={{0,3},{1,2},{2,1},{3,0},{4,7},{5,6},{6,5},{7,4}} | collective-permute-start | bytes 3145736 | tf_op jit(solution)/shard_map/ppermute | solution.py:233
  2137.8 120.2 %collective-permute-start.21 = (bf16[128,4096]{1,0:T(8,128)(2,1)S(1)}, bf16[128,4096]{1,0:T(8,128)(2,1)}, u32[]{:S(2)}, u32[]{:S(2)}) collective-permute-start(bf16[128,4096]{1,0:T(8,128)(2,1)S(1)} %copy-done.21), channel_id=1, source_target_pairs={{0,7},{1,6},{2,5},{3,4},{4,3},{5,2},{6,1},{7,0}} | collective-permute-start | bytes 3145736 | tf_op jit(solution)/shard_map/ppermute | solution.py:233
  (45 other events, 3851.1 us)

commit v3 on v2

--- a/solution.py
+++ b/solution.py
@@ -10,13 +10,12 @@
 HEAD_DIM = 128
 ROPE_BASE = 500000
 Q_TILE = 256
-STEP_HEADS = 2
+STEP_HEADS = 4
 EXP_SCALE = math.log2(math.e) / math.sqrt(HEAD_DIM)
-W_PIECES = 2
+W_PIECES = 4
 QKV_TILE = 512
 OUT_TILE = 512
 CP_SIZE = 4
-OWN = 4
 NEAR = (0, 2)
 
 
@@ -128,7 +127,7 @@
         for which, index in picks:
             src = rows_in[which]
             if index is not None:
-                src = src.at[index * CP_SIZE + cp_ref[0]] if index < OWN else src.at[index - OWN]
+                src = src.at[index * CP_SIZE + cp_ref[0]]
             chunk = src.shape[0]
             copies.append((src, x_all.at[pl.ds(first, chunk), :]))
             first += chunk
@@ -192,16 +191,18 @@
     out_ref[...] = (add_ref[...].astype(jnp.float32) + acc).astype(out_ref.dtype)
 
 
-def out_project(cp_i, w_parts, pieces, placed, addend, out_type, row_block, buf=None, n_tile=OUT_TILE):
+def out_project(cp_i, w_parts, pieces, placed, addend, out_type, row_block, buf=None, n_tile=OUT_TILE, add_block=None):
     chunk, width = pieces[0].shape
     depth = sum(w.shape[0] for w in w_parts)
     n_rows = chunk * len(pieces) * width // depth
     dim = addend.shape[1]
     n_tile = min(n_tile, dim)
     any_spec = pl.BlockSpec(memory_space=pl.ANY)
+    add_block = row_block if add_block is None else add_block
     row_spec = pl.BlockSpec((n_rows, n_tile), lambda g, cp_ref: (row_block, g))
+    add_spec = pl.BlockSpec((n_rows, n_tile), lambda g, cp_ref: (add_block, g))
     operands = [*w_parts, *pieces, addend]
-    in_specs = [pl.BlockSpec((w.shape[0], n_tile), lambda g, cp_ref: (0, g)) for w in w_parts] + [any_spec] * len(pieces) + [row_spec]
+    in_specs = [pl.BlockSpec((w.shape[0], n_tile), lambda g, cp_ref: (0, g)) for w in w_parts] + [any_spec] * len(pieces) + [add_spec]
     aliases = {}
     if buf is not None:
         aliases = {1 + len(operands): 0}
@@ -251,13 +252,13 @@
         def seq_of(s, mc):
             return s * cp_size + (cp_i ^ mc)
 
-        def rows_for(s, mc):
-            return lax.dynamic_index_in_dim(x_rows, seq_of(s, mc), 0, keepdims=False)
-
-        near_got = swap(jnp.stack([rows_for(s, 1) for s in range(n_own)]), NEAR[1])
-        far_got = []
+        far_got, near_got, x_src = [], [], x_rows
         for s in range(n_own):
-            outgoing = [rows_for(s, mc) for mc in range(cp_size)]
+            outgoing = [lax.dynamic_index_in_dim(x_src, seq_of(s, mc), 0, keepdims=False) for mc in range(cp_size)]
+            near_out = [lax.dynamic_index_in_dim(x_rows, seq_of(n, 1), 0, keepdims=False) for n in range(n_own)] if s == 0 else []
+            x_src = lax.optimization_barrier((x_rows, *outgoing))[0]
+            if s == 0:
+                near_got = [swap(rows, NEAR[1]) for rows in near_out]
             far_got.append([swap(outgoing[m // tp_size], m) for m in far])
 
         q_rows = w_out.shape[0] // cp_size
@@ -271,8 +272,8 @@
             w_got[3][p] = swap(w_got[2][p], tp_size)
         w_other = [piece for part in w_got for piece in part]
 
-        picks = tuple(pick for s in range(n_own) for pick in ((0, s), (1, OWN + s)))
-        qkv_near = project(cp_ref, [x_rows, near_got], picks, chunk, weights)
+        picks = tuple(pick for s in range(n_own) for pick in ((0, s), (1 + s, None)))
+        qkv_near = project(cp_ref, [x_rows] + near_got, picks, chunk, weights)
         o_got = []
         for s in range(n_own):
             pos_seq = lax.dynamic_index_in_dim(pos_all, seq_of(s, 0), 1, keepdims=False).reshape(-1)
@@ -286,15 +287,17 @@
 
         x_flat = x_rows.reshape(n_seqs * chunk, dim)
         early = n_own - 1
-        width = w_out.shape[0]
         y_type = jax.ShapeDtypeStruct(x_flat.shape, jnp.bfloat16)
         part_type = jax.ShapeDtypeStruct((early * cp_size * chunk, dim), jnp.float32)
         placed = [(s, mc, 0, False) for s in range(early) for mc in range(cp_size)]
         partial = out_project(cp_ref, [w_out], [o_got[s][mc * tp_size] for s, mc, _, _ in placed], placed, x_flat, part_type, 0)
         placed = [(s, mc, 0, True) for s in range(early) for mc in range(cp_size)]
         y = out_project(cp_ref, w_other, [o_got[s][mc * tp_size + 1] for s, mc, _, _ in placed], placed, partial, y_type, 0)
-        placed = [(0, m // tp_size, (m % tp_size) * width, bool(m % tp_size)) for m in range(n_peers)]
-        y = out_project(cp_ref, [w_out] + w_other, o_got[early], placed, x_flat, y_type, early, y)
+        last_type = jax.ShapeDtypeStruct((cp_size * chunk, dim), jnp.float32)
+        placed = [(0, mc, 0, False) for mc in range(cp_size)]
+        partial = out_project(cp_ref, [w_out], o_got[early][0::tp_size], placed, x_flat, last_type, 0, add_block=early)
+        placed = [(0, mc, 0, True) for mc in range(cp_size)]
+        y = out_project(cp_ref, w_other, o_got[early][1::tp_size], placed, partial, y_type, early, y, add_block=0)
         return y.reshape(n_seqs, chunk, dim)
 
 

time: 2350 us -> 2310 us (0.983)
  blocking collectives: 139 us -> 82.2 us
    all_gather x1, blocking collectives: 139 us -> 82.2 us  [local_fn(): pos_all = lax.all_gather(pos_rows, ('tp', 'cp'), axis=0, tiled=False)]
    ppermute x61 -> x72, waiting for transfers between devices: 608 us -> 628 us  [swap(): return lax.ppermute(vals, ('tp', 'cp'), pairs)]
    pallas_call x3 -> x4, Pallas kernels: 318 us -> 330 us  [out_project(): pl.pallas_call(functools.partial(out_kernel, len(w_parts), placed, width...]
    ppermute x61 -> x72, starting transfers between devices: 65.1 us -> 63.4 us  [swap(): return lax.ppermute(vals, ('tp', 'cp'), pairs)]
  transfers between devices with their start and end apart: 61 -> 72, of which waited for: 15 -> 15; matrix products, arithmetic and copies ran while one was open for 1% -> 2% of each run, Pallas kernels for 59% -> 62%
where the time goes in v3:
time: 2310 us; the launch traced here: 2300 us
  Pallas kernels  1460 us (63%)
  waiting for transfers between devices  628 us (27%)
  blocking collectives  82.2 us (4%)
  starting transfers between devices  63.4 us (3%)
  local copies, waits for them, and re-layouts  53.1 us (2%)
    pallas_call x5, Pallas kernels, project(): pl.pallas_call(functools.partial(qkv_kernel, len(rows_in), picks), out_sh...  896 us
    ppermute x72, waiting for transfers between devices, swap(): return lax.ppermute(vals, ('tp', 'cp'), pairs)  628 us
    pallas_call x4, Pallas kernels, out_project(): pl.pallas_call(functools.partial(out_kernel, len(w_parts), placed, width...  330 us
    pallas_call x4, Pallas kernels, attend(): pl.pallas_call(functools.partial(attend_kernel, sources), out_shape=[jax....  236 us
    all_gather x1, blocking collectives, local_fn(): pos_all = lax.all_gather(pos_rows, ('tp', 'cp'), axis=0, tiled=False)  82.2 us
    ppermute x72, starting transfers between devices, swap(): return lax.ppermute(vals, ('tp', 'cp'), pairs)  63.4 us
  transfers between devices with their start and end apart: 72, of which 15 were waited for; matrix products, arithmetic and copies ran while one was open for 2% of the time, Pallas kernels for 62%

profile of v3, /device:TPU:0, one launch (start us, length us, event | category | flops | bytes accessed | tf_op | source)
XLA Modules:
  0.0 2298.8 jit_solution(5667129933663058255)
XLA Ops:
  0.0 10.8 dynamic-slice_bitcast_fusion.12
  11.7 3.0 collective-permute-start.33
  16.2 7.0 dynamic-slice_bitcast_fusion.8
  23.3 7.0 dynamic-slice_bitcast_fusion.4
  30.3 82.2 %all-gather = s32[128,128]{1,0:T(8,128)S(1)} all-gather(s32[16,128]{1,0:T(8,128)S(1)} %copy-done.12), channel_id=2, replica_groups=mesh['data'=1,'tp'=2,'cp'=4] {'tp','cp'}, dimensions={0}, use_global_device_ids=true | all-gather | bytes 73728 | tf_op jit(solution)/shard_map/all_gather | solution.py:246
  113.9 7.5 fusion.3
  123.7 7.0 dynamic-slice_bitcast_fusion
  130.7 12.3 constant_dynamic-slice_fusion.4
  143.6 1.4 copy-done.14
  145.0 1.4 collective-permute-start.36
  148.5 221.6 %project.5.refs_0_.refs_2_.refs_4_ = bf16[1024,12288]{1,0:T(8,128)(2,1)} custom-call(s32[1]{0:T(128)} %bitcast.cp_ref, bf16[16,128,8192]{2,1,0:T(8,128)(2,1)} %refs_0_.3, bf16[128,8192]{1,0:T(8,128)(2,1)} %collective-permute-done.16.refs_1_, bf16[128,8192]{1,0:T(8,128)(2,1)} %copy-done.14, bf16[128,8192]{1,0:T(8,128)(2,1)} %collective-permute-done.18.refs_3_, ...), custom_call_target="tpu_custom_call" | custom-call | flops 206158430208 | bytes 243269632 | tf_op jit(solution)/shard_map/project/pallas_call | solution.py:150
  370.1 1.8 collective-permute-start.53
  373.3 2.8 collective-permute-start.56
  376.5 168.9 %project.7.refs_1_.refs_3_.refs_5_ = bf16[768,12288]{1,0:T(8,128)(2,1)} custom-call(s32[1]{0:T(128)} %bitcast.cp_ref, bf16[128,8192]{1,0:T(8,128)(2,1)} %collective-permute-done.33.refs_0_, bf16[128,8192]{1,0:T(8,128)(2,1)} %collective-permute-done.34.refs_1_, bf16[128,8192]{1,0:T(8,128)(2,1)} %collective-permute-done.35.refs_2_, ...), custom_call_target="tpu_custom_call" | custom-call | flops 154618822656 | bytes 232783872 | tf_op jit(solution)/shard_map/project/pallas_call | solution.py:150
  545.5 1.1 collective-permute-start.43
  546.6 1.9 collective-permute-start.48
  548.8 6.4 collective-permute-done.55.refs_2_
  555.8 168.5 %project.9.refs_1_.refs_3_.refs_5_ = bf16[768,12288]{1,0:T(8,128)(2,1)} custom-call(s32[1]{0:T(128)} %bitcast.cp_ref, bf16[128,8192]{1,0:T(8,128)(2,1)} %collective-permute-done.53.refs_0_, bf16[128,8192]{1,0:T(8,128)(2,1)} %collective-permute-done.54.refs_1_, bf16[128,8192]{1,0:T(8,128)(2,1)} %collective-permute-done.55.refs_2_, ...), custom_call_target="tpu_custom_call" | custom-call | flops 154618822656 | bytes 232783872 | tf_op jit(solution)/shard_map/project/pallas_call | solution.py:150
  725.0 2.8 collective-permute-done.43.refs_0_
  728.3 1.4 collective-permute-start.20
  729.6 58.8 %attend.7 = (bf16[128,4096]{1,0:T(8,128)(2,1)S(1)}, bf16[128,4096]{1,0:T(8,128)(2,1)}, bf16[128,4096]{1,0:T(8,128)(2,1)S(1)}, bf16[128,4096]{1,0:T(8,128)(2,1)},...) custom-call(s32[2,8]{1,0:T(2,128)S(1)} %pad_add_fusion.place_ref, ...), custom_call_target="tpu_custom_call" | custom-call | flops 34359738368 | bytes 33554432 | tf_op jit(solution)/shard_map/attend/pallas_call | solution.py:87
  788.4 1.0 copy-done
  789.4 2.0 collective-permute-start.25
  791.4 2.0 collective-permute-start.23
  794.1 71.8 %collective-permute-done.20.refs_0_ = bf16[128,8192]{1,0:T(8,128)(2,1)} collective-permute-done((bf16[128,8192]{1,0:T(8,128)(2,1)}, bf16[128,8192]{1,0:T(8,128)(2,1)}, u32[]{:S(2)}, u32[]{:S(2)}) %collective-permute-start.20) | collective-permute-done | bytes 2097184 | tf_op jit(solution)/shard_map/ppermute | solution.py:234
  865.9 1.0 collective-permute-start.59
  867.0 168.5 %project.8.refs_1_.refs_3_.refs_5_ = bf16[768,12288]{1,0:T(8,128)(2,1)} custom-call(s32[1]{0:T(128)} %bitcast.cp_ref, bf16[128,8192]{1,0:T(8,128)(2,1)} %collective-permute-done.43.refs_0_, bf16[128,8192]{1,0:T(8,128)(2,1)} %collective-permute-done.44.refs_1_, bf16[128,8192]{1,0:T(8,128)(2,1)} %collective-permute-done.45.refs_2_, ...), custom_call_target="tpu_custom_call" | custom-call | flops 154618822656 | bytes 232783872 | tf_op jit(solution)/shard_map/project/pallas_call | solution.py:150
  1035.5 2.5 collective-permute-start.61
  1038.8 1.6 collective-permute-start.70
  1040.4 58.9 %attend.6 = (bf16[128,4096]{1,0:T(8,128)(2,1)S(1)}, bf16[128,4096]{1,0:T(8,128)(2,1)S(1)}, bf16[128,4096]{1,0:T(8,128)(2,1)}, bf16[128,4096]{1,0:T(8,128)(2,1)S(...) custom-call(s32[2,8]{1,0:T(2,128)S(1)} %pad_add_fusion.place_ref, ...), custom_call_target="tpu_custom_call" | custom-call | flops 34359738368 | bytes 33554432 | tf_op jit(solution)/shard_map/attend/pallas_call | solution.py:87
  1099.3 6.7 collective-permute-done.60.refs_25_
  1106.0 1.2 collective-permute-start.71
  1107.7 1.5 collective-permute-start.50
  1109.6 2.0 collective-permute-start.52
  1111.6 59.0 %attend.5 = (bf16[128,4096]{1,0:T(8,128)(2,1)S(1)}, bf16[128,4096]{1,0:T(8,128)(2,1)}, bf16[128,4096]{1,0:T(8,128)(2,1)S(1)}, bf16[128,4096]{1,0:T(8,128)(2,1)},...) custom-call(s32[2,8]{1,0:T(2,128)S(1)} %pad_add_fusion.place_ref, ...), custom_call_target="tpu_custom_call" | custom-call | flops 34359738368 | bytes 33554432 | tf_op jit(solution)/shard_map/attend/pallas_call | solution.py:87
  1171.3 6.9 collective-permute-done.49.refs_20_
  1178.8 21.2 collective-permute-done.50.refs_21_
  1202.9 168.5 %project.6.refs_1_.refs_3_.refs_5_ = bf16[768,12288]{1,0:T(8,128)(2,1)} custom-call(s32[1]{0:T(128)} %bitcast.cp_ref, bf16[128,8192]{1,0:T(8,128)(2,1)} %collective-permute-done.20.refs_0_, bf16[128,8192]{1,0:T(8,128)(2,1)} %collective-permute-done.21.refs_1_, bf16[128,8192]{1,0:T(8,128)(2,1)} %collective-permute-done.22.refs_2_, ...), custom_call_target="tpu_custom_call" | custom-call | flops 154618822656 | bytes 232783872 | tf_op jit(solution)/shard_map/project/pallas_call | solution.py:150
  1372.1 2.3 collective-permute-start.41
  1375.1 1.6 collective-permute-start.64
  1376.7 59.4 %attend.4 = (bf16[128,4096]{1,0:T(8,128)(2,1)S(1)}, bf16[128,4096]{1,0:T(8,128)(2,1)S(1)}, bf16[128,4096]{1,0:T(8,128)(2,1)S(1)}, bf16[128,4096]{1,0:T(8,128)(2,...) custom-call(s32[2,8]{1,0:T(2,128)S(1)} %pad_add_fusion.place_ref, ...), custom_call_target="tpu_custom_call" | custom-call | flops 34359738368 | bytes 33554432 | tf_op jit(solution)/shard_map/attend/pallas_call | solution.py:87
  1436.7 1.6 collective-permute-start.31
  1438.3 5.8 collective-permute-done.64.refs_3_
  1444.7 21.0 collective-permute-done.65.refs_4_
  1465.7 1.0 copy-done.28
  1468.4 1.3 collective-permute-start.1
  1469.7 19.3 collective-permute-done.31.refs_3_
  1489.7 20.4 collective-permute-done.3.refs_3_
  1510.1 1.6 collective-permute-start.11
  1511.6 88.2 %collective-permute-done.2.refs_2_ = bf16[256,8192]{1,0:T(8,128)(2,1)S(1)} collective-permute-done((bf16[256,8192]{1,0:T(8,128)(2,1)}, bf16[256,8192]{1,0:T(8,128)(2,1)S(1)}, u32[]{:S(2)}, u32[]{:S(2)}) %collective-permute-start.2) | collective-permute-done | bytes 4194336 | tf_op jit(solution)/shard_map/ppermute | solution.py:234
  1599.9 1.6 collective-permute-start.10
  1601.4 88.3 %collective-permute-done.1.refs_1_ = bf16[256,8192]{1,0:T(8,128)(2,1)S(1)} collective-permute-done((bf16[256,8192]{1,0:T(8,128)(2,1)}, bf16[256,8192]{1,0:T(8,128)(2,1)S(1)}, u32[]{:S(2)}, u32[]{:S(2)}) %collective-permute-start.1) | collective-permute-done | bytes 4194336 | tf_op jit(solution)/shard_map/ppermute | solution.py:234
  1689.7 89.8 %collective-permute-done.refs_0_ = bf16[256,8192]{1,0:T(8,128)(2,1)} collective-permute-done((bf16[256,8192]{1,0:T(8,128)(2,1)S(1)}, bf16[256,8192]{1,0:T(8,128)(2,1)}, u32[]{:S(2)}, u32[]{:S(2)}) %collective-permute-start) | collective-permute-done | bytes 4194336 | tf_op jit(solution)/shard_map/ppermute | solution.py:234
  1779.5 1.7 collective-permute-start.9
  1782.1 90.9 %collective-permute-done.9.refs_9_ = bf16[256,8192]{1,0:T(8,128)(2,1)} collective-permute-done((bf16[256,8192]{1,0:T(8,128)(2,1)S(1)}, bf16[256,8192]{1,0:T(8,128)(2,1)}, u32[]{:S(2)}, u32[]{:S(2)}) %collective-permute-start.9) | collective-permute-done | bytes 4194336 | tf_op jit(solution)/shard_map/ppermute | solution.py:234
  1873.6 88.3 %collective-permute-done.8.refs_8_ = bf16[256,8192]{1,0:T(8,128)(2,1)} collective-permute-done((bf16[256,8192]{1,0:T(8,128)(2,1)}, bf16[256,8192]{1,0:T(8,128)(2,1)}, u32[]{:S(2)}, u32[]{:S(2)}) %collective-permute-start.8) | collective-permute-done | bytes 4194336 | tf_op jit(solution)/shard_map/ppermute | solution.py:234
  1961.9 117.7 %out_project.5.refs_28_ = f32[1536,8192]{1,0:T(8,128)} custom-call(s32[1]{0:T(128)} %bitcast.cp_ref, bf16[4096,8192]{1,0:T(8,128)(2,1)} %refs_0_.5, bf16[128,4096]{1,0:T(8,128)(2,1)S(1)} %get-tuple-element.65.refs_1_, bf16[128,4096]{1,0:T(8,128)(2,1)} %copy-done.26, bf16[128,4096]{1,0:T(8,128)(2,1)} %copy-done.27, bf16[128,4096]{1,0:T(8,128)(2,1)} %copy-done.28, ...), custom_call_target="tpu_custom_call" | custom-call | flops 103079215104 | bytes 130023424 | tf_op jit(solution)/shard_map/out_project/pallas_call | solution.py:211
  2079.6 46.7 %out_project.4.refs_20_ = f32[512,8192]{1,0:T(8,128)} custom-call(s32[1]{0:T(128)} %bitcast.cp_ref, bf16[4096,8192]{1,0:T(8,128)(2,1)} %refs_0_.5, bf16[128,4096]{1,0:T(8,128)(2,1)S(1)} %get-tuple-element.49.refs_1_, bf16[128,4096]{1,0:T(8,128)(2,1)} %copy-done.29, bf16[128,4096]{1,0:T(8,128)(2,1)} %copy-done.30, ...), custom_call_target="tpu_custom_call" | custom-call | flops 34359738368 | bytes 88080384 | tf_op jit(solution)/shard_map/out_project/pallas_call | solution.py:211
  2126.9 1.3 collective-permute-start.27
  2128.2 1.5 collective-permute-start.28
  2129.7 1.0 collective-permute-start.29
  2130.8 119.0 %out_project.6.refs_21_ = bf16[2048,8192]{1,0:T(8,128)(2,1)} custom-call(s32[1]{0:T(128)} %bitcast.cp_ref, bf16[256,8192]{1,0:T(8,128)(2,1)} %collective-permute-done.refs_0_, bf16[256,8192]{1,0:T(8,128)(2,1)} %copy-done.4, bf16[256,8192]{1,0:T(8,128)(2,1)} %copy-done.3, bf16[256,8192]{1,0:T(8,128)(2,1)} %collective-permute-done.3.refs_3_, ...), custom_call_target="tpu_custom_call" | custom-call | flops 103079215104 | bytes 130023424 | tf_op jit(solution)/shard_map/out_project/pallas_call | solution.py:211
  2251.1 1.0 copy-done.11
  2252.1 46.5 %out_project.7 = bf16[2048,8192]{1,0:T(8,128)(2,1)} custom-call(s32[1]{0:T(128)} %bitcast.cp_ref, bf16[256,8192]{1,0:T(8,128)(2,1)} %collective-permute-done.refs_0_, bf16[256,8192]{1,0:T(8,128)(2,1)} %copy-done.4, bf16[256,8192]{1,0:T(8,128)(2,1)} %copy-done.3, bf16[256,8192]{1,0:T(8,128)(2,1)} %collective-permute-done.3.refs_3_, ...), custom_call_target="tpu_custom_call", output_to_operand_aliasing={{}: (22, {})} | custom-call | flops 34359738368 | bytes 88080384 | tf_op jit(solution)/shard_map/out_project/pallas_call | solution.py:211
  (176 shorter events, 27.9 us)
Async XLA Ops:
  10.8 112.0 %collective-permute-start.19 = (bf16[128,8192]{1,0:T(8,128)(2,1)}, bf16[128,8192]{1,0:T(8,128)(2,1)}, u32[]{:S(2)}, u32[]{:S(2)}) collective-permute-start(bf16[128,8192]{1,0:T(8,128)(2,1)} %get-tuple-element.96), channel_id=1, source_target_pairs={{0,1},{1,0},{2,3},{3,2},{4,5},{5,4},{6,7},{7,6}} | collective-permute-start | bytes 6291464 | tf_op jit(solution)/shard_map/ppermute | solution.py:234
  11.7 131.3 %collective-permute-start.18 = (bf16[128,8192]{1,0:T(8,128)(2,1)}, bf16[128,8192]{1,0:T(8,128)(2,1)}, u32[]{:S(2)}, u32[]{:S(2)}) collective-permute-start(bf16[128,8192]{1,0:T(8,128)(2,1)} %get-tuple-element.97), channel_id=1, source_target_pairs={{0,1},{1,0},{2,3},{3,2},{4,5},{5,4},{6,7},{7,6}} | collective-permute-start | bytes 6291464 | tf_op jit(solution)/shard_map/ppermute | solution.py:234
  11.7 134.7 %collective-permute-start.33 = (bf16[128,8192]{1,0:T(8,128)(2,1)}, bf16[128,8192]{1,0:T(8,128)(2,1)}, u32[]{:S(2)}, u32[]{:S(2)}) collective-permute-start(bf16[128,8192]{1,0:T(8,128)(2,1)} %get-tuple-element.95), channel_id=1, source_target_pairs={{0,4},{1,5},{2,6},{3,7},{4,0},{5,1},{6,2},{7,3}} | collective-permute-start | bytes 6291464 | tf_op jit(solution)/shard_map/ppermute | solution.py:234
  14.7 132.1 %collective-permute-start.38 = (bf16[128,8192]{1,0:T(8,128)(2,1)}, bf16[128,8192]{1,0:T(8,128)(2,1)}, u32[]{:S(2)}, u32[]{:S(2)}) collective-permute-start(bf16[128,8192]{1,0:T(8,128)(2,1)} %get-tuple-element.93), channel_id=1, source_target_pairs={{0,7},{1,6},{2,5},{3,4},{4,3},{5,2},{6,1},{7,0}} | collective-permute-start | bytes 6291464 | tf_op jit(solution)/shard_map/ppermute | solution.py:234
  15.5 132.1 %collective-permute-start.16 = (bf16[128,8192]{1,0:T(8,128)(2,1)}, bf16[128,8192]{1,0:T(8,128)(2,1)}, u32[]{:S(2)}, u32[]{:S(2)}) collective-permute-start(bf16[128,8192]{1,0:T(8,128)(2,1)} %get-tuple-element.99), channel_id=1, source_target_pairs={{0,1},{1,0},{2,3},{3,2},{4,5},{5,4},{6,7},{7,6}} | collective-permute-start | bytes 6291464 | tf_op jit(solution)/shard_map/ppermute | solution.py:234
  142.9 227.1 %collective-permute-start.37 = (bf16[128,8192]{1,0:T(8,128)(2,1)}, bf16[128,8192]{1,0:T(8,128)(2,1)}, u32[]{:S(2)}, u32[]{:S(2)}) collective-permute-start(bf16[128,8192]{1,0:T(8,128)(2,1)} %get-tuple-element.93), channel_id=1, source_target_pairs={{0,3},{1,2},{2,1},{3,0},{4,7},{5,6},{6,5},{7,4}} | collective-permute-start | bytes 6291464 | tf_op jit(solution)/shard_map/ppermute | solution.py:234
  145.0 226.9 %collective-permute-start.36 = (bf16[128,8192]{1,0:T(8,128)(2,1)}, bf16[128,8192]{1,0:T(8,128)(2,1)}, u32[]{:S(2)}, u32[]{:S(2)}) collective-permute-start(bf16[128,8192]{1,0:T(8,128)(2,1)} %get-tuple-element.94), channel_id=1, source_target_pairs={{0,6},{1,7},{2,4},{3,5},{4,2},{5,3},{6,0},{7,1}} | collective-permute-start | bytes 6291464 | tf_op jit(solution)/shard_map/ppermute | solution.py:234
  146.4 226.2 %collective-permute-start.35 = (bf16[128,8192]{1,0:T(8,128)(2,1)}, bf16[128,8192]{1,0:T(8,128)(2,1)}, u32[]{:S(2)}, u32[]{:S(2)}) collective-permute-start(bf16[128,8192]{1,0:T(8,128)(2,1)} %get-tuple-element.94), channel_id=1, source_target_pairs={{0,2},{1,3},{2,0},{3,1},{4,6},{5,7},{6,4},{7,5}} | collective-permute-start | bytes 6291464 | tf_op jit(solution)/shard_map/ppermute | solution.py:234
  146.7 226.6 %collective-permute-start.34 = (bf16[128,8192]{1,0:T(8,128)(2,1)}, bf16[128,8192]{1,0:T(8,128)(2,1)}, u32[]{:S(2)}, u32[]{:S(2)}) collective-permute-start(bf16[128,8192]{1,0:T(8,128)(2,1)} %get-tuple-element.99), channel_id=1, source_target_pairs={{0,5},{1,4},{2,7},{3,6},{4,1},{5,0},{6,3},{7,2}} | collective-permute-start | bytes 6291464 | tf_op jit(solution)/shard_map/ppermute | solution.py:234
  147.5 228.6 %collective-permute-start.54 = (bf16[128,8192]{1,0:T(8,128)(2,1)}, bf16[128,8192]{1,0:T(8,128)(2,1)}, u32[]{:S(2)}, u32[]{:S(2)}) collective-permute-start(bf16[128,8192]{1,0:T(8,128)(2,1)} %get-tuple-element.87), channel_id=1, source_target_pairs={{0,5},{1,4},{2,7},{3,6},{4,1},{5,0},{6,3},{7,2}} | collective-permute-start | bytes 6291464 | tf_op jit(solution)/shard_map/ppermute | solution.py:234
  370.1 175.4 %collective-permute-start.53 = (bf16[128,8192]{1,0:T(8,128)(2,1)}, bf16[128,8192]{1,0:T(8,128)(2,1)}, u32[]{:S(2)}, u32[]{:S(2)}) collective-permute-start(bf16[128,8192]{1,0:T(8,128)(2,1)} %get-tuple-element.88), channel_id=1, source_target_pairs={{0,4},{1,5},{2,6},{3,7},{4,0},{5,1},{6,2},{7,3}} | collective-permute-start | bytes 6291464 | tf_op jit(solution)/shard_map/ppermute | solution.py:234
  371.8 173.7 %collective-permute-start.58 = (bf16[128,8192]{1,0:T(8,128)(2,1)}, bf16[128,8192]{1,0:T(8,128)(2,1)}, u32[]{:S(2)}, u32[]{:S(2)}) collective-permute-start(bf16[128,8192]{1,0:T(8,128)(2,1)} %get-tuple-element.85), channel_id=1, source_target_pairs={{0,7},{1,6},{2,5},{3,4},{4,3},{5,2},{6,1},{7,0}} | collective-permute-start | bytes 6291464 | tf_op jit(solution)/shard_map/ppermute | solution.py:234
  372.6 174.0 %collective-permute-start.57 = (bf16[128,8192]{1,0:T(8,128)(2,1)}, bf16[128,8192]{1,0:T(8,128)(2,1)}, u32[]{:S(2)}, u32[]{:S(2)}) collective-permute-start(bf16[128,8192]{1,0:T(8,128)(2,1)} %get-tuple-element.85), channel_id=1, source_target_pairs={{0,3},{1,2},{2,1},{3,0},{4,7},{5,6},{6,5},{7,4}} | collective-permute-start | bytes 6291464 | tf_op jit(solution)/shard_map/ppermute | solution.py:234
  373.3 175.2 %collective-permute-start.56 = (bf16[128,8192]{1,0:T(8,128)(2,1)}, bf16[128,8192]{1,0:T(8,128)(2,1)}, u32[]{:S(2)}, u32[]{:S(2)}) collective-permute-start(bf16[128,8192]{1,0:T(8,128)(2,1)} %get-tuple-element.86), channel_id=1, source_target_pairs={{0,6},{1,7},{2,4},{3,5},{4,2},{5,3},{6,0},{7,1}} | collective-permute-start | bytes 6291464 | tf_op jit(solution)/shard_map/ppermute | solution.py:234
  376.1 179.0 %collective-permute-start.55 = (bf16[128,8192]{1,0:T(8,128)(2,1)}, bf16[128,8192]{1,0:T(8,128)(2,1)}, u32[]{:S(2)}, u32[]{:S(2)}) collective-permute-start(bf16[128,8192]{1,0:T(8,128)(2,1)} %get-tuple-element.86), channel_id=1, source_target_pairs={{0,2},{1,3},{2,0},{3,1},{4,6},{5,7},{6,4},{7,5}} | collective-permute-start | bytes 6291464 | tf_op jit(solution)/shard_map/ppermute | solution.py:234
  545.5 178.8 %collective-permute-start.44 = (bf16[128,8192]{1,0:T(8,128)(2,1)}, bf16[128,8192]{1,0:T(8,128)(2,1)}, u32[]{:S(2)}, u32[]{:S(2)}) collective-permute-start(bf16[128,8192]{1,0:T(8,128)(2,1)} %get-tuple-element.91), channel_id=1, source_target_pairs={{0,5},{1,4},{2,7},{3,6},{4,1},{5,0},{6,3},{7,2}} | collective-permute-start | bytes 6291464 | tf_op jit(solution)/shard_map/ppermute | solution.py:234
  545.5 182.3 %collective-permute-start.43 = (bf16[128,8192]{1,0:T(8,128)(2,1)}, bf16[128,8192]{1,0:T(8,128)(2,1)}, u32[]{:S(2)}, u32[]{:S(2)}) collective-permute-start(bf16[128,8192]{1,0:T(8,128)(2,1)} %get-tuple-element.92), channel_id=1, source_target_pairs={{0,4},{1,5},{2,6},{3,7},{4,0},{5,1},{6,2},{7,3}} | collective-permute-start | bytes 6291464 | tf_op jit(solution)/shard_map/ppermute | solution.py:234
  546.6 181.7 %collective-permute-start.48 = (bf16[128,8192]{1,0:T(8,128)(2,1)}, bf16[128,8192]{1,0:T(8,128)(2,1)}, u32[]{:S(2)}, u32[]{:S(2)}) collective-permute-start(bf16[128,8192]{1,0:T(8,128)(2,1)} %get-tuple-element.89), channel_id=1, source_target_pairs={{0,7},{1,6},{2,5},{3,4},{4,3},{5,2},{6,1},{7,0}} | collective-permute-start | bytes 6291464 | tf_op jit(solution)/shard_map/ppermute | solution.py:234
  548.5 240.9 %collective-permute-start.47 = (bf16[128,8192]{1,0:T(8,128)(2,1)}, bf16[128,8192]{1,0:T(8,128)(2,1)}, u32[]{:S(2)}, u32[]{:S(2)}) collective-permute-start(bf16[128,8192]{1,0:T(8,128)(2,1)} %get-tuple-element.89), channel_id=1, source_target_pairs={{0,3},{1,2},{2,1},{3,0},{4,7},{5,6},{6,5},{7,4}} | collective-permute-start | bytes 6291464 | tf_op jit(solution)/shard_map/ppermute | solution.py:234
  555.1 236.3 %collective-permute-start.46 = (bf16[128,8192]{1,0:T(8,128)(2,1)}, bf16[128,8192]{1,0:T(8,128)(2,1)}, u32[]{:S(2)}, u32[]{:S(2)}) collective-permute-start(bf16[128,8192]{1,0:T(8,128)(2,1)} %get-tuple-element.90), channel_id=1, source_target_pairs={{0,6},{1,7},{2,4},{3,5},{4,2},{5,3},{6,0},{7,1}} | collective-permute-start | bytes 6291464 | tf_op jit(solution)/shard_map/ppermute | solution.py:234
  724.3 67.1 %collective-permute-start.45 = (bf16[128,8192]{1,0:T(8,128)(2,1)}, bf16[128,8192]{1,0:T(8,128)(2,1)}, u32[]{:S(2)}, u32[]{:S(2)}) collective-permute-start(bf16[128,8192]{1,0:T(8,128)(2,1)} %get-tuple-element.90), channel_id=1, source_target_pairs={{0,2},{1,3},{2,0},{3,1},{4,6},{5,7},{6,4},{7,5}} | collective-permute-start | bytes 6291464 | tf_op jit(solution)/shard_map/ppermute | solution.py:234
  727.8 65.7 %collective-permute-start.21 = (bf16[128,8192]{1,0:T(8,128)(2,1)}, bf16[128,8192]{1,0:T(8,128)(2,1)}, u32[]{:S(2)}, u32[]{:S(2)}) collective-permute-start(bf16[128,8192]{1,0:T(8,128)(2,1)} %get-tuple-element.83), channel_id=1, source_target_pairs={{0,5},{1,4},{2,7},{3,6},{4,1},{5,0},{6,3},{7,2}} | collective-permute-start | bytes 6291464 | tf_op jit(solution)/shard_map/ppermute | solution.py:234
  728.3 137.7 %collective-permute-start.20 = (bf16[128,8192]{1,0:T(8,128)(2,1)}, bf16[128,8192]{1,0:T(8,128)(2,1)}, u32[]{:S(2)}, u32[]{:S(2)}) collective-permute-start(bf16[128,8192]{1,0:T(8,128)(2,1)} %get-tuple-element.84), channel_id=1, source_target_pairs={{0,4},{1,5},{2,6},{3,7},{4,0},{5,1},{6,2},{7,3}} | collective-permute-start | bytes 6291464 | tf_op jit(solution)/shard_map/ppermute | solution.py:234
  789.4 246.0 %collective-permute-start.25 = (bf16[128,8192]{1,0:T(8,128)(2,1)}, bf16[128,8192]{1,0:T(8,128)(2,1)}, u32[]{:S(2)}, u32[]{:S(2)}) collective-permute-start(bf16[128,8192]{1,0:T(8,128)(2,1)} %get-tuple-element.81), channel_id=1, source_target_pairs={{0,7},{1,6},{2,5},{3,4},{4,3},{5,2},{6,1},{7,0}} | collective-permute-start | bytes 6291464 | tf_op jit(solution)/shard_map/ppermute | solution.py:234
  791.4 244.1 %collective-permute-start.24 = (bf16[128,8192]{1,0:T(8,128)(2,1)}, bf16[128,8192]{1,0:T(8,128)(2,1)}, u32[]{:S(2)}, u32[]{:S(2)}) collective-permute-start(bf16[128,8192]{1,0:T(8,128)(2,1)} %get-tuple-element.81), channel_id=1, source_target_pairs={{0,3},{1,2},{2,1},{3,0},{4,7},{5,6},{6,5},{7,4}} | collective-permute-start | bytes 6291464 | tf_op jit(solution)/shard_map/ppermute | solution.py:234
  791.4 246.6 %collective-permute-start.23 = (bf16[128,8192]{1,0:T(8,128)(2,1)}, bf16[128,8192]{1,0:T(8,128)(2,1)}, u32[]{:S(2)}, u32[]{:S(2)}) collective-permute-start(bf16[128,8192]{1,0:T(8,128)(2,1)} %get-tuple-element.82), channel_id=1, source_target_pairs={{0,6},{1,7},{2,4},{3,5},{4,2},{5,3},{6,0},{7,1}} | collective-permute-start | bytes 6291464 | tf_op jit(solution)/shard_map/ppermute | solution.py:234
  793.5 245.4 %collective-permute-start.22 = (bf16[128,8192]{1,0:T(8,128)(2,1)}, bf16[128,8192]{1,0:T(8,128)(2,1)}, u32[]{:S(2)}, u32[]{:S(2)}) collective-permute-start(bf16[128,8192]{1,0:T(8,128)(2,1)} %get-tuple-element.82), channel_id=1, source_target_pairs={{0,2},{1,3},{2,0},{3,1},{4,6},{5,7},{6,4},{7,5}} | collective-permute-start | bytes 6291464 | tf_op jit(solution)/shard_map/ppermute | solution.py:234
  865.9 172.9 %collective-permute-start.59 = (bf16[128,4096]{1,0:T(8,128)(2,1)}, bf16[128,4096]{1,0:T(8,128)(2,1)}, u32[]{:S(2)}, u32[]{:S(2)}) collective-permute-start(bf16[128,4096]{1,0:T(8,128)(2,1)} %get-tuple-element.61), channel_id=1, source_target_pairs={{0,4},{1,5},{2,6},{3,7},{4,0},{5,1},{6,2},{7,3}} | collective-permute-start | bytes 3145736 | tf_op jit(solution)/shard_map/ppermute | solution.py:234
  1035.4 70.6 %collective-permute-start.60 = (bf16[128,4096]{1,0:T(8,128)(2,1)}, bf16[128,4096]{1,0:T(8,128)(2,1)S(1)}, u32[]{:S(2)}, u32[]{:S(2)}) collective-permute-start(bf16[128,4096]{1,0:T(8,128)(2,1)} %get-tuple-element.62), channel_id=1, source_target_pairs={{0,5},{1,4},{2,7},{3,6},{4,1},{5,0},{6,3},{7,2}} | collective-permute-start | bytes 3145736 | tf_op jit(solution)/shard_map/ppermute | solution.py:234
  1035.5 71.7 %collective-permute-start.61 = (bf16[128,4096]{1,0:T(8,128)(2,1)}, bf16[128,4096]{1,0:T(8,128)(2,1)S(1)}, u32[]{:S(2)}, u32[]{:S(2)}) collective-permute-start(bf16[128,4096]{1,0:T(8,128)(2,1)} %get-tuple-element.63), channel_id=1, source_target_pairs={{0,6},{1,7},{2,4},{3,5},{4,2},{5,3},{6,0},{7,1}} | collective-permute-start | bytes 3145736 | tf_op jit(solution)/shard_map/ppermute | solution.py:234
  1038.0 69.7 %collective-permute-start.62 = (bf16[128,4096]{1,0:T(8,128)(2,1)}, bf16[128,4096]{1,0:T(8,128)(2,1)S(1)}, u32[]{:S(2)}, u32[]{:S(2)}) collective-permute-start(bf16[128,4096]{1,0:T(8,128)(2,1)} %get-tuple-element.64), channel_id=1, source_target_pairs={{0,7},{1,6},{2,5},{3,4},{4,3},{5,2},{6,1},{7,0}} | collective-permute-start | bytes 3145736 | tf_op jit(solution)/shard_map/ppermute | solution.py:234
  1038.8 70.4 %collective-permute-start.69 = (bf16[128,4096]{1,0:T(8,128)(2,1)S(1)}, bf16[128,4096]{1,0:T(8,128)(2,1)S(1)}, u32[]{:S(2)}, u32[]{:S(2)}) collective-permute-start(bf16[128,4096]{1,0:T(8,128)(2,1)S(1)} %get-tuple-element.74), channel_id=1, source_target_pairs={{0,1},{1,0},{2,3},{3,2},{4,5},{5,4},{6,7},{7,6}} | collective-permute-start | bytes 3145736 | tf_op jit(solution)/shard_map/ppermute | solution.py:234
  1038.8 70.8 %collective-permute-start.70 = (bf16[128,4096]{1,0:T(8,128)(2,1)}, bf16[128,4096]{1,0:T(8,128)(2,1)S(1)}, u32[]{:S(2)}, u32[]{:S(2)}) collective-permute-start(bf16[128,4096]{1,0:T(8,128)(2,1)} %get-tuple-element.75), channel_id=1, source_target_pairs={{0,2},{1,3},{2,0},{3,1},{4,6},{5,7},{6,4},{7,5}} | collective-permute-start | bytes 3145736 | tf_op jit(solution)/shard_map/ppermute | solution.py:234
  1107.2 71.0 %collective-permute-start.49 = (bf16[128,4096]{1,0:T(8,128)(2,1)S(1)}, bf16[128,4096]{1,0:T(8,128)(2,1)S(1)}, u32[]{:S(2)}, u32[]{:S(2)}) collective-permute-start(bf16[128,4096]{1,0:T(8,128)(2,1)S(1)} %get-tuple-element.57), channel_id=1, source_target_pairs={{0,4},{1,5},{2,6},{3,7},{4,0},{5,1},{6,2},{7,3}} | collective-permute-start | bytes 3145736 | tf_op jit(solution)/shard_map/ppermute | solution.py:234
  1107.7 92.3 %collective-permute-start.50 = (bf16[128,4096]{1,0:T(8,128)(2,1)S(1)}, bf16[128,4096]{1,0:T(8,128)(2,1)S(1)}, u32[]{:S(2)}, u32[]{:S(2)}) collective-permute-start(bf16[128,4096]{1,0:T(8,128)(2,1)S(1)} %get-tuple-element.58), channel_id=1, source_target_pairs={{0,5},{1,4},{2,7},{3,6},{4,1},{5,0},{6,3},{7,2}} | collective-permute-start | bytes 3145736 | tf_op jit(solution)/shard_map/ppermute | solution.py:234
  1109.2 92.3 %collective-permute-start.51 = (bf16[128,4096]{1,0:T(8,128)(2,1)}, bf16[128,4096]{1,0:T(8,128)(2,1)}, u32[]{:S(2)}, u32[]{:S(2)}) collective-permute-start(bf16[128,4096]{1,0:T(8,128)(2,1)} %get-tuple-element.59), channel_id=1, source_target_pairs={{0,6},{1,7},{2,4},{3,5},{4,2},{5,3},{6,0},{7,1}} | collective-permute-start | bytes 3145736 | tf_op jit(solution)/shard_map/ppermute | solution.py:234
  1109.6 92.5 %collective-permute-start.52 = (bf16[128,4096]{1,0:T(8,128)(2,1)}, bf16[128,4096]{1,0:T(8,128)(2,1)}, u32[]{:S(2)}, u32[]{:S(2)}) collective-permute-start(bf16[128,4096]{1,0:T(8,128)(2,1)} %get-tuple-element.60), channel_id=1, source_target_pairs={{0,7},{1,6},{2,5},{3,4},{4,3},{5,2},{6,1},{7,0}} | collective-permute-start | bytes 3145736 | tf_op jit(solution)/shard_map/ppermute | solution.py:234
  1170.7 200.6 %collective-permute-start.66 = (bf16[128,4096]{1,0:T(8,128)(2,1)}, bf16[128,4096]{1,0:T(8,128)(2,1)}, u32[]{:S(2)}, u32[]{:S(2)}) collective-permute-start(bf16[128,4096]{1,0:T(8,128)(2,1)} %get-tuple-element.70), channel_id=1, source_target_pairs={{0,1},{1,0},{2,3},{3,2},{4,5},{5,4},{6,7},{7,6}} | collective-permute-start | bytes 3145736 | tf_op jit(solution)/shard_map/ppermute | solution.py:234
  1178.2 193.9 %collective-permute-start.67 = (bf16[128,4096]{1,0:T(8,128)(2,1)}, bf16[128,4096]{1,0:T(8,128)(2,1)}, u32[]{:S(2)}, u32[]{:S(2)}) collective-permute-start(bf16[128,4096]{1,0:T(8,128)(2,1)} %get-tuple-element.71), channel_id=1, source_target_pairs={{0,2},{1,3},{2,0},{3,1},{4,6},{5,7},{6,4},{7,5}} | collective-permute-start | bytes 3145736 | tf_op jit(solution)/shard_map/ppermute | solution.py:234
  1200.9 173.5 %collective-permute-start.68 = (bf16[128,4096]{1,0:T(8,128)(2,1)}, bf16[128,4096]{1,0:T(8,128)(2,1)}, u32[]{:S(2)}, u32[]{:S(2)}) collective-permute-start(bf16[128,4096]{1,0:T(8,128)(2,1)} %get-tuple-element.72), channel_id=1, source_target_pairs={{0,3},{1,2},{2,1},{3,0},{4,7},{5,6},{6,5},{7,4}} | collective-permute-start | bytes 3145736 | tf_op jit(solution)/shard_map/ppermute | solution.py:234
  1201.5 173.3 %collective-permute-start.39 = (bf16[128,4096]{1,0:T(8,128)(2,1)}, bf16[128,4096]{1,0:T(8,128)(2,1)}, u32[]{:S(2)}, u32[]{:S(2)}) collective-permute-start(bf16[128,4096]{1,0:T(8,128)(2,1)} %get-tuple-element.53), channel_id=1, source_target_pairs={{0,4},{1,5},{2,6},{3,7},{4,0},{5,1},{6,2},{7,3}} | collective-permute-start | bytes 3145736 | tf_op jit(solution)/shard_map/ppermute | solution.py:234
  1202.1 173.0 %collective-permute-start.40 = (bf16[128,4096]{1,0:T(8,128)(2,1)}, bf16[128,4096]{1,0:T(8,128)(2,1)}, u32[]{:S(2)}, u32[]{:S(2)}) collective-permute-start(bf16[128,4096]{1,0:T(8,128)(2,1)} %get-tuple-element.54), channel_id=1, source_target_pairs={{0,5},{1,4},{2,7},{3,6},{4,1},{5,0},{6,3},{7,2}} | collective-permute-start | bytes 3145736 | tf_op jit(solution)/shard_map/ppermute | solution.py:234
  1371.4 138.7 %collective-permute-start.3 = (bf16[256,8192]{1,0:T(8,128)(2,1)}, bf16[256,8192]{1,0:T(8,128)(2,1)}, u32[]{:S(2)}, u32[]{:S(2)}) collective-permute-start(bf16[256,8192]{1,0:T(8,128)(2,1)} %get-tuple-element.77), channel_id=1, source_target_pairs={{0,4},{1,5},{2,6},{3,7},{4,0},{5,1},{6,2},{7,3}} | collective-permute-start | bytes 12582920 | tf_op jit(solution)/shard_map/ppermute | solution.py:234
  1375.1 68.9 %collective-permute-start.64 = (bf16[128,4096]{1,0:T(8,128)(2,1)}, bf16[128,4096]{1,0:T(8,128)(2,1)S(1)}, u32[]{:S(2)}, u32[]{:S(2)}) collective-permute-start(bf16[128,4096]{1,0:T(8,128)(2,1)} %get-tuple-element.67), channel_id=1, source_target_pairs={{0,2},{1,3},{2,0},{3,1},{4,6},{5,7},{6,4},{7,5}} | collective-permute-start | bytes 3145736 | tf_op jit(solution)/shard_map/ppermute | solution.py:234
  1444.1 67.6 %collective-permute-start.32 = (bf16[128,4096]{1,0:T(8,128)(2,1)}, bf16[128,4096]{1,0:T(8,128)(2,1)}, u32[]{:S(2)}, u32[]{:S(2)}) collective-permute-start(bf16[128,4096]{1,0:T(8,128)(2,1)} %get-tuple-element.52), channel_id=1, source_target_pairs={{0,3},{1,2},{2,1},{3,0},{4,7},{5,6},{6,5},{7,4}} | collective-permute-start | bytes 3145736 | tf_op jit(solution)/shard_map/ppermute | solution.py:234
  1466.7 133.1 %collective-permute-start.2 = (bf16[256,8192]{1,0:T(8,128)(2,1)}, bf16[256,8192]{1,0:T(8,128)(2,1)S(1)}, u32[]{:S(2)}, u32[]{:S(2)}) collective-permute-start(bf16[256,8192]{1,0:T(8,128)(2,1)} %get-tuple-element.78), channel_id=1, source_target_pairs={{0,4},{1,5},{2,6},{3,7},{4,0},{5,1},{6,2},{7,3}} | collective-permute-start | bytes 12582920 | tf_op jit(solution)/shard_map/ppermute | solution.py:234
  1468.4 221.3 %collective-permute-start.1 = (bf16[256,8192]{1,0:T(8,128)(2,1)}, bf16[256,8192]{1,0:T(8,128)(2,1)S(1)}, u32[]{:S(2)}, u32[]{:S(2)}) collective-permute-start(bf16[256,8192]{1,0:T(8,128)(2,1)} %get-tuple-element.79), channel_id=1, source_target_pairs={{0,4},{1,5},{2,6},{3,7},{4,0},{5,1},{6,2},{7,3}} | collective-permute-start | bytes 12582920 | tf_op jit(solution)/shard_map/ppermute | solution.py:234
  1489.0 290.5 %collective-permute-start = (bf16[256,8192]{1,0:T(8,128)(2,1)S(1)}, bf16[256,8192]{1,0:T(8,128)(2,1)}, u32[]{:S(2)}, u32[]{:S(2)}) collective-permute-start(bf16[256,8192]{1,0:T(8,128)(2,1)S(1)} %copy-done.2), channel_id=1, source_target_pairs={{0,4},{1,5},{2,6},{3,7},{4,0},{5,1},{6,2},{7,3}} | collective-permute-start | bytes 12582920 | tf_op jit(solution)/shard_map/ppermute | solution.py:234
  1510.1 271.1 %collective-permute-start.11 = (bf16[256,8192]{1,0:T(8,128)(2,1)}, bf16[256,8192]{1,0:T(8,128)(2,1)}, u32[]{:S(2)}, u32[]{:S(2)}) collective-permute-start(bf16[256,8192]{1,0:T(8,128)(2,1)} %collective-permute-done.3.refs_3_), channel_id=1, source_target_pairs={{0,2},{1,3},{2,0},{3,1},{4,6},{5,7},{6,4},{7,5}} | collective-permute-start | bytes 12582920 | tf_op jit(solution)/shard_map/ppermute | solution.py:234
  1511.6 269.6 %collective-permute-start.7 = (bf16[256,8192]{1,0:T(8,128)(2,1)}, bf16[256,8192]{1,0:T(8,128)(2,1)S(1)}, u32[]{:S(2)}, u32[]{:S(2)}) collective-permute-start(bf16[256,8192]{1,0:T(8,128)(2,1)} %collective-permute-done.3.refs_3_), channel_id=1, source_target_pairs={{0,1},{1,0},{2,3},{3,2},{4,5},{5,4},{6,7},{7,6}} | collective-permute-start | bytes 12582920 | tf_op jit(solution)/shard_map/ppermute | solution.py:234
  1599.9 181.7 %collective-permute-start.10 = (bf16[256,8192]{1,0:T(8,128)(2,1)S(1)}, bf16[256,8192]{1,0:T(8,128)(2,1)}, u32[]{:S(2)}, u32[]{:S(2)}) collective-permute-start(bf16[256,8192]{1,0:T(8,128)(2,1)S(1)} %collective-permute-done.2.refs_2_), channel_id=1, source_target_pairs={{0,2},{1,3},{2,0},{3,1},{4,6},{5,7},{6,4},{7,5}} | collective-permute-start | bytes 12582920 | tf_op jit(solution)/shard_map/ppermute | solution.py:234
  1689.7 92.0 %collective-permute-start.6 = (bf16[256,8192]{1,0:T(8,128)(2,1)S(1)}, bf16[256,8192]{1,0:T(8,128)(2,1)S(1)}, u32[]{:S(2)}, u32[]{:S(2)}) collective-permute-start(bf16[256,8192]{1,0:T(8,128)(2,1)S(1)} %collective-permute-done.2.refs_2_), channel_id=1, source_target_pairs={{0,1},{1,0},{2,3},{3,2},{4,5},{5,4},{6,7},{7,6}} | collective-permute-start | bytes 12582920 | tf_op jit(solution)/shard_map/ppermute | solution.py:234
  1779.5 93.6 %collective-permute-start.9 = (bf16[256,8192]{1,0:T(8,128)(2,1)S(1)}, bf16[256,8192]{1,0:T(8,128)(2,1)}, u32[]{:S(2)}, u32[]{:S(2)}) collective-permute-start(bf16[256,8192]{1,0:T(8,128)(2,1)S(1)} %collective-permute-done.1.refs_1_), channel_id=1, source_target_pairs={{0,2},{1,3},{2,0},{3,1},{4,6},{5,7},{6,4},{7,5}} | collective-permute-start | bytes 12582920 | tf_op jit(solution)/shard_map/ppermute | solution.py:234
  1781.2 91.9 %collective-permute-start.5 = (bf16[256,8192]{1,0:T(8,128)(2,1)S(1)}, bf16[256,8192]{1,0:T(8,128)(2,1)S(1)}, u32[]{:S(2)}, u32[]{:S(2)}) collective-permute-start(bf16[256,8192]{1,0:T(8,128)(2,1)S(1)} %collective-permute-done.1.refs_1_), channel_id=1, source_target_pairs={{0,1},{1,0},{2,3},{3,2},{4,5},{5,4},{6,7},{7,6}} | collective-permute-start | bytes 12582920 | tf_op jit(solution)/shard_map/ppermute | solution.py:234
  1781.2 180.7 %collective-permute-start.8 = (bf16[256,8192]{1,0:T(8,128)(2,1)}, bf16[256,8192]{1,0:T(8,128)(2,1)}, u32[]{:S(2)}, u32[]{:S(2)}) collective-permute-start(bf16[256,8192]{1,0:T(8,128)(2,1)} %collective-permute-done.refs_0_), channel_id=1, source_target_pairs={{0,2},{1,3},{2,0},{3,1},{4,6},{5,7},{6,4},{7,5}} | collective-permute-start | bytes 12582920 | tf_op jit(solution)/shard_map/ppermute | solution.py:234
  1781.6 344.7 %collective-permute-start.4 = (bf16[256,8192]{1,0:T(8,128)(2,1)}, bf16[256,8192]{1,0:T(8,128)(2,1)}, u32[]{:S(2)}, u32[]{:S(2)}) collective-permute-start(bf16[256,8192]{1,0:T(8,128)(2,1)} %collective-permute-done.refs_0_), channel_id=1, source_target_pairs={{0,1},{1,0},{2,3},{3,2},{4,5},{5,4},{6,7},{7,6}} | collective-permute-start | bytes 12582920 | tf_op jit(solution)/shard_map/ppermute | solution.py:234
  1781.8 345.1 %collective-permute-start.15 = (bf16[256,8192]{1,0:T(8,128)(2,1)}, bf16[256,8192]{1,0:T(8,128)(2,1)}, u32[]{:S(2)}, u32[]{:S(2)}) collective-permute-start(bf16[256,8192]{1,0:T(8,128)(2,1)} %collective-permute-done.11.refs_11_), channel_id=1, source_target_pairs={{0,1},{1,0},{2,3},{3,2},{4,5},{5,4},{6,7},{7,6}} | collective-permute-start | bytes 12582920 | tf_op jit(solution)/shard_map/ppermute | solution.py:234
  1873.1 255.1 %collective-permute-start.14 = (bf16[256,8192]{1,0:T(8,128)(2,1)}, bf16[256,8192]{1,0:T(8,128)(2,1)}, u32[]{:S(2)}, u32[]{:S(2)}) collective-permute-start(bf16[256,8192]{1,0:T(8,128)(2,1)} %collective-permute-done.10.refs_10_), channel_id=1, source_target_pairs={{0,1},{1,0},{2,3},{3,2},{4,5},{5,4},{6,7},{7,6}} | collective-permute-start | bytes 12582920 | tf_op jit(solution)/shard_map/ppermute | solution.py:234
  1873.1 256.6 %collective-permute-start.13 = (bf16[256,8192]{1,0:T(8,128)(2,1)}, bf16[256,8192]{1,0:T(8,128)(2,1)}, u32[]{:S(2)}, u32[]{:S(2)}) collective-permute-start(bf16[256,8192]{1,0:T(8,128)(2,1)} %collective-permute-done.9.refs_9_), channel_id=1, source_target_pairs={{0,1},{1,0},{2,3},{3,2},{4,5},{5,4},{6,7},{7,6}} | collective-permute-start | bytes 12582920 | tf_op jit(solution)/shard_map/ppermute | solution.py:234
  1961.9 168.8 %collective-permute-start.12 = (bf16[256,8192]{1,0:T(8,128)(2,1)}, bf16[256,8192]{1,0:T(8,128)(2,1)}, u32[]{:S(2)}, u32[]{:S(2)}) collective-permute-start(bf16[256,8192]{1,0:T(8,128)(2,1)} %collective-permute-done.8.refs_8_), channel_id=1, source_target_pairs={{0,1},{1,0},{2,3},{3,2},{4,5},{5,4},{6,7},{7,6}} | collective-permute-start | bytes 12582920 | tf_op jit(solution)/shard_map/ppermute | solution.py:234
  2126.3 123.5 %collective-permute-start.26 = (bf16[128,4096]{1,0:T(8,128)(2,1)S(1)}, bf16[128,4096]{1,0:T(8,128)(2,1)S(1)}, u32[]{:S(2)}, u32[]{:S(2)}) collective-permute-start(bf16[128,4096]{1,0:T(8,128)(2,1)S(1)} %get-tuple-element.45), channel_id=1, source_target_pairs={{0,4},{1,5},{2,6},{3,7},{4,0},{5,1},{6,2},{7,3}} | collective-permute-start | bytes 3145736 | tf_op jit(solution)/shard_map/ppermute | solution.py:234
  2126.9 122.9 %collective-permute-start.27 = (bf16[128,4096]{1,0:T(8,128)(2,1)S(1)}, bf16[128,4096]{1,0:T(8,128)(2,1)S(1)}, u32[]{:S(2)}, u32[]{:S(2)}) collective-permute-start(bf16[128,4096]{1,0:T(8,128)(2,1)S(1)} %get-tuple-element.46), channel_id=1, source_target_pairs={{0,5},{1,4},{2,7},{3,6},{4,1},{5,0},{6,3},{7,2}} | collective-permute-start | bytes 3145736 | tf_op jit(solution)/shard_map/ppermute | solution.py:234
  2128.2 121.6 %collective-permute-start.28 = (bf16[128,4096]{1,0:T(8,128)(2,1)S(1)}, bf16[128,4096]{1,0:T(8,128)(2,1)S(1)}, u32[]{:S(2)}, u32[]{:S(2)}) collective-permute-start(bf16[128,4096]{1,0:T(8,128)(2,1)S(1)} %copy-done.25), channel_id=1, source_target_pairs={{0,6},{1,7},{2,4},{3,5},{4,2},{5,3},{6,0},{7,1}} | collective-permute-start | bytes 3145736 | tf_op jit(solution)/shard_map/ppermute | solution.py:234
  2129.7 120.1 %collective-permute-start.29 = (bf16[128,4096]{1,0:T(8,128)(2,1)S(1)}, bf16[128,4096]{1,0:T(8,128)(2,1)S(1)}, u32[]{:S(2)}, u32[]{:S(2)}) collective-permute-start(bf16[128,4096]{1,0:T(8,128)(2,1)S(1)} %copy-done.24), channel_id=1, source_target_pairs={{0,7},{1,6},{2,5},{3,4},{4,3},{5,2},{6,1},{7,0}} | collective-permute-start | bytes 3145736 | tf_op jit(solution)/shard_map/ppermute | solution.py:234
  (39 other events, 3151.7 us)
